TPU v7x, 256 devices: a whole 4x4x8 slice. The times are simulated.
256 devices in a mesh: fft: 32 (over x_lo, z, core), scal: 8 (over x_hi, y).
Axes of the slice: x: 4 (x_hi: 2, x_lo: 2; x = x_hi * 2 + x_lo), y: 4, z: 8, core: 2. Of those that a mesh axis runs over, the one named last changes fastest.
Arguments:
- scalar_state: float32 [8, 2, 256, 256, 128], P('scal', None, 'fft'), may hold values from -12 to 12
- velocity: bfloat16 [3, 256, 256, 256], P(None, 'fft', 'scal'), may hold values from -6 to 6
- species: int32 [8], P('scal'), may hold values from 0 to 63
- kappa_table: float32 [64], replicated, may hold values from 0.1 to 1
- dealias_bound: int32 [8], P('scal'), may hold values from 64 to 85
Outputs:
- new_state: float32 [8, 2, 256, 256, 128], P('scal', None, 'fft')
- kappa: float32 [8], P('scal')
All inputs are finite; a program needn't handle non-finite values.
Results may differ from a plain program's by a relative error of at most 0.0027.
Values may be sent and summed in bfloat16 or wider, within the bound.
No kernel may reach another device: no remote copies, remote signals or barrier semaphores. Data moves between devices by JAX's collectives and lax.ppermute only.
A program may use at most 128 MiB of HBM per device.

v0:
```python
import math

import jax
import jax.numpy as jnp
from jax import lax
from jax.sharding import PartitionSpec as P

cfl_number = 0.2


def in_one_piece(arrays, axis, split_dim, concat_dim, along):
    widths = [a.shape[along] for a in arrays]
    both = jnp.concatenate(arrays, axis=along)
    out = lax.all_to_all(both, axis, split_axis=split_dim, concat_axis=concat_dim, tiled=True)
    return tuple(jnp.split(out, [sum(widths[:k]) for k in range(1, len(widths))], axis=along))


def copy_for_each(x, axis):
    count = lax.axis_size(axis)
    return lax.all_to_all(jnp.broadcast_to(x[None], (count, *x.shape)), axis, 0, 0, tiled=True)


def collected_together(x, axis):
    leaves = jax.tree.leaves(x)
    sequence = sorted(range(len(leaves)), key=lambda k: -leaves[k].size)
    width = (1, *leaves[sequence[0]].shape)[-1]
    lines = [
        jnp.pad(leaves[k].reshape(-1), (0, -leaves[k].size % width)).reshape(-1, width)
        for k in sequence
    ]
    both, at, found = (copy_for_each(jnp.concatenate(lines), axis), 0, {})
    for k, line in zip(sequence, lines):
        section = both[:, at : at + len(line)].reshape(len(both), -1)
        found[k] = section[:, : leaves[k].size].reshape(-1, *leaves[k].shape)
        at += len(line)
    numbers = iter(range(len(leaves)))
    return jax.tree.map(lambda _: found[next(numbers)], x)


def folded_in_pairs(pieces, combine):
    while len(jax.tree.leaves(pieces)[0]) > 1:
        pieces = jax.vmap(combine)(
            *(jax.tree.map(lambda part: part[side::2], pieces) for side in (0, 1))
        )
    return jax.tree.map(lambda part: part[0], pieces)


def combined_all(x, axis, combine):
    pieces = collected_together(x, axis)
    return folded_in_pairs(pieces, combine)


def twiddle(size_in, size_out, length):
    row_index = jnp.arange(size_in, dtype=jnp.int32)[:, None]
    col_index = jnp.arange(size_out, dtype=jnp.int32)[None, :]
    angles = (row_index * col_index % length).astype(jnp.float32) * (2.0 * math.pi / length)
    norming = 1.0 / math.sqrt(length)
    return (jnp.cos(angles) * norming, jnp.sin(angles) * norming)


def build_tables(length):
    half_len = length // 2
    full_cos, full_sin = twiddle(length, length, length)
    inv_cos, inv_sin = twiddle(half_len, length, length)
    weight = jnp.where(jnp.arange(half_len, dtype=jnp.int32) == 0, 1.0, 2.0).astype(jnp.float32)[
        :, None
    ]
    fwd_cos, fwd_sin = twiddle(length, half_len, length)
    listed = (full_cos, full_sin, inv_cos * weight, inv_sin * weight, fwd_cos, fwd_sin)
    return tuple((matrix.astype(jnp.bfloat16) for matrix in listed))


def product(formula, operand, matrix):
    return jnp.einsum(formula, operand, matrix, preferred_element_type=jnp.float32)


def complex_section(real_part, imag_part, cos_matrix, sin_matrix, formula, inverse):
    real_cos = product(formula, real_part, cos_matrix)
    real_sin = product(formula, real_part, sin_matrix)
    imag_cos = product(formula, imag_part, cos_matrix)
    imag_sin = product(formula, imag_part, sin_matrix)
    if inverse:
        return (real_cos - imag_sin, real_sin + imag_cos)
    return (real_cos + imag_sin, imag_cos - real_sin)


def combine_stats(earlier, later):
    return (earlier[0] + later[0], earlier[1] + later[1], jnp.maximum(earlier[2], later[2]))


def times_wave(wavenumber, real_part, imag_part):
    new_real = (-wavenumber * imag_part.astype(jnp.float32)).astype(jnp.bfloat16)
    new_imag = (wavenumber * real_part.astype(jnp.float32)).astype(jnp.bfloat16)
    return (new_real, new_imag)


def body(scalar_state, velocity, species, kappa_table, dealias_bound):
    ky_local = scalar_state.shape[2]
    length = scalar_state.shape[3]
    half_len = length // 2
    total_count = kappa_table.shape[0]
    full_cos, full_sin, inv_cos, inv_sin, fwd_cos, fwd_sin = build_tables(length)
    ky_index = lax.axis_index("fft") * ky_local + jnp.arange(ky_local, dtype=jnp.int32)
    ky_wave = jnp.where(ky_index < half_len, ky_index, ky_index - length).astype(jnp.float32)[
        :, None, None
    ]
    kz_index = jnp.arange(length, dtype=jnp.int32)
    signed_full = jnp.where(kz_index < half_len, kz_index, kz_index - length).astype(jnp.float32)
    kz_wave = signed_full[None, :, None]
    ky_whole = signed_full[:, None, None]
    kx_wave = jnp.arange(half_len, dtype=jnp.int32).astype(jnp.float32)[None, None, :]
    ksquare = kx_wave * kx_wave + ky_wave * ky_wave + kz_wave * kz_wave
    weight = jnp.where(kx_wave == 0.0, 1.0, 2.0).astype(jnp.float32)
    cell_count = float(length) ** 3
    step_size = cfl_number * 2.0 * math.pi / length
    speeds = lax.all_gather(velocity, "scal", axis=2, tiled=True)

    def finish_inverse(halves):
        y_section = complex_section(
            halves[0], halves[1], full_cos, full_sin, "...yzx,yw->...zwx", True
        )
        y_real = y_section[0].astype(jnp.bfloat16)
        y_imag = y_section[1].astype(jnp.bfloat16)
        return product("...zwk,kx->...zwx", y_real, inv_cos) - product(
            "...zwk,kx->...zwx", y_imag, inv_sin
        )

    def gradient_set(real_part, imag_part):
        pair_real = jnp.stack([real_part, -kz_wave * imag_part]).astype(jnp.bfloat16)
        pair_imag = jnp.stack([imag_part, kz_wave * real_part]).astype(jnp.bfloat16)
        z_section = complex_section(
            pair_real, pair_imag, full_cos, full_sin, "...ykx,kz->...yzx", True
        )
        z_real = z_section[0].astype(jnp.bfloat16)
        z_imag = z_section[1].astype(jnp.bfloat16)
        came_real, came_imag = in_one_piece((z_real, z_imag), "fft", 2, 1, 0)
        x_real, x_imag = times_wave(kx_wave, came_real[0], came_imag[0])
        y_real, y_imag = times_wave(ky_whole, came_real[0], came_imag[0])
        all_real = jnp.stack([x_real, y_real, came_real[1]])
        all_imag = jnp.stack([x_imag, y_imag, came_imag[1]])
        return finish_inverse((all_real, all_imag))

    def advect(gradients):
        total = speeds[0].astype(jnp.float32) * gradients[0]
        total = total + speeds[1].astype(jnp.float32) * gradients[1]
        total = total + speeds[2].astype(jnp.float32) * gradients[2]
        return total.astype(jnp.bfloat16)

    def finish_forward(halves):
        return complex_section(halves[0], halves[1], full_cos, full_sin, "...wzk,zv->...wvk", False)

    def tendency(advected, bound):
        real_x = product("zyx,xk->zyk", advected, fwd_cos).astype(jnp.bfloat16)
        imag_x = (-product("zyx,xk->zyk", advected, fwd_sin)).astype(jnp.bfloat16)
        y_section = complex_section(real_x, imag_x, full_cos, full_sin, "zyk,yw->wzk", False)
        y_real = y_section[0].astype(jnp.bfloat16)
        y_imag = y_section[1].astype(jnp.bfloat16)
        spectral = finish_forward(
            (
                lax.all_to_all(y_real, "fft", split_axis=0, concat_axis=1, tiled=True),
                lax.all_to_all(y_imag, "fft", split_axis=0, concat_axis=1, tiled=True),
            )
        )
        dealias_mask = (ksquare <= bound * bound).astype(jnp.float32)
        return (-dealias_mask * spectral[0], -dealias_mask * spectral[1])

    scalar = 0
    start_real = scalar_state[scalar, 0]
    start_imag = scalar_state[scalar, 1]
    energy = start_real * start_real + start_imag * start_imag
    local_var = [jnp.sum(weight * energy) / cell_count]
    local_grad = [jnp.sum(weight * ksquare * energy) / cell_count]
    gradients = gradient_set(start_real, start_imag)
    magnitude = jnp.sqrt(
        gradients[0] * gradients[0] + gradients[1] * gradients[1] + gradients[2] * gradients[2]
    )
    local_peak = [jnp.max(magnitude)]
    advect_saved = [advect(gradients)]
    var_part = jnp.stack(local_var)
    grad_part = jnp.stack(local_grad)
    peak_part = jnp.stack(local_peak)
    variance, mean_grad, peak_value = combined_all(
        (var_part, grad_part, peak_part), "fft", combine_stats
    )
    matches = species[:, None] == jnp.arange(total_count, dtype=jnp.int32)[None, :]
    base_kappa = jnp.sum(jnp.where(matches, kappa_table[None, :], 0.0), axis=1)
    kappa = base_kappa * peak_value * jnp.sqrt(variance) / (mean_grad + 1e-06)
    scalar = 0
    start_real = scalar_state[scalar, 0]
    start_imag = scalar_state[scalar, 1]
    factor = jnp.exp(-kappa[scalar] * ksquare * step_size)
    bound = dealias_bound[scalar].astype(jnp.float32)
    first_real, first_imag = tendency(advect_saved[scalar], bound)
    mid_real = factor * (start_real + step_size * first_real)
    mid_imag = factor * (start_imag + step_size * first_imag)
    second_real, second_imag = tendency(advect(gradient_set(mid_real, mid_imag)), bound)
    new_real = factor * start_real + 0.5 * step_size * (factor * first_real + second_real)
    new_imag = factor * start_imag + 0.5 * step_size * (factor * first_imag + second_imag)
    updated_list = [jnp.stack([new_real, new_imag])]
    return (jnp.stack(updated_list), kappa)


def solution(mesh):
    placed = (
        P("scal", None, "fft", None, None),
        P(None, "fft", "scal", None),
        P("scal"),
        P(),
        P("scal"),
    )
    return jax.shard_map(
        body,
        mesh=mesh,
        in_specs=placed,
        out_specs=(P("scal", None, "fft", None, None), P("scal")),
        check_vma=False,
    )
```

profile of v0, /device:TPU:1, one launch (start us, length us, event | category | flops | bytes accessed | tf_op | source)
XLA Modules:
  0.0 341.0 jit_solution(12632958124329488233)
XLA Ops:
  7.2 1.9 bitcast_convert_fusion
  9.7 1.4 fusion.55
  11.1 1.3 fusion.56
  12.4 1.4 fusion.13
  13.8 1.4 fusion.12
  15.3 2.7 copy.71
  18.0 11.1 %all-to-all-start = ((bf16[4,8,256,128]{3,1,0,2:T(8,128)(2,1)}), bf16[4,8,256,128]{3,1,0,2:T(8,128)(2,1)}, u32[]{:S(2)}, u32[]{:S(2)}) async-start(bf16[4,8,256,128]{3,1,0,2:T(8,128)(2,1)} %copy.71), calls=%async_computation | async-start | bytes 4194304 | tf_op jit(solution)/shard_map/all_to_all | solution.py:14
  32.1 46.3 %all-to-all-done = bf16[4,8,256,128]{3,1,0,2:T(8,128)(2,1)} async-done(((bf16[4,8,256,128]{3,1,0,2:T(8,128)(2,1)}), bf16[4,8,256,128]{3,1,0,2:T(8,128)(2,1)}, u32[]{:S(2)}, u32[]{:S(2)}) %all-to-all-start) | async-done | bytes 2097184 | tf_op jit(solution)/shard_map/all_to_all | solution.py:14
  78.4 2.4 copy.150
  82.1 3.1 fusion.60
  85.2 3.1 fusion.59
  89.4 7.1 %fusion.10 = f32[3,8,256,256]{3,2,1,0:T(8,128)} fusion(f32[256,3,8,128]{3,0,2,1:T(8,128)} %fusion.60, bf16[1,256,8,128]{3,1,2,0:T(8,128)(2,1)S(1)} %copy.82, bf16[1,256,8,128]{3,1,2,0:T(8,128)(2,1)} %get-tuple-element.32, bf16[1,256,8,128]{3,1,2,0:T(8,128)(2,1)S(1)} %get-tuple-element.31, f32[128]{0:T(128)S(1)} %fusion.155), kind=kOutput, calls=%fused_computation.39 | convolution fusion | flops 813170688 | bytes 11010560 | tf_op jit(solution)/shard_map/...zwk,kx->...zwx/dot_general | solution.py:74
  96.5 9.0 %convolution_subtract_fusion.1 = f32[3,8,256,256]{3,2,1,0:T(8,128)} fusion(f32[3,8,256,256]{3,2,1,0:T(8,128)} %fusion.10, f32[256,3,8,128]{3,0,2,1:T(8,128)} %fusion.59, bf16[1,256,8,128]{3,1,2,0:T(8,128)(2,1)S(1)} %copy.82, bf16[1,256,8,128]{3,1,2,0:T(8,128)(2,1)} %get-tuple-element.32, bf16[1,256,8,128]{3,1,2,0:T(8,128)(2,1)S(1)} %get-tuple-element.31, ...), kind=kOutput, calls=%fused_computation.5 | convolution fusion | flops 814743552 | bytes 17302016 | tf_op jit(solution)/shard_map/...zwk,kx->...zwx/dot_general | solution.py:74
  105.5 5.7 %sqrt_reduce_fusion = (f32[]{:T(128)}, bf16[8,256,256]{2,1,0:T(8,128)(2,1)S(1)}) fusion(f32[3,8,256,256]{3,2,1,0:T(8,128)} %convolution_subtract_fusion.1, bf16[3,8,256,256]{3,2,1,0:T(8,128)(2,1)} %all-gather.2.cloned.1.call-done), kind=kLoop, calls=%fused_computation.23 | loop fusion | flops 7864319 | bytes 10485764 | tf_op jit(solution)/shard_map/reduce_max | solution.py:177
  111.3 1.4 fusion.32
  112.7 1.7 convolution_convert_fusion.1
  116.9 6.6 %all-to-all-start.1 = ((f32[32,3,1]{1,2,0:T(1,128)}), f32[32,3,1]{1,2,0:T(1,128)S(1)}, u32[]{:S(2)}, u32[]{:S(2)}) async-start(f32[32,3,1]{1,2,0:T(1,128)} %broadcast_in_dim.23), calls=%async_computation.1 | async-start | bytes 32768 | tf_op jit(solution)/shard_map/all_to_all | solution.py:20
  123.5 2.2 fusion.35
  126.9 4.5 %all-to-all-done.1 = f32[32,3,1]{1,2,0:T(1,128)S(1)} async-done(((f32[32,3,1]{1,2,0:T(1,128)}), f32[32,3,1]{1,2,0:T(1,128)S(1)}, u32[]{:S(2)}, u32[]{:S(2)}) %all-to-all-start.1) | async-done | bytes 416 | tf_op jit(solution)/shard_map/all_to_all | solution.py:20
  131.4 4.3 %all-to-all-start.3 = ((bf16[256,8,128]{2,1,0:T(8,128)(2,1)}), bf16[256,8,128]{2,1,0:T(8,128)(2,1)S(1)}, u32[]{:S(2)}, u32[]{:S(2)}) async-start(bf16[256,8,128]{2,1,0:T(8,128)(2,1)} %copy.85), calls=%async_computation.3 | async-start | bytes 1048576 | tf_op jit(solution)/shard_map/all_to_all | solution.py:161
  135.8 2.2 fusion.113
  140.4 12.1 %all-to-all-done.3 = bf16[256,8,128]{2,1,0:T(8,128)(2,1)S(1)} async-done(((bf16[256,8,128]{2,1,0:T(8,128)(2,1)}), bf16[256,8,128]{2,1,0:T(8,128)(2,1)S(1)}, u32[]{:S(2)}, u32[]{:S(2)}) %all-to-all-start.3) | async-done | bytes 524320 | tf_op jit(solution)/shard_map/all_to_all | solution.py:161
  152.5 5.8 %all-to-all-start.2 = ((bf16[256,8,128]{2,1,0:T(8,128)(2,1)}), bf16[256,8,128]{2,1,0:T(8,128)(2,1)S(1)}, u32[]{:S(2)}, u32[]{:S(2)}) async-start(bf16[256,8,128]{2,1,0:T(8,128)(2,1)} %copy.83), calls=%async_computation.2 | async-start | bytes 1048576 | tf_op jit(solution)/shard_map/all_to_all | solution.py:160
  169.8 2.2 fusion.72
  172.0 2.8 all-to-all-done.2
  176.0 2.5 fusion.29
  180.7 1.3 fusion.53
  182.0 1.3 fusion.54
  183.4 1.4 fusion.15
  184.8 1.4 fusion.14
  186.5 1.4 copy.87
  187.9 54.4 %all_to_all.107 = bf16[4,8,256,128]{3,1,0,2:T(8,128)(2,1)S(1)} all-to-all(bf16[4,8,256,128]{3,1,0,2:T(8,128)(2,1)S(1)} %copy.87), channel_id=1, replica_groups=mesh['fft'=32,'scal'=8] {'fft'}, dimensions={2} | all-to-all | bytes 4194304 | tf_op jit(solution)/shard_map/all_to_all | solution.py:14
  244.0 3.1 fusion.58
  247.1 3.1 fusion.57
  251.7 7.1 %fusion.7 = f32[3,8,256,256]{3,2,1,0:T(8,128)} fusion(f32[256,3,8,128]{3,0,2,1:T(8,128)} %fusion.58, bf16[1,256,8,128]{3,1,2,0:T(8,128)(2,1)S(1)} %copy.98, bf16[1,256,8,128]{3,1,2,0:T(8,128)(2,1)} %get-tuple-element.28, bf16[1,256,8,128]{3,1,2,0:T(8,128)(2,1)S(1)} %get-tuple-element.27, f32[128]{0:T(128)S(1)} %fusion.155), kind=kOutput, calls=%fused_computation.36 | convolution fusion | flops 813170688 | bytes 11010560 | tf_op jit(solution)/shard_map/...zwk,kx->...zwx/dot_general | solution.py:74
  258.8 8.9 %convolution_subtract_fusion = f32[3,8,256,256]{3,2,1,0:T(8,128)} fusion(f32[3,8,256,256]{3,2,1,0:T(8,128)} %fusion.7, f32[256,3,8,128]{3,0,2,1:T(8,128)} %fusion.57, bf16[1,256,8,128]{3,1,2,0:T(8,128)(2,1)S(1)} %copy.98, bf16[1,256,8,128]{3,1,2,0:T(8,128)(2,1)} %get-tuple-element.28, bf16[1,256,8,128]{3,1,2,0:T(8,128)(2,1)S(1)} %get-tuple-element.27, ...), kind=kOutput, calls=%fused_computation.4 | convolution fusion | flops 814743552 | bytes 17302016 | tf_op jit(solution)/shard_map/...zwk,kx->...zwx/dot_general | solution.py:74
  267.7 4.5 %fusion.48 = bf16[8,256,256]{2,1,0:T(8,128)(2,1)S(1)} fusion(f32[3,8,256,256]{3,2,1,0:T(8,128)} %convolution_subtract_fusion, bf16[3,8,256,256]{3,2,1,0:T(8,128)(2,1)} %all-gather.2.cloned.1.call-done), kind=kLoop, calls=%fused_computation.89 | loop fusion | flops 4718592 | bytes 10485760 | tf_op jit(solution)/shard_map/add | solution.py:146
  273.1 1.3 convolution_convert_fusion
  278.0 5.9 %all-to-all-start.6 = ((bf16[256,8,128]{2,1,0:T(8,128)(2,1)}), bf16[256,8,128]{2,1,0:T(8,128)(2,1)S(1)}, u32[]{:S(2)}, u32[]{:S(2)}) async-start(bf16[256,8,128]{2,1,0:T(8,128)(2,1)} %copy.101), calls=%async_computation.6 | async-start | bytes 1048576 | tf_op jit(solution)/shard_map/all_to_all | solution.py:161
  283.9 2.2 fusion.107
  288.5 12.0 %all-to-all-done.6 = bf16[256,8,128]{2,1,0:T(8,128)(2,1)S(1)} async-done(((bf16[256,8,128]{2,1,0:T(8,128)(2,1)}), bf16[256,8,128]{2,1,0:T(8,128)(2,1)S(1)}, u32[]{:S(2)}, u32[]{:S(2)}) %all-to-all-start.6) | async-done | bytes 524320 | tf_op jit(solution)/shard_map/all_to_all | solution.py:161
  301.3 6.6 %all-to-all-start.5 = ((bf16[256,8,128]{2,1,0:T(8,128)(2,1)}), bf16[256,8,128]{2,1,0:T(8,128)(2,1)}, u32[]{:S(2)}, u32[]{:S(2)}) async-start(bf16[256,8,128]{2,1,0:T(8,128)(2,1)} %copy.99), calls=%async_computation.5 | async-start | bytes 1048576 | tf_op jit(solution)/shard_map/all_to_all | solution.py:160
  307.9 3.3 fusion.66
  311.2 13.2 %all-to-all-done.5 = bf16[256,8,128]{2,1,0:T(8,128)(2,1)} async-done(((bf16[256,8,128]{2,1,0:T(8,128)(2,1)}), bf16[256,8,128]{2,1,0:T(8,128)(2,1)}, u32[]{:S(2)}, u32[]{:S(2)}) %all-to-all-start.5) | async-done | bytes 524320 | tf_op jit(solution)/shard_map/all_to_all | solution.py:160
  324.5 2.2 fusion.64
  326.7 3.0 fusion.21
  329.8 1.5 fusion.27
  331.4 1.5 maximum_bitcast_fusion
  (114 shorter events, 31.1 us)
Async XLA Ops:
  7.2 2.2 copy-start
  18.0 60.4 %all-to-all-start = ((bf16[4,8,256,128]{3,1,0,2:T(8,128)(2,1)}), bf16[4,8,256,128]{3,1,0,2:T(8,128)(2,1)}, u32[]{:S(2)}, u32[]{:S(2)}) async-start(bf16[4,8,256,128]{3,1,0,2:T(8,128)(2,1)} %copy.71), calls=%async_computation | async-start | bytes 4194304 | tf_op jit(solution)/shard_map/all_to_all | solution.py:14
  29.1 76.4 %all-gather.2.cloned.1.call-start = ((), (), s32[]{:S(2)}) async-start(), calls=%async_computation.7 | async-start | bytes 3538944 | tf_op jit(solution)/shard_map/all_gather | solution.py:116
  112.7 1.7 copy-start.7
  116.9 14.5 %all-to-all-start.1 = ((f32[32,3,1]{1,2,0:T(1,128)}), f32[32,3,1]{1,2,0:T(1,128)S(1)}, u32[]{:S(2)}, u32[]{:S(2)}) async-start(f32[32,3,1]{1,2,0:T(1,128)} %broadcast_in_dim.23), calls=%async_computation.1 | async-start | bytes 32768 | tf_op jit(solution)/shard_map/all_to_all | solution.py:20
  125.8 12.2 %copy-start.8 = (bf16[8,256,128]{2,1,0:T(8,128)(2,1)S(1)}, bf16[8,256,128]{2,1,0:T(8,128)(2,1)}, u32[]{:S(2)}) copy-start(bf16[8,256,128]{2,1,0:T(8,128)(2,1)} %copy-done.7) | copy-start | bytes 1572868
  131.4 21.0 %all-to-all-start.3 = ((bf16[256,8,128]{2,1,0:T(8,128)(2,1)}), bf16[256,8,128]{2,1,0:T(8,128)(2,1)S(1)}, u32[]{:S(2)}, u32[]{:S(2)}) async-start(bf16[256,8,128]{2,1,0:T(8,128)(2,1)} %copy.85), calls=%async_computation.3 | async-start | bytes 1048576 | tf_op jit(solution)/shard_map/all_to_all | solution.py:161
  138.0 21.5 %copy-start.10 = (f32[64]{0:T(128)S(1)}, f32[64]{0:T(128)}, u32[]{:S(2)}) copy-start(f32[64]{0:T(128)} %param.8) | copy-start | bytes 772
  152.5 22.3 %all-to-all-start.2 = ((bf16[256,8,128]{2,1,0:T(8,128)(2,1)}), bf16[256,8,128]{2,1,0:T(8,128)(2,1)S(1)}, u32[]{:S(2)}, u32[]{:S(2)}) async-start(bf16[256,8,128]{2,1,0:T(8,128)(2,1)} %copy.83), calls=%async_computation.2 | async-start | bytes 1048576 | tf_op jit(solution)/shard_map/all_to_all | solution.py:160
  178.5 2.1 copy-start.3
  179.7 1.0 copy-start.1
  274.4 2.4 copy-start.9
  278.0 22.5 %all-to-all-start.6 = ((bf16[256,8,128]{2,1,0:T(8,128)(2,1)}), bf16[256,8,128]{2,1,0:T(8,128)(2,1)S(1)}, u32[]{:S(2)}, u32[]{:S(2)}) async-start(bf16[256,8,128]{2,1,0:T(8,128)(2,1)} %copy.101), calls=%async_computation.6 | async-start | bytes 1048576 | tf_op jit(solution)/shard_map/all_to_all | solution.py:161
  300.5 0.8 copy-start.5
  301.3 23.2 %all-to-all-start.5 = ((bf16[256,8,128]{2,1,0:T(8,128)(2,1)}), bf16[256,8,128]{2,1,0:T(8,128)(2,1)}, u32[]{:S(2)}, u32[]{:S(2)}) async-start(bf16[256,8,128]{2,1,0:T(8,128)(2,1)} %copy.99), calls=%async_computation.5 | async-start | bytes 1048576 | tf_op jit(solution)/shard_map/all_to_all | solution.py:160
  307.9 18.8 %copy-start.4 = (f32[8,256,128]{2,1,0:T(8,128)S(1)}, f32[8,256,128]{2,1,0:T(8,128)}, u32[]{:S(2)}) copy-start(f32[8,256,128]{2,1,0:T(8,128)} %copy-done.3) | copy-start | bytes 3145732
  326.7 3.1 copy-start.2
  326.7 3.1 copy-start.6
Sparse Core Ops, SparseCore 0:
  32.5 72.3 all-gather.1
where the time goes:
time: 348 us; the launch traced here: 341 us
  waiting for transfers between devices  91.2 us (26%)
  matrix products  90.6 us (26%)
  blocking collectives  54.4 us (16%)
  starting transfers between devices  40.6 us (12%)
  between operations  23 us (7%)
  local copies, waits for them, and re-layouts  21.8 us (6%)
  other arithmetic  19.3 us (6%)
    dot_general x36, matrix products, product(): jnp.einsum(formula, operand, matrix, preferred_element_type=jnp.float32)  90.6 us
    all_to_all x1, blocking collectives, in_one_piece(): lax.all_to_all(both, axis, split_axis=split_dim, concat_axis=concat_dim,...  54.4 us
    all_to_all x1, waiting for transfers between devices, in_one_piece(): lax.all_to_all(both, axis, split_axis=split_dim, concat_axis=concat_dim,...  46.3 us
    all_to_all x2, waiting for transfers between devices, tendency(): lax.all_to_all(y_imag, 'fft', split_axis=0, concat_axis=1, tiled=True)  24.1 us
    all_to_all x2, waiting for transfers between devices, tendency(): lax.all_to_all(y_real, 'fft', split_axis=0, concat_axis=1, tiled=True)  16 us
    all_to_all x2, starting transfers between devices, tendency(): lax.all_to_all(y_real, 'fft', split_axis=0, concat_axis=1, tiled=True)  12.4 us
    all_to_all x1, starting transfers between devices, in_one_piece(): lax.all_to_all(both, axis, split_axis=split_dim, concat_axis=concat_dim,...  11.1 us
    all_to_all x2, starting transfers between devices, tendency(): lax.all_to_all(y_imag, 'fft', split_axis=0, concat_axis=1, tiled=True)  10.2 us
  transfers between devices with their start and end apart: 7, of which 6 were waited for; matrix products, arithmetic and copies ran while one was open for 15% of the time, Pallas kernels for 0%

commit v1 on v0

v1 whole, which is shorter than its diff:
```python
import math

import jax
import jax.numpy as jnp
import numpy as np
from jax import lax
from jax.experimental import pallas as pl
from jax.experimental.pallas import tpu as pltpu
from jax.sharding import PartitionSpec as P

N = 256
HALF = 128
PEERS = 32
ROWS = N // PEERS
GROUP = 4
KEPT = 96
LIMIT = 86
PACKED = ROWS * KEPT
PITCH = 2 * N + 8
STEP = 0.2 * 2.0 * math.pi / N
CELLS = float(N) ** 3
F32 = jnp.float32
BF16 = jnp.bfloat16


def tables():
    index = np.arange(N)
    angles = (index[:, None] * index[None, :] % N).astype(np.float32) * np.float32(2.0 * math.pi / N)
    cos = np.cos(angles) * np.float32(1.0 / math.sqrt(N))
    sin = np.sin(angles) * np.float32(1.0 / math.sqrt(N))
    weight = np.where(np.arange(HALF) == 0, 1.0, 2.0).astype(np.float32)[:, None]
    inverse = np.block([[cos, -sin], [sin, cos]])
    forward = np.block([[cos, sin], [-sin, cos]])
    order = np.arange(2 * N).reshape(2, PEERS, ROWS).transpose(1, 0, 2).reshape(-1)
    x_inv = np.concatenate([-weight * sin[:HALF], -weight * cos[:HALF]], axis=0)
    keep = (np.arange(HALF) < LIMIT).astype(np.float32)[None, :]
    x_fwd = np.concatenate([cos[:, :HALF] * keep, -sin[:, :HALF] * keep], axis=1)
    listed = {
        "z_inv": inverse,
        "y_inv": inverse[:, order],
        "x_inv": x_inv,
        "x_fwd": x_fwd,
        "y_fwd": forward[order, :],
        "z_fwd": forward[:, order],
    }
    return {name: jnp.asarray(value.astype(np.float32)).astype(BF16) for name, value in listed.items()}


def dot(left, right):
    return jnp.dot(left, right, preferred_element_type=F32)


def iota(shape, dim):
    return lax.broadcasted_iota(jnp.int32, shape, dim)


def signed(index):
    return jnp.where(index < HALF, index, index - N).astype(F32)


def z_rows(real_part, imag_part, kz_wave):
    both = jnp.concatenate([real_part, imag_part], axis=0)
    waves = jnp.concatenate([kz_wave, kz_wave], axis=0)
    return jnp.concatenate([both.astype(BF16), (waves * both).astype(BF16)], axis=1)


def send_planes(out_ref, whole_ref, deriv_ref):
    def one_peer(peer, carry):
        for local in range(ROWS):
            for at, ref in ((0, whole_ref), (HALF, deriv_ref)):
                start = peer * ROWS + local
                real_part = ref[pl.ds(start, ROWS, stride=PITCH), :]
                imag_part = ref[pl.ds(start + N, ROWS, stride=PITCH), :]
                tile = jnp.concatenate([real_part, imag_part], axis=0).astype(BF16)
                out_ref[peer, local, :, at : at + HALF] = tile
        return carry

    lax.fori_loop(0, PEERS, one_peer, 0)


def z_inverse(local, rows, table_ref, whole_ref, deriv_ref):
    found = dot(table_ref[...], rows)
    start = pl.multiple_of(local * PITCH, 8)
    whole_ref[pl.ds(start, 2 * N), :] = found[:, :HALF]
    deriv_ref[pl.ds(start, 2 * N), :] = found[:, HALF:]


def waves_of(info_ref, local):
    ky_wave = signed(info_ref[0] + local)
    kz_wave = signed(iota((N, HALF), 0))
    kx_wave = iota((N, HALF), 1).astype(F32)
    return kz_wave, kx_wave * kx_wave + ky_wave * ky_wave + kz_wave * kz_wave


def start_kernel(info_ref, state_ref, table_ref, out_ref, stats_ref, whole_ref, deriv_ref):
    step = pl.program_id(0)

    @pl.when(step == 0)
    def _():
        stats_ref[...] = jnp.zeros_like(stats_ref)

    for pos in range(GROUP):
        local = step * GROUP + pos
        kz_wave, ksquare = waves_of(info_ref, local)
        real_part = state_ref[0, pos]
        imag_part = state_ref[1, pos]
        weight = jnp.where(iota((N, HALF), 1) == 0, 1.0, 2.0)
        energy = weight * (real_part * real_part + imag_part * imag_part)
        stats_ref[0] += jnp.sum(energy.reshape(N // 8, 8, HALF), axis=0)
        stats_ref[1] += jnp.sum((ksquare * energy).reshape(N // 8, 8, HALF), axis=0)
        z_inverse(local, z_rows(real_part, imag_part, kz_wave), table_ref, whole_ref, deriv_ref)

    @pl.when(step == pl.num_programs(0) - 1)
    def _():
        send_planes(out_ref, whole_ref, deriv_ref)


def in_three(value):
    high = value.astype(BF16).astype(F32)
    rest = value - high
    middle = rest.astype(BF16).astype(F32)
    return high, middle, (rest - middle).astype(BF16).astype(F32)


def packed_four(parts):
    lane = iota((2 * ROWS, HALF), 1)
    turned = [parts[0]] + [pltpu.roll(parts[k], HALF - 32 * k, 1) for k in (1, 2, 3)]
    return [jnp.where(lane < HALF - 32 * (k + 1), turned[k], turned[k + 1]) for k in (0, 1, 2)]


def unpacked_four(packed):
    lane = iota((2 * N, HALF), 1)
    first, second, third = (packed[:, k * HALF : (k + 1) * HALF] for k in (0, 1, 2))
    return [
        first,
        pltpu.roll(jnp.where(lane >= 96, first, second), 32, 1),
        pltpu.roll(jnp.where(lane >= 64, second, third), 64, 1),
        pltpu.roll(third, 96, 1),
    ]


def grid_kernel(
    planes_ref, speed_ref, stats_ref, y_inv_ref, x_inv_ref, x_fwd_ref, y_fwd_ref, out_ref, sums_ref, peak_ref
):
    step = pl.program_id(0)
    pair = planes_ref.shape[1]
    count = 2 * N

    @pl.when(step == 0)
    def _():
        peak_ref[...] = jnp.zeros_like(peak_ref)

    row = iota((count, HALF), 0)
    ky_wave = signed(row // (2 * ROWS) * ROWS + row % ROWS)
    kx_wave = iota((N, HALF), 1).astype(F32)
    came = [planes_ref[:, k].reshape(count, N) for k in range(pair)]
    scaled = [(ky_wave * part[:, :HALF].astype(F32)).astype(BF16) for part in came]
    y_section = dot(y_inv_ref[...], jnp.concatenate(came + scaled, axis=1))
    x_rows = []
    for k in range(pair):
        starts = (k * N, pair * N + k * HALF, k * N + HALF)
        for which, at in enumerate(starts):
            halves = [y_section[part * N : (part + 1) * N, at : at + HALF] for part in (0, 1)]
            if which == 0:
                halves = [kx_wave * half for half in halves]
            x_rows.append(jnp.concatenate(halves, axis=1).astype(BF16))
    gradients = dot(jnp.concatenate(x_rows, axis=0), x_inv_ref[...])
    fields = []
    for k in range(pair):
        parts = [gradients[(3 * k + d) * N : (3 * k + d + 1) * N] for d in range(3)]
        total = speed_ref[0, k].astype(F32) * parts[0]
        total = total + speed_ref[1, k].astype(F32) * parts[1]
        total = total + speed_ref[2, k].astype(F32) * parts[2]
        fields.append(total.astype(BF16))
        square = parts[0] * parts[0] + parts[1] * parts[1] + parts[2] * parts[2]
        peak_ref[...] = jnp.maximum(peak_ref[...], jnp.max(square.reshape(N // 8, 8, N), axis=0))
    x_section = dot(jnp.concatenate(fields, axis=0), x_fwd_ref[...]).astype(BF16)
    columns = []
    for k in range(pair):
        part = x_section[k * N : (k + 1) * N]
        columns.append(jnp.concatenate([part[:, :HALF], part[:, HALF:]], axis=0))
    sums = dot(y_fwd_ref[...], jnp.concatenate(columns, axis=1))
    for k in range(pair):
        start = pl.multiple_of((step * pair + k) * PITCH, 8)
        sums_ref[pl.ds(start, count), :] = sums[:, k * HALF : (k + 1) * HALF]

    @pl.when(step == pl.num_programs(0) - 1)
    def _():
        shape = (2 * ROWS, HALF)
        peak = jnp.sqrt(jnp.max(peak_ref[...], keepdims=True))
        pieces = []
        for value in (jnp.sum(stats_ref[0], keepdims=True), jnp.sum(stats_ref[1], keepdims=True), peak):
            pieces.extend(in_three(jnp.broadcast_to(value, shape)))
        line = jnp.zeros(shape, F32)
        for k, piece in enumerate(pieces):
            line = jnp.where((iota(shape, 0) == 0) & (iota(shape, 1) == LIMIT + k), piece, line)

        def one_peer(peer, carry):
            for group in range(ROWS // GROUP):
                parts = []
                for pos in range(GROUP):
                    start = peer * 2 * ROWS + group * GROUP + pos
                    real_part = sums_ref[pl.ds(start, ROWS, stride=PITCH), :]
                    imag_part = sums_ref[pl.ds(start + ROWS, ROWS, stride=PITCH), :]
                    parts.append(jnp.concatenate([real_part, imag_part], axis=0))
                if group == 0:
                    parts[0] = parts[0] + line
                for k, tile in enumerate(packed_four(parts)):
                    at = (group * 3 + k) * HALF
                    out_ref[peer, :, at : at + HALF] = tile.astype(BF16)
            return carry

        lax.fori_loop(0, PEERS, one_peer, 0)


def tendency(came_ref, table_ref):
    packed = dot(table_ref[...], came_ref[...].reshape(2 * N, GROUP * KEPT))
    return [(part[:N], part[N:]) for part in unpacked_four(packed)]


def middle_kernel(
    info_ref,
    came_ref,
    state_ref,
    base_ref,
    z_fwd_ref,
    z_inv_ref,
    out_ref,
    kept_ref,
    kappa_ref,
    whole_ref,
    deriv_ref,
):
    step = pl.program_id(0)

    @pl.when(step == 0)
    def _():
        shape = (PEERS, 2 * ROWS, HALF)
        found = jnp.where(iota(shape, 1) == 0, came_ref[:, :, :HALF].astype(F32), 0.0)
        lane = iota(shape, 2)

        def piece(which):
            low = LIMIT + 3 * which
            inside = jnp.where((lane >= low) & (lane < low + 3), found, 0.0)
            return jnp.sum(jnp.sum(inside, axis=1), axis=1, keepdims=True)

        def spread(value):
            return jnp.broadcast_to(value, (8, HALF))

        variance = spread(jnp.sum(piece(0), axis=0, keepdims=True)) / CELLS
        mean_grad = spread(jnp.sum(piece(1), axis=0, keepdims=True)) / CELLS
        peak = spread(jnp.max(piece(2), axis=0, keepdims=True))
        match = iota(base_ref.shape, 1) == info_ref[2]
        base = spread(jnp.sum(jnp.where(match, base_ref[...], 0.0), axis=1, keepdims=True))
        kappa_ref[...] = base * peak * jnp.sqrt(variance) / (mean_grad + 1e-06)

    kappa = kappa_ref[0:1, :]
    bound = (info_ref[1] * info_ref[1]).astype(F32)
    for pos, (sum_real, sum_imag) in enumerate(tendency(came_ref, z_fwd_ref)):
        local = step * GROUP + pos
        kz_wave, ksquare = waves_of(info_ref, local)
        factor = jnp.exp(-kappa * ksquare * STEP)
        inside = ksquare <= bound
        first = [jnp.where(inside, -part, 0.0) for part in (sum_real, sum_imag)]
        middle = []
        for part in (0, 1):
            start = state_ref[part, pos]
            middle.append(factor * (start + STEP * first[part]))
            kept_ref[part, pos] = factor * start + (0.5 * STEP) * (factor * first[part])
        z_inverse(local, z_rows(*middle, kz_wave), z_inv_ref, whole_ref, deriv_ref)

    @pl.when(step == pl.num_programs(0) - 1)
    def _():
        send_planes(out_ref, whole_ref, deriv_ref)


def final_kernel(info_ref, came_ref, kept_ref, z_fwd_ref, out_ref):
    step = pl.program_id(0)
    bound = (info_ref[1] * info_ref[1]).astype(F32)
    for pos, sums in enumerate(tendency(came_ref, z_fwd_ref)):
        _, ksquare = waves_of(info_ref, step * GROUP + pos)
        for part in (0, 1):
            second = jnp.where(ksquare <= bound, -sums[part], 0.0)
            out_ref[part, pos] = kept_ref[part, pos] + (0.5 * STEP) * second


def whole(shape):
    return pl.BlockSpec(shape, lambda step: (0,) * len(shape))


SCALARS = pl.BlockSpec(memory_space=pltpu.SMEM)
HELD = pl.BlockSpec((2, GROUP, N, HALF), lambda step: (0, step, 0, 0))
CAME = pl.BlockSpec((PEERS, 2 * ROWS, GROUP * KEPT), lambda step: (0, 0, step))
TABLE = whole((2 * N, 2 * N))
SMALL = whole((N, N))
PLANES = (PEERS, ROWS, 2 * ROWS, N)
PAIR = 2
STATE = (2, ROWS, N, HALF)


def params():
    return pltpu.CompilerParams(dimension_semantics=("arbitrary",))


def shaped(shape, dtype):
    return jax.ShapeDtypeStruct(shape, dtype)


def turned():
    return pltpu.VMEM((ROWS * PITCH, HALF), F32)


def gathered(velocity):
    groups = lax.axis_size("scal")
    me = lax.axis_index("scal")
    ring = 4

    def moved(x, change):
        return lax.ppermute(x, "scal", [(s, change(s)) for s in range(groups)])

    def beside(shift):
        return lambda s: s // ring * ring + (s + shift) % ring

    across = moved(velocity, lambda s: (s + ring) % groups)
    out = jnp.zeros((*velocity.shape[:2], N, N), velocity.dtype)
    high, low = me // ring, me % ring
    half = velocity.shape[1] // 2

    def placed(out, x, owner, first=0):
        return lax.dynamic_update_slice(out, x, (0, first, owner * x.shape[2], 0))

    for x, own in ((velocity, high), (across, 1 - high)):
        up = moved(x, beside(1))
        down = moved(x, beside(-1))
        far_up = moved(up[:, :half], beside(1))
        far_down = moved(down[:, half:], beside(-1))
        start = own * ring
        out = placed(out, x, start + low)
        out = placed(out, up, start + (low + ring - 1) % ring)
        out = placed(out, down, start + (low + 1) % ring)
        out = placed(out, far_up, start + (low + 2) % ring)
        out = placed(out, far_down, start + (low + 2) % ring, half)
    return out


def exchanged(x):
    return lax.all_to_all(x, "fft", 0, 0, tiled=True)


def body(scalar_state, velocity, species, kappa_table, dealias_bound):
    table = tables()
    state = scalar_state[0]
    ky_first = lax.axis_index("fft").astype(jnp.int32) * ROWS
    info = jnp.stack([ky_first, dealias_bound[0], species[0]])
    speeds = gathered(velocity)

    planes, stats = pl.pallas_call(
        start_kernel,
        grid=(ROWS // GROUP,),
        in_specs=[SCALARS, HELD, TABLE],
        out_specs=[whole(PLANES), whole((2, 8, HALF))],
        out_shape=[shaped(PLANES, BF16), shaped((2, 8, HALF), F32)],
        scratch_shapes=[turned(), turned()],
        compiler_params=params(),
        name="start",
    )(info, state, table["z_inv"])

    def grid_side(planes):
        sent = (PEERS, 2 * ROWS, PACKED)
        return pl.pallas_call(
            grid_kernel,
            grid=(ROWS // PAIR,),
            in_specs=[
                pl.BlockSpec((PEERS, PAIR, 2 * ROWS, N), lambda step: (0, step, 0, 0)),
                pl.BlockSpec((3, PAIR, N, N), lambda step: (0, step, 0, 0)),
                whole((2, 8, HALF)),
                TABLE,
                SMALL,
                SMALL,
                TABLE,
            ],
            out_specs=whole(sent),
            out_shape=shaped(sent, BF16),
            scratch_shapes=[turned(), pltpu.VMEM((8, N), F32)],
            compiler_params=params(),
            name="grid",
        )(planes, speeds, stats, table["y_inv"], table["x_inv"], table["x_fwd"], table["y_fwd"])

    came = exchanged(grid_side(exchanged(planes)))
    planes, kept, kappa = pl.pallas_call(
        middle_kernel,
        grid=(ROWS // GROUP,),
        in_specs=[SCALARS, CAME, HELD, whole((1, kappa_table.shape[0])), TABLE, TABLE],
        out_specs=[whole(PLANES), HELD, whole((8, HALF))],
        out_shape=[shaped(PLANES, BF16), shaped(STATE, F32), shaped((8, HALF), F32)],
        scratch_shapes=[turned(), turned()],
        compiler_params=params(),
        name="middle",
    )(info, came, state, kappa_table[None], table["z_fwd"], table["z_inv"])
    came = exchanged(grid_side(exchanged(planes)))
    updated = pl.pallas_call(
        final_kernel,
        grid=(ROWS // GROUP,),
        in_specs=[SCALARS, CAME, HELD, TABLE],
        out_specs=HELD,
        out_shape=shaped(STATE, F32),
        compiler_params=params(),
        name="final",
    )(info, came, kept, table["z_fwd"])
    return (updated[None], kappa[0, :1])


def solution(mesh):
    placed = (
        P("scal", None, "fft", None, None),
        P(None, "fft", "scal", None),
        P("scal"),
        P(),
        P("scal"),
    )
    return jax.shard_map(
        body,
        mesh=mesh,
        in_specs=placed,
        out_specs=(P("scal", None, "fft", None, None), P("scal")),
        check_vma=False,
    )
```

time: 348 us -> 214 us (0.61); the launches traced: 341 us -> 212 us
  matrix products: 90.6 us -> 0 us
  waiting for transfers between devices: 91.2 us -> 51 us
  Pallas kernels: 0 us -> 38.5 us
  blocking collectives: 54.4 us -> 82.6 us
  between operations: 23 us -> 2.12 us
  other arithmetic: 19.3 us -> 0.59 us
  local copies, waits for them, and re-layouts: 21.8 us -> 6.68 us
  starting transfers between devices: 40.6 us -> 30.8 us
    dot_general x36 -> x0, matrix products: 90.6 us -> none  [product(): jnp.einsum(formula, operand, matrix, preferred_element_type=jnp.float32)]
    all_to_all x6 -> x2, waiting for transfers between devices: 90.8 us -> 30.4 us  [exchanged(): return lax.all_to_all(x, 'fft', 0, 0, tiled=True)]
    pallas_call x0 -> x5, Pallas kernels: none -> 38.5 us  [the longest x2 22.8 us: grid_side(): pl.pallas_call(grid_kernel, grid=(ROWS // PAIR,), in_specs=[pl.BlockSpec(...]
    all_to_all x1 -> x2, blocking collectives: 54.4 us -> 82.6 us  [exchanged(): return lax.all_to_all(x, 'fft', 0, 0, tiled=True)]
    all_to_all x6 -> x2, starting transfers between devices: 40.3 us -> 17.1 us  [exchanged(): return lax.all_to_all(x, 'fft', 0, 0, tiled=True)]
    ppermute x0 -> x9, waiting for transfers between devices: none -> 20.6 us  [moved(): return lax.ppermute(x, 'scal', [(s, change(s)) for s in range(groups)])]
    ppermute x0 -> x9, starting transfers between devices: none -> 13.7 us  [moved(): return lax.ppermute(x, 'scal', [(s, change(s)) for s in range(groups)])]
    reduce_max x1 -> x0, other arithmetic: 5.75 us -> none  [body(): local_peak = [jnp.max(magnitude)]]
  transfers between devices with their start and end apart: 7 -> 11, of which waited for: 6 -> 6; matrix products, arithmetic and copies ran while one was open for 15% -> 3% of each run, Pallas kernels for 0% -> 0%
where the time goes in v1:
time: 214 us; the launch traced here: 212 us
  blocking collectives  82.6 us (39%)
  waiting for transfers between devices  51 us (24%)
  Pallas kernels  38.5 us (18%)
  starting transfers between devices  30.8 us (14%)
  local copies, waits for them, and re-layouts  6.68 us (3%)
    all_to_all x2, blocking collectives, exchanged(): return lax.all_to_all(x, 'fft', 0, 0, tiled=True)  82.6 us
    all_to_all x2, waiting for transfers between devices, exchanged(): return lax.all_to_all(x, 'fft', 0, 0, tiled=True)  30.4 us
    pallas_call x2, Pallas kernels, grid_side(): pl.pallas_call(grid_kernel, grid=(ROWS // PAIR,), in_specs=[pl.BlockSpec(...  22.8 us
    ppermute x9, waiting for transfers between devices, moved(): return lax.ppermute(x, 'scal', [(s, change(s)) for s in range(groups)])  20.6 us
    all_to_all x2, starting transfers between devices, exchanged(): return lax.all_to_all(x, 'fft', 0, 0, tiled=True)  17.1 us
    ppermute x9, starting transfers between devices, moved(): return lax.ppermute(x, 'scal', [(s, change(s)) for s in range(groups)])  13.7 us
    pallas_call x1, Pallas kernels, body(): pl.pallas_call(middle_kernel, grid=(ROWS // GROUP,), in_specs=[SCALARS, C...  6.96 us
    pallas_call x1, Pallas kernels, body(): pl.pallas_call(start_kernel, grid=(ROWS // GROUP,), in_specs=[SCALARS, HE...  5.12 us
  transfers between devices with their start and end apart: 11, of which 6 were waited for; matrix products, arithmetic and copies ran while one was open for 3% of the time, Pallas kernels for 0%

profile of v1, /device:TPU:1, one launch (start us, length us, event | category | flops | bytes accessed | tf_op | source)
XLA Modules:
  0.0 212.3 jit_solution(14143654483893450667)
XLA Ops:
  1.9 0.6 pad_add_fusion.info_ref
  2.5 5.1 %start.1 = (bf16[32,8,16,256]{3,2,1,0:T(8,128)(2,1)}, f32[2,8,128]{2,1,0:T(8,128)}) custom-call(s32[3]{0:T(128)} %pad_add_fusion.info_ref, f32[2,8,256,128]{3,2,1,0:T(8,128)} %bitcast.5, bf16[512,512]{1,0:T(8,128)(2,1)} %constant.92.table_ref.z_inv_ref), custom_call_target="tpu_custom_call" | custom-call | tf_op jit(solution)/shard_map/start/pallas_call | solution.py:357
  7.6 11.1 %all-to-all-start = ((bf16[32,8,16,256]{3,2,1,0:T(8,128)(2,1)}), bf16[32,8,16,256]{3,2,1,0:T(8,128)(2,1)}, u32[]{:S(2)}, u32[]{:S(2)}) async-start(bf16[32,8,16,256]{3,2,1,0:T(8,128)(2,1)} %get-tuple-element.7), calls=%async_computation | async-start | bytes 4194304 | tf_op jit(solution)/shard_map/all_to_all | solution.py:347
  18.7 1.4 collective-permute-start
  20.1 1.5 collective-permute-start.1
  21.6 2.5 %collective-permute-start.4 = (bf16[3,8,32,256]{3,2,1,0:T(8,128)(2,1)}, bf16[3,8,32,256]{3,2,1,0:T(8,128)(2,1)}, u32[]{:S(2)}, u32[]{:S(2)}) collective-permute-start(bf16[3,8,32,256]{3,2,1,0:T(8,128)(2,1)} %param.12), channel_id=1, source_target_pairs={{0,4},{1,5},{2,6},{3,7},{4,0},{5,1},{6,2},{7,3},{8,12},{9,13},{10,... | collective-permute-start | bytes 1179656 | tf_op jit(solution)/shard_map/ppermute | solution.py:319
  24.1 0.3 broadcast_in_dim.9
  24.4 1.0 constant_dynamic-update-slice_fusion.9
  25.5 5.4 %collective-permute-done = bf16[3,8,32,256]{3,2,1,0:T(8,128)(2,1)S(1)} collective-permute-done((bf16[3,8,32,256]{3,2,1,0:T(8,128)(2,1)}, bf16[3,8,32,256]{3,2,1,0:T(8,128)(2,1)S(1)}, u32[]{:S(2)}, u32[]{:S(2)}) %collective-permute-start) | collective-permute-done | bytes 393248 | tf_op jit(solution)/shard_map/ppermute | solution.py:319
  30.8 0.1 collective-permute-start.2
  30.9 0.0 collective-permute-done.1
  30.9 0.9 slice.21
  31.9 2.7 %collective-permute-start.3 = (bf16[3,4,32,256]{3,2,1,0:T(8,128)(2,1)S(1)}, bf16[3,4,32,256]{3,2,1,0:T(8,128)(2,1)S(1)}, u32[]{:S(2)}, u32[]{:S(2)}) collective-permute-start(bf16[3,4,32,256]{3,2,1,0:T(8,128)(2,1)S(1)} %slice.21), channel_id=1, source_target_pairs={{0,3},{1,0},{2,1},{3,2},{4,7},{5,4},{6,5},{7,6},{8,11},{9,8},{10,9... | collective-permute-start | bytes 589832 | tf_op jit(solution)/shard_map/ppermute | solution.py:319
  34.6 5.8 %collective-permute-done.4 = bf16[3,8,32,256]{3,2,1,0:T(8,128)(2,1)} collective-permute-done((bf16[3,8,32,256]{3,2,1,0:T(8,128)(2,1)}, bf16[3,8,32,256]{3,2,1,0:T(8,128)(2,1)}, u32[]{:S(2)}, u32[]{:S(2)}) %collective-permute-start.4) | collective-permute-done | bytes 393248 | tf_op jit(solution)/shard_map/ppermute | solution.py:319
  40.4 1.0 collective-permute-start.5
  41.3 1.7 collective-permute-start.6
  43.1 1.0 constant_dynamic-update-slice_fusion.7
  44.1 0.0 collective-permute-done.2
  44.2 0.0 collective-permute-done.3
  44.2 1.0 constant_dynamic-update-slice_fusion.4
  45.2 6.2 %collective-permute-done.5 = bf16[3,8,32,256]{3,2,1,0:T(8,128)(2,1)S(1)} collective-permute-done((bf16[3,8,32,256]{3,2,1,0:T(8,128)(2,1)}, bf16[3,8,32,256]{3,2,1,0:T(8,128)(2,1)S(1)}, u32[]{:S(2)}, u32[]{:S(2)}) %collective-permute-start.5) | collective-permute-done | bytes 393248 | tf_op jit(solution)/shard_map/ppermute | solution.py:319
  51.5 0.1 collective-permute-start.7
  51.6 0.0 collective-permute-done.6
  51.6 2.7 %collective-permute-start.8 = (bf16[3,4,32,256]{3,2,1,0:T(8,128)(2,1)S(1)}, bf16[3,4,32,256]{3,2,1,0:T(8,128)(2,1)S(1)}, u32[]{:S(2)}, u32[]{:S(2)}) collective-permute-start(bf16[3,4,32,256]{3,2,1,0:T(8,128)(2,1)S(1)} %slice.23), channel_id=1, source_target_pairs={{0,3},{1,0},{2,1},{3,2},{4,7},{5,4},{6,5},{7,6},{8,11},{9,8},{10,9... | collective-permute-start | bytes 589832 | tf_op jit(solution)/shard_map/ppermute | solution.py:319
  54.4 3.3 %collective-permute-done.7 = bf16[3,4,32,256]{3,2,1,0:T(8,128)(2,1)S(1)} collective-permute-done((bf16[3,4,32,256]{3,2,1,0:T(8,128)(2,1)S(1)}, bf16[3,4,32,256]{3,2,1,0:T(8,128)(2,1)S(1)}, u32[]{:S(2)}, u32[]{:S(2)}) %collective-permute-start.7) | collective-permute-done | bytes 196640 | tf_op jit(solution)/shard_map/ppermute | solution.py:319
  57.7 0.0 collective-permute-done.8
  57.7 0.0 copy-start
  57.8 10.3 %all-to-all-done.planes_ref = bf16[32,8,16,256]{3,2,1,0:T(8,128)(2,1)} async-done(((bf16[32,8,16,256]{3,2,1,0:T(8,128)(2,1)}), bf16[32,8,16,256]{3,2,1,0:T(8,128)(2,1)}, u32[]{:S(2)}, u32[]{:S(2)}) %all-to-all-start) | async-done | bytes 2097184 | tf_op jit(solution)/shard_map/all_to_all | solution.py:347
  68.0 0.0 copy-done
  68.0 11.4 %grid.2 = bf16[32,16,768]{2,1,0:T(8,128)(2,1)} custom-call(bf16[32,8,16,256]{3,2,1,0:T(8,128)(2,1)} %all-to-all-done.planes_ref, bf16[3,8,256,256]{3,2,1,0:T(8,128)(2,1)} %copy-done, f32[2,8,128]{2,1,0:T(8,128)} %get-tuple-element.8.stats_ref, bf16[512,512]{1,0:T(8,128)(2,1)} %constant.93.y_inv_ref, bf16[256,256]{1,0:T(8,128)(2,1)} %constant.94.x_inv_ref, ...), custom_call_target="tpu_custom_call" | custom-call | tf_op jit(solution)/shard_map/grid/pallas_call | solution.py:370
  79.5 27.0 %all_to_all.20.came_ref = bf16[32,16,768]{2,1,0:T(8,128)(2,1)} all-to-all(bf16[32,16,768]{2,1,0:T(8,128)(2,1)} %grid.2), channel_id=1, replica_groups=mesh['fft'=32,'scal'=8] {'fft'}, dimensions={0} | all-to-all | bytes 1572864 | tf_op jit(solution)/shard_map/all_to_all | solution.py:347
  106.5 7.0 %middle.1 = (bf16[32,8,16,256]{3,2,1,0:T(8,128)(2,1)}, f32[2,8,256,128]{3,2,1,0:T(8,128)}, f32[8,128]{1,0:T(8,128)}) custom-call(s32[3]{0:T(128)} %pad_add_fusion.info_ref, bf16[32,16,768]{2,1,0:T(8,128)(2,1)} %all_to_all.20.came_ref, f32[2,8,256,128]{3,2,1,0:T(8,128)} %bitcast.6, f32[1,64]{1,0:T(1,128)} %bitcast.8, bf16[512,512]{1,0:T(8,128)(2,1)} %constant.97.z_fwd_ref, ...), custom_call_target="tpu_custom_call" | custom-call | tf_op jit(solution)/shard_map/middle/pallas_call | solution.py:390
  113.4 55.6 %all_to_all.21.planes_ref = bf16[32,8,16,256]{3,2,1,0:T(8,128)(2,1)} all-to-all(bf16[32,8,16,256]{3,2,1,0:T(8,128)(2,1)} %get-tuple-element.9), channel_id=1, replica_groups=mesh['fft'=32,'scal'=8] {'fft'}, dimensions={0} | all-to-all | bytes 4194304 | tf_op jit(solution)/shard_map/all_to_all | solution.py:347
  169.0 11.4 %grid.3 = bf16[32,16,768]{2,1,0:T(8,128)(2,1)} custom-call(bf16[32,8,16,256]{3,2,1,0:T(8,128)(2,1)} %all_to_all.21.planes_ref, bf16[3,8,256,256]{3,2,1,0:T(8,128)(2,1)} %copy-done, f32[2,8,128]{2,1,0:T(8,128)} %get-tuple-element.8.stats_ref, bf16[512,512]{1,0:T(8,128)(2,1)} %constant.93.y_inv_ref, bf16[256,256]{1,0:T(8,128)(2,1)} %constant.94.x_inv_ref, ...), custom_call_target="tpu_custom_call" | custom-call | tf_op jit(solution)/shard_map/grid/pallas_call | solution.py:370
  180.4 6.1 %all-to-all-start.3 = ((bf16[32,16,768]{2,1,0:T(8,128)(2,1)}), bf16[32,16,768]{2,1,0:T(8,128)(2,1)S(1)}, u32[]{:S(2)}, u32[]{:S(2)}) async-start(bf16[32,16,768]{2,1,0:T(8,128)(2,1)} %grid.3), calls=%async_computation.3 | async-start | bytes 1572864 | tf_op jit(solution)/shard_map/all_to_all | solution.py:347
  186.5 1.2 slice.19
  187.7 20.1 %all-to-all-done.3.came_ref = bf16[32,16,768]{2,1,0:T(8,128)(2,1)S(1)} async-done(((bf16[32,16,768]{2,1,0:T(8,128)(2,1)}), bf16[32,16,768]{2,1,0:T(8,128)(2,1)S(1)}, u32[]{:S(2)}, u32[]{:S(2)}) %all-to-all-start.3) | async-done | bytes 786464 | tf_op jit(solution)/shard_map/all_to_all | solution.py:347
  207.8 0.0 copy-start.1
  207.8 0.9 copy-done.1
  208.7 3.7 %final.1 = f32[2,8,256,128]{3,2,1,0:T(8,128)} custom-call(s32[3]{0:T(128)} %pad_add_fusion.info_ref, bf16[32,16,768]{2,1,0:T(8,128)(2,1)} %copy-done.1, f32[2,8,256,128]{3,2,1,0:T(8,128)} %get-tuple-element.10.kept_ref, bf16[512,512]{1,0:T(8,128)(2,1)} %constant.97.z_fwd_ref), custom_call_target="tpu_custom_call" | custom-call | tf_op jit(solution)/shard_map/final/pallas_call | solution.py:401
  (10 shorter events, 0.2 us)
Async XLA Ops:
  7.6 60.4 %all-to-all-start = ((bf16[32,8,16,256]{3,2,1,0:T(8,128)(2,1)}), bf16[32,8,16,256]{3,2,1,0:T(8,128)(2,1)}, u32[]{:S(2)}, u32[]{:S(2)}) async-start(bf16[32,8,16,256]{3,2,1,0:T(8,128)(2,1)} %get-tuple-element.7), calls=%async_computation | async-start | bytes 4194304 | tf_op jit(solution)/shard_map/all_to_all | solution.py:347
  18.7 12.1 %collective-permute-start = (bf16[3,8,32,256]{3,2,1,0:T(8,128)(2,1)}, bf16[3,8,32,256]{3,2,1,0:T(8,128)(2,1)S(1)}, u32[]{:S(2)}, u32[]{:S(2)}) collective-permute-start(bf16[3,8,32,256]{3,2,1,0:T(8,128)(2,1)} %param.12), channel_id=1, source_target_pairs={{0,1},{1,2},{2,3},{3,0},{4,5},{5,6},{6,7},{7,4},{8,9},{9,10},{10,1... | collective-permute-start | bytes 1179656 | tf_op jit(solution)/shard_map/ppermute | solution.py:319
  20.1 10.8 %collective-permute-start.1 = (bf16[3,8,32,256]{3,2,1,0:T(8,128)(2,1)}, bf16[3,8,32,256]{3,2,1,0:T(8,128)(2,1)}, u32[]{:S(2)}, u32[]{:S(2)}) collective-permute-start(bf16[3,8,32,256]{3,2,1,0:T(8,128)(2,1)} %param.12), channel_id=1, source_target_pairs={{0,3},{1,0},{2,1},{3,2},{4,7},{5,4},{6,5},{7,6},{8,11},{9,8},{10,9... | collective-permute-start | bytes 1179656 | tf_op jit(solution)/shard_map/ppermute | solution.py:319
  21.6 18.7 %collective-permute-start.4 = (bf16[3,8,32,256]{3,2,1,0:T(8,128)(2,1)}, bf16[3,8,32,256]{3,2,1,0:T(8,128)(2,1)}, u32[]{:S(2)}, u32[]{:S(2)}) collective-permute-start(bf16[3,8,32,256]{3,2,1,0:T(8,128)(2,1)} %param.12), channel_id=1, source_target_pairs={{0,4},{1,5},{2,6},{3,7},{4,0},{5,1},{6,2},{7,3},{8,12},{9,13},{10,... | collective-permute-start | bytes 1179656 | tf_op jit(solution)/shard_map/ppermute | solution.py:319
  30.8 13.3 %collective-permute-start.2 = (bf16[3,4,32,256]{3,2,1,0:T(8,128)(2,1)S(1)}, bf16[3,4,32,256]{3,2,1,0:T(8,128)(2,1)S(1)}, u32[]{:S(2)}, u32[]{:S(2)}) collective-permute-start(bf16[3,4,32,256]{3,2,1,0:T(8,128)(2,1)S(1)} %slice.20), channel_id=1, source_target_pairs={{0,1},{1,2},{2,3},{3,0},{4,5},{5,6},{6,7},{7,4},{8,9},{9,10},{10,1... | collective-permute-start | bytes 589832 | tf_op jit(solution)/shard_map/ppermute | solution.py:319
  31.9 12.3 %collective-permute-start.3 = (bf16[3,4,32,256]{3,2,1,0:T(8,128)(2,1)S(1)}, bf16[3,4,32,256]{3,2,1,0:T(8,128)(2,1)S(1)}, u32[]{:S(2)}, u32[]{:S(2)}) collective-permute-start(bf16[3,4,32,256]{3,2,1,0:T(8,128)(2,1)S(1)} %slice.21), channel_id=1, source_target_pairs={{0,3},{1,0},{2,1},{3,2},{4,7},{5,4},{6,5},{7,6},{8,11},{9,8},{10,9... | collective-permute-start | bytes 589832 | tf_op jit(solution)/shard_map/ppermute | solution.py:319
  40.4 11.1 %collective-permute-start.5 = (bf16[3,8,32,256]{3,2,1,0:T(8,128)(2,1)}, bf16[3,8,32,256]{3,2,1,0:T(8,128)(2,1)S(1)}, u32[]{:S(2)}, u32[]{:S(2)}) collective-permute-start(bf16[3,8,32,256]{3,2,1,0:T(8,128)(2,1)} %collective-permute-done.4), channel_id=1, source_target_pairs={{0,1},{1,2},{2,3},{3,0},{4,5},{5,6},{6,7},{7,4},{8,9},{9,10},{10,1... | collective-permute-start | bytes 1179656 | tf_op jit(solution)/shard_map/ppermute | solution.py:319
  41.3 10.2 %collective-permute-start.6 = (bf16[3,8,32,256]{3,2,1,0:T(8,128)(2,1)}, bf16[3,8,32,256]{3,2,1,0:T(8,128)(2,1)S(1)}, u32[]{:S(2)}, u32[]{:S(2)}) collective-permute-start(bf16[3,8,32,256]{3,2,1,0:T(8,128)(2,1)} %collective-permute-done.4), channel_id=1, source_target_pairs={{0,3},{1,0},{2,1},{3,2},{4,7},{5,4},{6,5},{7,6},{8,11},{9,8},{10,9... | collective-permute-start | bytes 1179656 | tf_op jit(solution)/shard_map/ppermute | solution.py:319
  51.5 6.2 %collective-permute-start.7 = (bf16[3,4,32,256]{3,2,1,0:T(8,128)(2,1)S(1)}, bf16[3,4,32,256]{3,2,1,0:T(8,128)(2,1)S(1)}, u32[]{:S(2)}, u32[]{:S(2)}) collective-permute-start(bf16[3,4,32,256]{3,2,1,0:T(8,128)(2,1)S(1)} %slice.22), channel_id=1, source_target_pairs={{0,1},{1,2},{2,3},{3,0},{4,5},{5,6},{6,7},{7,4},{8,9},{9,10},{10,1... | collective-permute-start | bytes 589832 | tf_op jit(solution)/shard_map/ppermute | solution.py:319
  51.6 6.1 %collective-permute-start.8 = (bf16[3,4,32,256]{3,2,1,0:T(8,128)(2,1)S(1)}, bf16[3,4,32,256]{3,2,1,0:T(8,128)(2,1)S(1)}, u32[]{:S(2)}, u32[]{:S(2)}) collective-permute-start(bf16[3,4,32,256]{3,2,1,0:T(8,128)(2,1)S(1)} %slice.23), channel_id=1, source_target_pairs={{0,3},{1,0},{2,1},{3,2},{4,7},{5,4},{6,5},{7,6},{8,11},{9,8},{10,9... | collective-permute-start | bytes 589832 | tf_op jit(solution)/shard_map/ppermute | solution.py:319
  57.7 10.3 %copy-start = (bf16[3,8,256,256]{3,2,1,0:T(8,128)(2,1)}, bf16[3,8,256,256]{3,2,1,0:T(8,128)(2,1)S(1)}, u32[]{:S(2)}) copy-start(bf16[3,8,256,256]{3,2,1,0:T(8,128)(2,1)S(1)} %constant_dynamic-update-slice_fusion.speed_ref) | copy-start | bytes 9437188
  180.4 27.3 %all-to-all-start.3 = ((bf16[32,16,768]{2,1,0:T(8,128)(2,1)}), bf16[32,16,768]{2,1,0:T(8,128)(2,1)S(1)}, u32[]{:S(2)}, u32[]{:S(2)}) async-start(bf16[32,16,768]{2,1,0:T(8,128)(2,1)} %grid.3), calls=%async_computation.3 | async-start | bytes 1572864 | tf_op jit(solution)/shard_map/all_to_all | solution.py:347
  207.8 0.9 copy-start.1

commit v2 on v1

v2 whole, which is shorter than its diff:
```python
import math

import jax
import jax.numpy as jnp
import numpy as np
from jax import lax
from jax.experimental import pallas as pl
from jax.experimental.pallas import tpu as pltpu
from jax.sharding import PartitionSpec as P

N = 256
HALF = 128
PEERS = 32
ROWS = N // PEERS
GROUP = 4
KEPT = 96
LIMIT = 86
PACKED = ROWS * KEPT
PITCH = 2 * N + 8
STEP = 0.2 * 2.0 * math.pi / N
CELLS = float(N) ** 3
F32 = jnp.float32
BF16 = jnp.bfloat16


def tables():
    index = np.arange(N)
    angles = (index[:, None] * index[None, :] % N).astype(np.float32) * np.float32(2.0 * math.pi / N)
    cos = np.cos(angles) * np.float32(1.0 / math.sqrt(N))
    sin = np.sin(angles) * np.float32(1.0 / math.sqrt(N))
    weight = np.where(np.arange(HALF) == 0, 1.0, 2.0).astype(np.float32)[:, None]
    inverse = np.block([[cos, -sin], [sin, cos]])
    forward = np.block([[cos, sin], [-sin, cos]])
    order = np.arange(2 * N).reshape(2, PEERS, ROWS).transpose(1, 0, 2).reshape(-1)
    x_inv = np.concatenate([-weight * sin[:HALF], -weight * cos[:HALF]], axis=0)
    keep = (np.arange(HALF) < LIMIT).astype(np.float32)[None, :]
    x_fwd = np.concatenate([cos[:, :HALF] * keep, -sin[:, :HALF] * keep], axis=1)
    listed = {
        "z_inv": inverse,
        "y_inv": inverse[:, order],
        "x_inv": x_inv,
        "x_fwd": x_fwd,
        "y_fwd": forward[order, :],
        "z_fwd": forward[:, order],
    }
    return {name: jnp.asarray(value.astype(np.float32)).astype(BF16) for name, value in listed.items()}


def dot(left, right):
    return jnp.dot(left, right, preferred_element_type=F32)


def iota(shape, dim):
    return lax.broadcasted_iota(jnp.int32, shape, dim)


def signed(index):
    return jnp.where(index < HALF, index, index - N).astype(F32)


def z_rows(real_part, imag_part, kz_wave):
    both = jnp.concatenate([real_part, imag_part], axis=0)
    waves = jnp.concatenate([kz_wave, kz_wave], axis=0)
    return jnp.concatenate([both.astype(BF16), (waves * both).astype(BF16)], axis=1)


def send_planes(out_ref, whole_ref, deriv_ref):
    def one_peer(peer, carry):
        for local in range(ROWS):
            for at, ref in ((0, whole_ref), (HALF, deriv_ref)):
                start = peer * ROWS + local
                real_part = ref[pl.ds(start, ROWS, stride=PITCH), :]
                imag_part = ref[pl.ds(start + N, ROWS, stride=PITCH), :]
                tile = jnp.concatenate([real_part, imag_part], axis=0).astype(BF16)
                out_ref[peer, local, :, at : at + HALF] = tile
        return carry

    lax.fori_loop(0, PEERS, one_peer, 0)


def z_inverse(local, rows, table_ref, whole_ref, deriv_ref):
    found = dot(table_ref[...], rows)
    start = pl.multiple_of(local * PITCH, 8)
    whole_ref[pl.ds(start, 2 * N), :] = found[:, :HALF]
    deriv_ref[pl.ds(start, 2 * N), :] = found[:, HALF:]


def waves_of(local):
    ky_wave = signed(lax.axis_index("fft").astype(jnp.int32) * ROWS + local)
    kz_wave = signed(iota((N, HALF), 0))
    kx_wave = iota((N, HALF), 1).astype(F32)
    return kz_wave, kx_wave * kx_wave + ky_wave * ky_wave + kz_wave * kz_wave


def start_kernel(state_ref, table_ref, out_ref, stats_ref, whole_ref, deriv_ref):
    step = pl.program_id(0)
    rows = state_ref.shape[1]

    @pl.when(step == 0)
    def _():
        stats_ref[...] = jnp.zeros_like(stats_ref)

    for pos in range(rows):
        local = step * rows + pos
        kz_wave, ksquare = waves_of(local)
        real_part = state_ref[0, pos]
        imag_part = state_ref[1, pos]
        weight = jnp.where(iota((N, HALF), 1) == 0, 1.0, 2.0)
        energy = weight * (real_part * real_part + imag_part * imag_part)
        stats_ref[0] += jnp.sum(energy.reshape(N // 8, 8, HALF), axis=0)
        stats_ref[1] += jnp.sum((ksquare * energy).reshape(N // 8, 8, HALF), axis=0)
        z_inverse(local, z_rows(real_part, imag_part, kz_wave), table_ref, whole_ref, deriv_ref)

    @pl.when(step == pl.num_programs(0) - 1)
    def _():
        send_planes(out_ref, whole_ref, deriv_ref)


def in_three(value):
    high = value.astype(BF16).astype(F32)
    rest = value - high
    middle = rest.astype(BF16).astype(F32)
    return high, middle, (rest - middle).astype(BF16).astype(F32)


def packed_four(parts):
    lane = iota((2 * ROWS, HALF), 1)
    turned = [parts[0]] + [pltpu.roll(parts[k], HALF - 32 * k, 1) for k in (1, 2, 3)]
    return [jnp.where(lane < HALF - 32 * (k + 1), turned[k], turned[k + 1]) for k in (0, 1, 2)]


def unpacked_four(packed):
    lane = iota((2 * N, HALF), 1)
    first, second, third = (packed[:, k * HALF : (k + 1) * HALF] for k in (0, 1, 2))
    return [
        first,
        pltpu.roll(jnp.where(lane >= 96, first, second), 32, 1),
        pltpu.roll(jnp.where(lane >= 64, second, third), 64, 1),
        pltpu.roll(third, 96, 1),
    ]


def grid_kernel(
    planes_ref, speed_ref, stats_ref, y_inv_ref, x_inv_ref, x_fwd_ref, y_fwd_ref, out_ref, sums_ref, peak_ref
):
    count = 2 * N
    peak_ref[...] = jnp.zeros_like(peak_ref)
    row = iota((count, HALF), 0)
    ky_wave = signed(row // (2 * ROWS) * ROWS + row % ROWS)
    kx_wave = iota((N, HALF), 1).astype(F32)

    def one_pair(step, carry):
        came = [planes_ref[:, step * PAIR + k].reshape(count, N) for k in range(PAIR)]
        scaled = [(ky_wave * part[:, :HALF].astype(F32)).astype(BF16) for part in came]
        y_section = dot(y_inv_ref[...], jnp.concatenate(came + scaled, axis=1))
        x_rows = []
        for k in range(PAIR):
            starts = (k * N, PAIR * N + k * HALF, k * N + HALF)
            for which, at in enumerate(starts):
                halves = [y_section[part * N : (part + 1) * N, at : at + HALF] for part in (0, 1)]
                if which == 0:
                    halves = [kx_wave * half for half in halves]
                x_rows.append(jnp.concatenate(halves, axis=1).astype(BF16))
        gradients = dot(jnp.concatenate(x_rows, axis=0), x_inv_ref[...])
        fields = []
        for k in range(PAIR):
            parts = [gradients[(3 * k + d) * N : (3 * k + d + 1) * N] for d in range(3)]
            total = speed_ref[0, step * PAIR + k].astype(F32) * parts[0]
            total = total + speed_ref[1, step * PAIR + k].astype(F32) * parts[1]
            total = total + speed_ref[2, step * PAIR + k].astype(F32) * parts[2]
            fields.append(total.astype(BF16))
            square = parts[0] * parts[0] + parts[1] * parts[1] + parts[2] * parts[2]
            peak_ref[...] = jnp.maximum(peak_ref[...], jnp.max(square.reshape(N // 8, 8, N), axis=0))
        x_section = dot(jnp.concatenate(fields, axis=0), x_fwd_ref[...]).astype(BF16)
        columns = []
        for k in range(PAIR):
            part = x_section[k * N : (k + 1) * N]
            columns.append(jnp.concatenate([part[:, :HALF], part[:, HALF:]], axis=0))
        sums = dot(y_fwd_ref[...], jnp.concatenate(columns, axis=1))
        for k in range(PAIR):
            start = pl.multiple_of((step * PAIR + k) * PITCH, 8)
            sums_ref[pl.ds(start, count), :] = sums[:, k * HALF : (k + 1) * HALF]
        return carry

    lax.fori_loop(0, ROWS // PAIR, one_pair, 0)
    shape = (2 * ROWS, HALF)
    peak = jnp.sqrt(jnp.max(peak_ref[...], keepdims=True))
    pieces = []
    for value in (jnp.sum(stats_ref[0], keepdims=True), jnp.sum(stats_ref[1], keepdims=True), peak):
        pieces.extend(in_three(jnp.broadcast_to(value, shape)))
    line = jnp.zeros(shape, F32)
    for k, piece in enumerate(pieces):
        line = jnp.where((iota(shape, 0) == 0) & (iota(shape, 1) == LIMIT + k), piece, line)

    def one_peer(peer, carry):
        for group in range(ROWS // GROUP):
            parts = []
            for pos in range(GROUP):
                start = peer * 2 * ROWS + group * GROUP + pos
                real_part = sums_ref[pl.ds(start, ROWS, stride=PITCH), :]
                imag_part = sums_ref[pl.ds(start + ROWS, ROWS, stride=PITCH), :]
                parts.append(jnp.concatenate([real_part, imag_part], axis=0))
            if group == 0:
                parts[0] = parts[0] + line
            for k, tile in enumerate(packed_four(parts)):
                at = (group * 3 + k) * HALF
                out_ref[peer, :, at : at + HALF] = tile.astype(BF16)
        return carry

    lax.fori_loop(0, PEERS, one_peer, 0)


def tendency(came_ref, table_ref, group):
    at = group * GROUP * KEPT
    packed = dot(table_ref[...], came_ref[:, :, at : at + GROUP * KEPT].reshape(2 * N, GROUP * KEPT))
    return [(part[:N], part[N:]) for part in unpacked_four(packed)]


def middle_kernel(
    bound_ref,
    species_ref,
    came_ref,
    state_ref,
    base_ref,
    z_fwd_ref,
    z_inv_ref,
    out_ref,
    kept_ref,
    kappa_ref,
    whole_ref,
    deriv_ref,
):
    shape = (PEERS, 2 * ROWS, HALF)
    found = jnp.where(iota(shape, 1) == 0, came_ref[:, :, :HALF].astype(F32), 0.0)
    lane = iota(shape, 2)

    def piece(which):
        low = LIMIT + 3 * which
        inside = jnp.where((lane >= low) & (lane < low + 3), found, 0.0)
        return jnp.sum(jnp.sum(inside, axis=1), axis=1, keepdims=True)

    def spread(value):
        return jnp.broadcast_to(value, (8, HALF))

    variance = spread(jnp.sum(piece(0), axis=0, keepdims=True)) / CELLS
    mean_grad = spread(jnp.sum(piece(1), axis=0, keepdims=True)) / CELLS
    peak = spread(jnp.max(piece(2), axis=0, keepdims=True))
    match = iota(base_ref.shape, 1) == species_ref[0]
    base = spread(jnp.sum(jnp.where(match, base_ref[...], 0.0), axis=1, keepdims=True))
    kappa_ref[...] = base * peak * jnp.sqrt(variance) / (mean_grad + 1e-06)
    kappa = kappa_ref[0:1, :]
    bound = (bound_ref[0] * bound_ref[0]).astype(F32)
    for group in range(ROWS // GROUP):
        for pos, (sum_real, sum_imag) in enumerate(tendency(came_ref, z_fwd_ref, group)):
            local = group * GROUP + pos
            kz_wave, ksquare = waves_of(local)
            factor = jnp.exp(-kappa * ksquare * STEP)
            inside = ksquare <= bound
            first = [jnp.where(inside, -part, 0.0) for part in (sum_real, sum_imag)]
            middle = []
            for part in (0, 1):
                start = state_ref[part, local]
                middle.append(factor * (start + STEP * first[part]))
                kept_ref[part, local] = factor * start + (0.5 * STEP) * (factor * first[part])
            z_inverse(local, z_rows(*middle, kz_wave), z_inv_ref, whole_ref, deriv_ref)
    send_planes(out_ref, whole_ref, deriv_ref)


def final_kernel(bound_ref, came_ref, kept_ref, z_fwd_ref, out_ref):
    bound = (bound_ref[0] * bound_ref[0]).astype(F32)
    for group in range(ROWS // GROUP):
        for pos, sums in enumerate(tendency(came_ref, z_fwd_ref, group)):
            local = group * GROUP + pos
            _, ksquare = waves_of(local)
            for part in (0, 1):
                second = jnp.where(ksquare <= bound, -sums[part], 0.0)
                out_ref[part, local] = kept_ref[part, local] + (0.5 * STEP) * second


SCALARS = pl.BlockSpec(memory_space=pltpu.SMEM)
NEAR = pl.BlockSpec(memory_space=pltpu.VMEM)
PLANES = (PEERS, ROWS, 2 * ROWS, N)
SENT = (PEERS, 2 * ROWS, PACKED)
STATE = (2, ROWS, N, HALF)
PAIR = 2
AHEAD = 2


def params(mebibytes):
    return pltpu.CompilerParams(vmem_limit_bytes=mebibytes * 2**20)


def shaped(shape, dtype):
    return jax.ShapeDtypeStruct(shape, dtype)


def near(x):
    return pltpu.with_memory_space_constraint(x, pltpu.VMEM)


def turned():
    return pltpu.VMEM((ROWS * PITCH, HALF), F32)


def gathered(velocity):
    groups = lax.axis_size("scal")
    me = lax.axis_index("scal")
    ring = 4

    def moved(x, change):
        return lax.ppermute(x, "scal", [(s, change(s)) for s in range(groups)])

    def beside(shift):
        return lambda s: s // ring * ring + (s + shift) % ring

    across = moved(velocity, lambda s: (s + ring) % groups)
    out = jnp.zeros((*velocity.shape[:2], N, N), velocity.dtype)
    high, low = me // ring, me % ring
    half = velocity.shape[1] // 2

    def placed(out, x, owner, first=0):
        return lax.dynamic_update_slice(out, x, (0, first, owner * x.shape[2], 0))

    for x, own in ((velocity, high), (across, 1 - high)):
        up = moved(x, beside(1))
        down = moved(x, beside(-1))
        far_up = moved(up[:, :half], beside(1))
        far_down = moved(down[:, half:], beside(-1))
        start = own * ring
        out = placed(out, x, start + low)
        out = placed(out, up, start + (low + ring - 1) % ring)
        out = placed(out, down, start + (low + 1) % ring)
        out = placed(out, far_up, start + (low + 2) % ring)
        out = placed(out, far_down, start + (low + 2) % ring, half)
    return out


def exchanged(x):
    return lax.all_to_all(x, "fft", 0, 0, tiled=True)


def start_call(state, table):
    return pl.pallas_call(
        start_kernel,
        grid=(ROWS // AHEAD,),
        in_specs=[pl.BlockSpec((2, AHEAD, N, HALF), lambda step: (0, step, 0, 0)), NEAR],
        out_specs=[NEAR, NEAR],
        out_shape=[pltpu.VMEM(PLANES, BF16), pltpu.VMEM((2, 8, HALF), F32)],
        scratch_shapes=[turned(), turned()],
        compiler_params=params(24),
        name="start",
    )(state, near(table["z_inv"]))


def grid_call(planes, speeds, stats, table):
    return pl.pallas_call(
        grid_kernel,
        in_specs=[NEAR] * 7,
        out_specs=NEAR,
        out_shape=pltpu.VMEM(SENT, BF16),
        scratch_shapes=[turned(), pltpu.VMEM((8, N), F32)],
        compiler_params=params(24),
        name="grid",
    )(
        *(near(x) for x in (planes, speeds, stats)),
        *(near(table[name]) for name in ("y_inv", "x_inv", "x_fwd", "y_fwd")),
    )


def middle_call(bound, species, came, state, kappa_table, table):
    return pl.pallas_call(
        middle_kernel,
        in_specs=[SCALARS, SCALARS] + [NEAR] * 5,
        out_specs=[NEAR] * 3,
        out_shape=[pltpu.VMEM(PLANES, BF16), pltpu.VMEM(STATE, F32), shaped((8, HALF), F32)],
        scratch_shapes=[turned(), turned()],
        compiler_params=params(24),
        name="middle",
    )(
        bound,
        species,
        near(came),
        near(state),
        kappa_table[None],
        near(table["z_fwd"]),
        near(table["z_inv"]),
    )


def final_call(bound, came, kept, table):
    return pl.pallas_call(
        final_kernel,
        in_specs=[SCALARS] + [NEAR] * 3,
        out_specs=NEAR,
        out_shape=shaped(STATE, F32),
        compiler_params=params(16),
        name="final",
    )(bound, near(came), near(kept), near(table["z_fwd"]))


def body(scalar_state, velocity, species, kappa_table, dealias_bound):
    table = tables()
    state = scalar_state[0]
    speeds = gathered(velocity)
    planes, stats = start_call(state, table)
    came = exchanged(grid_call(exchanged(planes), speeds, stats, table))
    planes, kept, kappa = middle_call(dealias_bound, species, came, state, kappa_table, table)
    came = exchanged(grid_call(exchanged(planes), speeds, stats, table))
    return (final_call(dealias_bound, came, kept, table)[None], kappa[0, :1])


def solution(mesh):
    placed = (
        P("scal", None, "fft", None, None),
        P(None, "fft", "scal", None),
        P("scal"),
        P(),
        P("scal"),
    )
    return jax.shard_map(
        body,
        mesh=mesh,
        in_specs=placed,
        out_specs=(P("scal", None, "fft", None, None), P("scal")),
        check_vma=False,
    )
```

time: 214 us -> 216 us (level)
  blocking collectives: 82.6 us -> 54.3 us
  waiting for transfers between devices: 51 us -> 69.8 us
  local copies, waits for them, and re-layouts: 6.68 us -> 21.1 us
  Pallas kernels: 38.5 us -> 30.1 us
  starting transfers between devices: 30.8 us -> 36.4 us
    all_to_all x2 -> x1, blocking collectives: 82.6 us -> 54.3 us  [exchanged(): return lax.all_to_all(x, 'fft', 0, 0, tiled=True)]
    all_to_all x2 -> x3, waiting for transfers between devices: 30.4 us -> 51.1 us  [exchanged(): return lax.all_to_all(x, 'fft', 0, 0, tiled=True)]
    unnamed x4 -> x34, local copies, waits for them, and re-layouts: 0.91 us -> 14.1 us
    pallas_call x5, Pallas kernels: 38.5 us -> 30.1 us  [the longest x2 19.3 us: grid_call(): pl.pallas_call(grid_kernel, in_specs=[NEAR] * 7, out_specs=NEAR, out_shap...]
    all_to_all x2 -> x3, starting transfers between devices: 17.1 us -> 22.7 us  [exchanged(): return lax.all_to_all(x, 'fft', 0, 0, tiled=True)]
  transfers between devices with their start and end apart: 11 -> 12, of which waited for: 6 -> 7; matrix products, arithmetic and copies ran while one was open for 3% -> 3% of each run, Pallas kernels for 0% -> 0%
where the time goes in v2:
time: 216 us; the launch traced here: 214 us
  waiting for transfers between devices  69.8 us (32%)
  blocking collectives  54.3 us (25%)
  starting transfers between devices  36.4 us (17%)
  Pallas kernels  30.1 us (14%)
  local copies, waits for them, and re-layouts  21.1 us (10%)
  between operations  2.17 us (1%)
    all_to_all x1, blocking collectives, exchanged(): return lax.all_to_all(x, 'fft', 0, 0, tiled=True)  54.3 us
    all_to_all x3, waiting for transfers between devices, exchanged(): return lax.all_to_all(x, 'fft', 0, 0, tiled=True)  51.1 us
    all_to_all x3, starting transfers between devices, exchanged(): return lax.all_to_all(x, 'fft', 0, 0, tiled=True)  22.7 us
    pallas_call x2, Pallas kernels, grid_call(): pl.pallas_call(grid_kernel, in_specs=[NEAR] * 7, out_specs=NEAR, out_shap...  19.3 us
    ppermute x9, waiting for transfers between devices, moved(): return lax.ppermute(x, 'scal', [(s, change(s)) for s in range(groups)])  18.7 us
    unnamed x34, local copies, waits for them, and re-layouts  14.1 us
    ppermute x9, starting transfers between devices, moved(): return lax.ppermute(x, 'scal', [(s, change(s)) for s in range(groups)])  13.7 us
    pallas_call x1, Pallas kernels, middle_call(): pl.pallas_call(middle_kernel, in_specs=[SCALARS, SCALARS] + [NEAR] * 5, o...  4.4 us
  transfers between devices with their start and end apart: 12, of which 7 were waited for; matrix products, arithmetic and copies ran while one was open for 3% of the time, Pallas kernels for 0%

profile of v2, /device:TPU:1, one launch (start us, length us, event | category | flops | bytes accessed | tf_op | source)
XLA Modules:
  0.0 213.9 jit_solution(4758369062508478680)
XLA Ops:
  0.6 0.0 copy-start
  0.6 1.6 copy-done
  2.2 1.0 copy-done.4
  3.3 4.3 %start.1 = (bf16[32,8,16,256]{3,2,1,0:T(8,128)(2,1)}, f32[2,8,128]{2,1,0:T(8,128)S(1)}) custom-call(f32[2,8,256,128]{3,2,1,0:T(8,128)S(1)} %bitcast.4, bf16[512,512]{1,0:T(8,128)(2,1)S(1)} %copy-done.4), custom_call_target="tpu_custom_call" | custom-call | tf_op jit(solution)/shard_map/start/pallas_call | solution.py:343
  7.5 11.1 %all-to-all-start = ((bf16[32,8,16,256]{3,2,1,0:T(8,128)(2,1)}), bf16[32,8,16,256]{3,2,1,0:T(8,128)(2,1)}, u32[]{:S(2)}, u32[]{:S(2)}) async-start(bf16[32,8,16,256]{3,2,1,0:T(8,128)(2,1)} %get-tuple-element.7), calls=%async_computation | async-start | bytes 4194304 | tf_op jit(solution)/shard_map/all_to_all | solution.py:339
  18.6 1.4 collective-permute-start
  20.0 1.5 collective-permute-start.1
  21.5 2.4 %collective-permute-start.4 = (bf16[3,8,32,256]{3,2,1,0:T(8,128)(2,1)}, bf16[3,8,32,256]{3,2,1,0:T(8,128)(2,1)}, u32[]{:S(2)}, u32[]{:S(2)}) collective-permute-start(bf16[3,8,32,256]{3,2,1,0:T(8,128)(2,1)} %param.12), channel_id=1, source_target_pairs={{0,4},{1,5},{2,6},{3,7},{4,0},{5,1},{6,2},{7,3},{8,12},{9,13},{10,... | collective-permute-start | bytes 1179656 | tf_op jit(solution)/shard_map/ppermute | solution.py:311
  24.0 0.3 broadcast_in_dim.9
  24.3 1.0 constant_dynamic-update-slice_fusion.9
  25.4 5.4 %collective-permute-done = bf16[3,8,32,256]{3,2,1,0:T(8,128)(2,1)} collective-permute-done((bf16[3,8,32,256]{3,2,1,0:T(8,128)(2,1)}, bf16[3,8,32,256]{3,2,1,0:T(8,128)(2,1)}, u32[]{:S(2)}, u32[]{:S(2)}) %collective-permute-start) | collective-permute-done | bytes 393248 | tf_op jit(solution)/shard_map/ppermute | solution.py:311
  30.7 0.9 slice.20
  31.7 0.1 collective-permute-start.2
  31.8 0.9 slice.21
  32.7 0.0 copy-start.14
  32.7 0.0 copy-start.15
  32.8 2.7 %collective-permute-start.3 = (bf16[3,4,32,256]{3,2,1,0:T(8,128)(2,1)S(1)}, bf16[3,4,32,256]{3,2,1,0:T(8,128)(2,1)S(1)}, u32[]{:S(2)}, u32[]{:S(2)}) collective-permute-start(bf16[3,4,32,256]{3,2,1,0:T(8,128)(2,1)S(1)} %slice.21), channel_id=1, source_target_pairs={{0,3},{1,0},{2,1},{3,2},{4,7},{5,4},{6,5},{7,6},{8,11},{9,8},{10,9... | collective-permute-start | bytes 589832 | tf_op jit(solution)/shard_map/ppermute | solution.py:311
  35.5 4.8 %collective-permute-done.4 = bf16[3,8,32,256]{3,2,1,0:T(8,128)(2,1)} collective-permute-done((bf16[3,8,32,256]{3,2,1,0:T(8,128)(2,1)}, bf16[3,8,32,256]{3,2,1,0:T(8,128)(2,1)}, u32[]{:S(2)}, u32[]{:S(2)}) %collective-permute-start.4) | collective-permute-done | bytes 393248 | tf_op jit(solution)/shard_map/ppermute | solution.py:311
  40.3 0.9 collective-permute-start.5
  41.2 1.7 collective-permute-start.6
  43.0 1.0 constant_dynamic-update-slice_fusion.8
  44.0 1.0 constant_dynamic-update-slice_fusion.7
  45.1 1.0 constant_dynamic-update-slice_fusion.4
  46.1 5.2 %collective-permute-done.5 = bf16[3,8,32,256]{3,2,1,0:T(8,128)(2,1)S(1)} collective-permute-done((bf16[3,8,32,256]{3,2,1,0:T(8,128)(2,1)}, bf16[3,8,32,256]{3,2,1,0:T(8,128)(2,1)S(1)}, u32[]{:S(2)}, u32[]{:S(2)}) %collective-permute-start.5) | collective-permute-done | bytes 393248 | tf_op jit(solution)/shard_map/ppermute | solution.py:311
  51.4 0.1 collective-permute-start.7
  51.5 2.7 %collective-permute-start.8 = (bf16[3,4,32,256]{3,2,1,0:T(8,128)(2,1)S(1)}, bf16[3,4,32,256]{3,2,1,0:T(8,128)(2,1)S(1)}, u32[]{:S(2)}, u32[]{:S(2)}) collective-permute-start(bf16[3,4,32,256]{3,2,1,0:T(8,128)(2,1)S(1)} %slice.23), channel_id=1, source_target_pairs={{0,3},{1,0},{2,1},{3,2},{4,7},{5,4},{6,5},{7,6},{8,11},{9,8},{10,9... | collective-permute-start | bytes 589832 | tf_op jit(solution)/shard_map/ppermute | solution.py:311
  54.3 3.3 %collective-permute-done.7 = bf16[3,4,32,256]{3,2,1,0:T(8,128)(2,1)S(1)} collective-permute-done((bf16[3,4,32,256]{3,2,1,0:T(8,128)(2,1)S(1)}, bf16[3,4,32,256]{3,2,1,0:T(8,128)(2,1)S(1)}, u32[]{:S(2)}, u32[]{:S(2)}) %collective-permute-start.7) | collective-permute-done | bytes 196640 | tf_op jit(solution)/shard_map/ppermute | solution.py:311
  57.6 10.3 %all-to-all-done.planes_ref = bf16[32,8,16,256]{3,2,1,0:T(8,128)(2,1)} async-done(((bf16[32,8,16,256]{3,2,1,0:T(8,128)(2,1)}), bf16[32,8,16,256]{3,2,1,0:T(8,128)(2,1)}, u32[]{:S(2)}, u32[]{:S(2)}) %all-to-all-start) | async-done | bytes 2097184 | tf_op jit(solution)/shard_map/all_to_all | solution.py:339
  67.9 1.0 copy-done.6
  69.0 1.0 copy-done.8
  70.0 10.4 %grid.2 = bf16[32,16,768]{2,1,0:T(8,128)(2,1)S(1)} custom-call(bf16[32,8,16,256]{3,2,1,0:T(8,128)(2,1)} %all-to-all-done.planes_ref, bf16[3,8,256,256]{3,2,1,0:T(8,128)(2,1)S(1)} %constant_dynamic-update-slice_fusion.speed_ref, f32[2,8,128]{2,1,0:T(8,128)S(1)} %get-tuple-element.8.stats_ref, bf16[512,512]{1,0:T(8,128)(2,1)S(1)} %copy-done.6, ...), custom_call_target="tpu_custom_call" | custom-call | tf_op jit(solution)/shard_map/grid/pallas_call | solution.py:356
  80.5 0.9 copy-done.3
  81.4 5.7 %all-to-all-start.1 = ((bf16[32,16,768]{2,1,0:T(8,128)(2,1)}), bf16[32,16,768]{2,1,0:T(8,128)(2,1)}, u32[]{:S(2)}, u32[]{:S(2)}) async-start(bf16[32,16,768]{2,1,0:T(8,128)(2,1)} %copy-done.3), calls=%async_computation.1 | async-start | bytes 1572864 | tf_op jit(solution)/shard_map/all_to_all | solution.py:339
  88.4 20.0 %all-to-all-done.1.came_ref = bf16[32,16,768]{2,1,0:T(8,128)(2,1)} async-done(((bf16[32,16,768]{2,1,0:T(8,128)(2,1)}), bf16[32,16,768]{2,1,0:T(8,128)(2,1)}, u32[]{:S(2)}, u32[]{:S(2)}) %all-to-all-start.1) | async-done | bytes 786464 | tf_op jit(solution)/shard_map/all_to_all | solution.py:339
  108.4 1.6 copy-done.1
  110.0 1.0 copy-done.5
  111.0 1.0 copy-done.12
  112.1 4.4 %middle.1 = (bf16[32,8,16,256]{3,2,1,0:T(8,128)(2,1)S(1)}, f32[2,8,256,128]{3,2,1,0:T(8,128)S(1)}, f32[8,128]{1,0:T(8,128)S(1)}) custom-call(s32[1]{0:T(128)S(6)} %copy.24.bound_ref, s32[1]{0:T(128)S(6)} %copy.23.species_ref, bf16[32,16,768]{2,1,0:T(8,128)(2,1)} %all-to-all-done.1.came_ref, f32[2,8,256,128]{3,2,1,0:T(8,128)S(1)} %bitcast.5, ...), custom_call_target="tpu_custom_call" | custom-call | tf_op jit(solution)/shard_map/middle/pallas_call | solution.py:371
  116.5 1.3 copy-done.10
  117.8 54.3 %all_to_all.20.planes_ref = bf16[32,8,16,256]{3,2,1,0:T(8,128)(2,1)S(1)} all-to-all(bf16[32,8,16,256]{3,2,1,0:T(8,128)(2,1)S(1)} %get-tuple-element.9), channel_id=1, replica_groups=mesh['fft'=32,'scal'=8] {'fft'}, dimensions={0} | all-to-all | bytes 4194304 | tf_op jit(solution)/shard_map/all_to_all | solution.py:339
  172.1 8.8 %grid.3 = bf16[32,16,768]{2,1,0:T(8,128)(2,1)S(1)} custom-call(bf16[32,8,16,256]{3,2,1,0:T(8,128)(2,1)S(1)} %all_to_all.20.planes_ref, bf16[3,8,256,256]{3,2,1,0:T(8,128)(2,1)S(1)} %constant_dynamic-update-slice_fusion.speed_ref, f32[2,8,128]{2,1,0:T(8,128)S(1)} %get-tuple-element.8.stats_ref, bf16[512,512]{1,0:T(8,128)(2,1)S(1)} %copy-done.7, ...), custom_call_target="tpu_custom_call" | custom-call | tf_op jit(solution)/shard_map/grid/pallas_call | solution.py:356
  180.9 0.9 copy-done.2
  181.8 5.9 %all-to-all-start.3 = ((bf16[32,16,768]{2,1,0:T(8,128)(2,1)}), bf16[32,16,768]{2,1,0:T(8,128)(2,1)S(1)}, u32[]{:S(2)}, u32[]{:S(2)}) async-start(bf16[32,16,768]{2,1,0:T(8,128)(2,1)} %copy-done.2), calls=%async_computation.3 | async-start | bytes 1572864 | tf_op jit(solution)/shard_map/all_to_all | solution.py:339
  187.8 0.5 slice.19
  188.3 20.8 %all-to-all-done.3.came_ref = bf16[32,16,768]{2,1,0:T(8,128)(2,1)S(1)} async-done(((bf16[32,16,768]{2,1,0:T(8,128)(2,1)}), bf16[32,16,768]{2,1,0:T(8,128)(2,1)S(1)}, u32[]{:S(2)}, u32[]{:S(2)}) %all-to-all-start.3) | async-done | bytes 786464 | tf_op jit(solution)/shard_map/all_to_all | solution.py:339
  209.0 1.6 copy-done.11
  210.6 1.0 copy-done.13
  211.7 2.2 %final.1 = f32[2,8,256,128]{3,2,1,0:T(8,128)} custom-call(s32[1]{0:T(128)S(6)} %copy.24.bound_ref, bf16[32,16,768]{2,1,0:T(8,128)(2,1)S(1)} %all-to-all-done.3.came_ref, f32[2,8,256,128]{3,2,1,0:T(8,128)S(1)} %copy-done.11, bf16[512,512]{1,0:T(8,128)(2,1)S(1)} %copy-done.13), custom_call_target="tpu_custom_call" | custom-call | tf_op jit(solution)/shard_map/final/pallas_call | solution.py:391
  (32 shorter events, 0.2 us)
Async XLA Ops:
  0.6 1.6 copy-start
  2.2 1.0 copy-start.4
  7.5 60.4 %all-to-all-start = ((bf16[32,8,16,256]{3,2,1,0:T(8,128)(2,1)}), bf16[32,8,16,256]{3,2,1,0:T(8,128)(2,1)}, u32[]{:S(2)}, u32[]{:S(2)}) async-start(bf16[32,8,16,256]{3,2,1,0:T(8,128)(2,1)} %get-tuple-element.7), calls=%async_computation | async-start | bytes 4194304 | tf_op jit(solution)/shard_map/all_to_all | solution.py:339
  18.6 12.1 %collective-permute-start = (bf16[3,8,32,256]{3,2,1,0:T(8,128)(2,1)}, bf16[3,8,32,256]{3,2,1,0:T(8,128)(2,1)}, u32[]{:S(2)}, u32[]{:S(2)}) collective-permute-start(bf16[3,8,32,256]{3,2,1,0:T(8,128)(2,1)} %param.12), channel_id=1, source_target_pairs={{0,1},{1,2},{2,3},{3,0},{4,5},{5,6},{6,7},{7,4},{8,9},{9,10},{10,1... | collective-permute-start | bytes 1179656 | tf_op jit(solution)/shard_map/ppermute | solution.py:311
  20.0 11.8 %collective-permute-start.1 = (bf16[3,8,32,256]{3,2,1,0:T(8,128)(2,1)}, bf16[3,8,32,256]{3,2,1,0:T(8,128)(2,1)}, u32[]{:S(2)}, u32[]{:S(2)}) collective-permute-start(bf16[3,8,32,256]{3,2,1,0:T(8,128)(2,1)} %param.12), channel_id=1, source_target_pairs={{0,3},{1,0},{2,1},{3,2},{4,7},{5,4},{6,5},{7,6},{8,11},{9,8},{10,9... | collective-permute-start | bytes 1179656 | tf_op jit(solution)/shard_map/ppermute | solution.py:311
  21.5 18.7 %collective-permute-start.4 = (bf16[3,8,32,256]{3,2,1,0:T(8,128)(2,1)}, bf16[3,8,32,256]{3,2,1,0:T(8,128)(2,1)}, u32[]{:S(2)}, u32[]{:S(2)}) collective-permute-start(bf16[3,8,32,256]{3,2,1,0:T(8,128)(2,1)} %param.12), channel_id=1, source_target_pairs={{0,4},{1,5},{2,6},{3,7},{4,0},{5,1},{6,2},{7,3},{8,12},{9,13},{10,... | collective-permute-start | bytes 1179656 | tf_op jit(solution)/shard_map/ppermute | solution.py:311
  31.7 13.3 %collective-permute-start.2 = (bf16[3,4,32,256]{3,2,1,0:T(8,128)(2,1)S(1)}, bf16[3,4,32,256]{3,2,1,0:T(8,128)(2,1)S(1)}, u32[]{:S(2)}, u32[]{:S(2)}) collective-permute-start(bf16[3,4,32,256]{3,2,1,0:T(8,128)(2,1)S(1)} %slice.20), channel_id=1, source_target_pairs={{0,1},{1,2},{2,3},{3,0},{4,5},{5,6},{6,7},{7,4},{8,9},{9,10},{10,1... | collective-permute-start | bytes 589832 | tf_op jit(solution)/shard_map/ppermute | solution.py:311
  32.7 35.2 %copy-start.14 = (bf16[256,256]{1,0:T(8,128)(2,1)S(1)}, bf16[256,256]{1,0:T(8,128)(2,1)}, u32[]{:S(2)}) copy-start(bf16[256,256]{1,0:T(8,128)(2,1)} %constant.87.x_inv_ref) | copy-start | bytes 393220
  32.7 35.2 %copy-start.15 = (bf16[256,256]{1,0:T(8,128)(2,1)S(1)}, bf16[256,256]{1,0:T(8,128)(2,1)}, u32[]{:S(2)}) copy-start(bf16[256,256]{1,0:T(8,128)(2,1)} %constant.88.x_fwd_ref) | copy-start | bytes 393220
  32.8 12.3 %collective-permute-start.3 = (bf16[3,4,32,256]{3,2,1,0:T(8,128)(2,1)S(1)}, bf16[3,4,32,256]{3,2,1,0:T(8,128)(2,1)S(1)}, u32[]{:S(2)}, u32[]{:S(2)}) collective-permute-start(bf16[3,4,32,256]{3,2,1,0:T(8,128)(2,1)S(1)} %slice.21), channel_id=1, source_target_pairs={{0,3},{1,0},{2,1},{3,2},{4,7},{5,4},{6,5},{7,6},{8,11},{9,8},{10,9... | collective-permute-start | bytes 589832 | tf_op jit(solution)/shard_map/ppermute | solution.py:311
  40.3 11.1 %collective-permute-start.5 = (bf16[3,8,32,256]{3,2,1,0:T(8,128)(2,1)}, bf16[3,8,32,256]{3,2,1,0:T(8,128)(2,1)S(1)}, u32[]{:S(2)}, u32[]{:S(2)}) collective-permute-start(bf16[3,8,32,256]{3,2,1,0:T(8,128)(2,1)} %collective-permute-done.4), channel_id=1, source_target_pairs={{0,1},{1,2},{2,3},{3,0},{4,5},{5,6},{6,7},{7,4},{8,9},{9,10},{10,1... | collective-permute-start | bytes 1179656 | tf_op jit(solution)/shard_map/ppermute | solution.py:311
  41.2 10.2 %collective-permute-start.6 = (bf16[3,8,32,256]{3,2,1,0:T(8,128)(2,1)}, bf16[3,8,32,256]{3,2,1,0:T(8,128)(2,1)S(1)}, u32[]{:S(2)}, u32[]{:S(2)}) collective-permute-start(bf16[3,8,32,256]{3,2,1,0:T(8,128)(2,1)} %collective-permute-done.4), channel_id=1, source_target_pairs={{0,3},{1,0},{2,1},{3,2},{4,7},{5,4},{6,5},{7,6},{8,11},{9,8},{10,9... | collective-permute-start | bytes 1179656 | tf_op jit(solution)/shard_map/ppermute | solution.py:311
  51.4 6.2 %collective-permute-start.7 = (bf16[3,4,32,256]{3,2,1,0:T(8,128)(2,1)S(1)}, bf16[3,4,32,256]{3,2,1,0:T(8,128)(2,1)S(1)}, u32[]{:S(2)}, u32[]{:S(2)}) collective-permute-start(bf16[3,4,32,256]{3,2,1,0:T(8,128)(2,1)S(1)} %slice.22), channel_id=1, source_target_pairs={{0,1},{1,2},{2,3},{3,0},{4,5},{5,6},{6,7},{7,4},{8,9},{9,10},{10,1... | collective-permute-start | bytes 589832 | tf_op jit(solution)/shard_map/ppermute | solution.py:311
  51.5 6.1 %collective-permute-start.8 = (bf16[3,4,32,256]{3,2,1,0:T(8,128)(2,1)S(1)}, bf16[3,4,32,256]{3,2,1,0:T(8,128)(2,1)S(1)}, u32[]{:S(2)}, u32[]{:S(2)}) collective-permute-start(bf16[3,4,32,256]{3,2,1,0:T(8,128)(2,1)S(1)} %slice.23), channel_id=1, source_target_pairs={{0,3},{1,0},{2,1},{3,2},{4,7},{5,4},{6,5},{7,6},{8,11},{9,8},{10,9... | collective-permute-start | bytes 589832 | tf_op jit(solution)/shard_map/ppermute | solution.py:311
  67.9 1.0 copy-start.6
  69.0 1.0 copy-start.8
  70.0 38.4 %copy-start.16 = (f32[64]{0:T(128)S(1)}, f32[64]{0:T(128)}, u32[]{:S(2)}) copy-start(f32[64]{0:T(128)} %param.14) | copy-start | bytes 772
  80.5 0.9 copy-start.3
  81.4 27.0 %all-to-all-start.1 = ((bf16[32,16,768]{2,1,0:T(8,128)(2,1)}), bf16[32,16,768]{2,1,0:T(8,128)(2,1)}, u32[]{:S(2)}, u32[]{:S(2)}) async-start(bf16[32,16,768]{2,1,0:T(8,128)(2,1)} %copy-done.3), calls=%async_computation.1 | async-start | bytes 1572864 | tf_op jit(solution)/shard_map/all_to_all | solution.py:339
  108.4 1.6 copy-start.1
  110.0 1.0 copy-start.5
  111.0 1.0 copy-start.12
  112.1 60.0 %copy-start.7 = (bf16[512,512]{1,0:T(8,128)(2,1)S(1)}, bf16[512,512]{1,0:T(8,128)(2,1)}, u32[]{:S(2)}) copy-start(bf16[512,512]{1,0:T(8,128)(2,1)} %constant.86.y_inv_ref) | copy-start | bytes 1572868
  112.1 60.0 %copy-start.9 = (bf16[512,512]{1,0:T(8,128)(2,1)S(1)}, bf16[512,512]{1,0:T(8,128)(2,1)}, u32[]{:S(2)}) copy-start(bf16[512,512]{1,0:T(8,128)(2,1)} %constant.89.y_fwd_ref) | copy-start | bytes 1572868
  116.5 1.3 copy-start.10
  180.9 0.9 copy-start.2
  181.8 27.2 %all-to-all-start.3 = ((bf16[32,16,768]{2,1,0:T(8,128)(2,1)}), bf16[32,16,768]{2,1,0:T(8,128)(2,1)S(1)}, u32[]{:S(2)}, u32[]{:S(2)}) async-start(bf16[32,16,768]{2,1,0:T(8,128)(2,1)} %copy-done.2), calls=%async_computation.3 | async-start | bytes 1572864 | tf_op jit(solution)/shard_map/all_to_all | solution.py:339
  209.0 1.6 copy-start.11
  210.6 1.0 copy-start.13

commit v3 on v2

--- a/solution.py
+++ b/solution.py
@@ -64,18 +64,20 @@
     return jnp.concatenate([both.astype(BF16), (waves * both).astype(BF16)], axis=1)
 
 
-def send_planes(out_ref, whole_ref, deriv_ref):
-    def one_peer(peer, carry):
-        for local in range(ROWS):
-            for at, ref in ((0, whole_ref), (HALF, deriv_ref)):
-                start = peer * ROWS + local
-                real_part = ref[pl.ds(start, ROWS, stride=PITCH), :]
-                imag_part = ref[pl.ds(start + N, ROWS, stride=PITCH), :]
-                tile = jnp.concatenate([real_part, imag_part], axis=0).astype(BF16)
-                out_ref[peer, local, :, at : at + HALF] = tile
+def send_planes(first, count, planes_ref, whole_ref, deriv_ref):
+    def some_peers(step, carry):
+        for turn in range(UNROLL):
+            peer = first + step * UNROLL + turn
+            for local in range(ROWS):
+                for at, ref in ((0, whole_ref), (HALF, deriv_ref)):
+                    start = peer * ROWS + local
+                    real_part = ref[pl.ds(start, ROWS, stride=PITCH), :]
+                    imag_part = ref[pl.ds(start + N, ROWS, stride=PITCH), :]
+                    tile = jnp.concatenate([real_part, imag_part], axis=0).astype(BF16)
+                    planes_ref[peer, local, :, at : at + HALF] = tile
         return carry
 
-    lax.fori_loop(0, PEERS, one_peer, 0)
+    lax.fori_loop(0, count // UNROLL, some_peers, 0)
 
 
 def z_inverse(local, rows, table_ref, whole_ref, deriv_ref):
@@ -92,28 +94,46 @@
     return kz_wave, kx_wave * kx_wave + ky_wave * ky_wave + kz_wave * kz_wave
 
 
-def start_kernel(state_ref, table_ref, out_ref, stats_ref, whole_ref, deriv_ref):
-    step = pl.program_id(0)
-    rows = state_ref.shape[1]
-
-    @pl.when(step == 0)
-    def _():
-        stats_ref[...] = jnp.zeros_like(stats_ref)
-
-    for pos in range(rows):
-        local = step * rows + pos
+def copy_of(source, target, sem):
+    return pltpu.make_async_copy(source, target, sem)
+
+
+def start_kernel(
+    state_hbm, table_hbm, out_hbm, stats_ref, state_ref, table_ref, planes_ref, whole_ref, deriv_ref, in_sems, out_sems
+):
+    loads = [copy_of(table_hbm, table_ref, in_sems.at[ROWS])]
+    loads += [copy_of(state_hbm.at[:, k], state_ref.at[:, k], in_sems.at[k]) for k in range(ROWS)]
+    for load in loads:
+        load.start()
+    stats_ref[...] = jnp.zeros_like(stats_ref)
+    loads[0].wait()
+
+    def one_row(local, carry):
+        copy_of(state_hbm.at[:, local], state_ref.at[:, local], in_sems.at[local]).wait()
         kz_wave, ksquare = waves_of(local)
-        real_part = state_ref[0, pos]
-        imag_part = state_ref[1, pos]
+        real_part = state_ref[0, local]
+        imag_part = state_ref[1, local]
         weight = jnp.where(iota((N, HALF), 1) == 0, 1.0, 2.0)
         energy = weight * (real_part * real_part + imag_part * imag_part)
         stats_ref[0] += jnp.sum(energy.reshape(N // 8, 8, HALF), axis=0)
         stats_ref[1] += jnp.sum((ksquare * energy).reshape(N // 8, 8, HALF), axis=0)
         z_inverse(local, z_rows(real_part, imag_part, kz_wave), table_ref, whole_ref, deriv_ref)
-
-    @pl.when(step == pl.num_programs(0) - 1)
-    def _():
-        send_planes(out_ref, whole_ref, deriv_ref)
+        return carry
+
+    lax.fori_loop(0, ROWS, one_row, 0, unroll=2)
+
+    def leaving(k):
+        part = pl.ds(k * CHUNK, CHUNK)
+        return copy_of(planes_ref.at[part], out_hbm.at[part], out_sems.at[k])
+
+    def one_chunk(k, carry):
+        send_planes(k * CHUNK, CHUNK, planes_ref, whole_ref, deriv_ref)
+        leaving(k).start()
+        return carry
+
+    lax.fori_loop(0, PEERS // CHUNK, one_chunk, 0)
+    for k in range(PEERS // CHUNK):
+        leaving(k).wait()
 
 
 def in_three(value):
@@ -141,17 +161,64 @@
 
 
 def grid_kernel(
-    planes_ref, speed_ref, stats_ref, y_inv_ref, x_inv_ref, x_fwd_ref, y_fwd_ref, out_ref, sums_ref, peak_ref
+    scalars,
+    planes_hbm,
+    speed_ref,
+    stats_ref,
+    y_inv_hbm,
+    x_inv_hbm,
+    x_fwd_hbm,
+    y_fwd_hbm,
+    out_ref,
+    y_inv_ref,
+    x_inv_ref,
+    x_fwd_ref,
+    y_fwd_ref,
+    sums_ref,
+    peak_ref,
+    sems,
+    planes_ref=None,
+    planes_sems=None,
 ):
     count = 2 * N
+
+    def came_pair(step):
+        part = pl.ds(step * PAIR, PAIR)
+        return copy_of(planes_hbm.at[:, part], planes_ref.at[:, part], planes_sems.at[step])
+
+    loads = [
+        copy_of(source, target, sems.at[k])
+        for k, (source, target) in enumerate(
+            (
+                (y_inv_hbm, y_inv_ref),
+                (x_inv_hbm, x_inv_ref),
+                (x_fwd_hbm, x_fwd_ref),
+                (y_fwd_hbm, y_fwd_ref),
+            )
+        )
+    ]
+    far = planes_ref is not None
+    loads[0].start()
+    if far:
+        came_pair(0).start()
+    for load in loads[1:]:
+        load.start()
+    if far:
+        for k in range(1, ROWS // PAIR):
+            came_pair(k).start()
+    else:
+        planes_ref = planes_hbm
     peak_ref[...] = jnp.zeros_like(peak_ref)
     row = iota((count, HALF), 0)
     ky_wave = signed(row // (2 * ROWS) * ROWS + row % ROWS)
     kx_wave = iota((N, HALF), 1).astype(F32)
 
     def one_pair(step, carry):
+        if far:
+            came_pair(step).wait()
         came = [planes_ref[:, step * PAIR + k].reshape(count, N) for k in range(PAIR)]
         scaled = [(ky_wave * part[:, :HALF].astype(F32)).astype(BF16) for part in came]
+        pl.when(step == 0)(loads[0].wait)
         y_section = dot(y_inv_ref[...], jnp.concatenate(came + scaled, axis=1))
         x_rows = []
         for k in range(PAIR):
@@ -161,6 +228,8 @@
                 if which == 0:
                     halves = [kx_wave * half for half in halves]
                 x_rows.append(jnp.concatenate(halves, axis=1).astype(BF16))
+        for load in loads[1:]:
+            pl.when(step == 0)(load.wait)
         gradients = dot(jnp.concatenate(x_rows, axis=0), x_inv_ref[...])
         fields = []
         for k in range(PAIR):
@@ -192,22 +261,24 @@
     for k, piece in enumerate(pieces):
         line = jnp.where((iota(shape, 0) == 0) & (iota(shape, 1) == LIMIT + k), piece, line)
 
-    def one_peer(peer, carry):
-        for group in range(ROWS // GROUP):
-            parts = []
-            for pos in range(GROUP):
-                start = peer * 2 * ROWS + group * GROUP + pos
-                real_part = sums_ref[pl.ds(start, ROWS, stride=PITCH), :]
-                imag_part = sums_ref[pl.ds(start + ROWS, ROWS, stride=PITCH), :]
-                parts.append(jnp.concatenate([real_part, imag_part], axis=0))
-            if group == 0:
-                parts[0] = parts[0] + line
-            for k, tile in enumerate(packed_four(parts)):
-                at = (group * 3 + k) * HALF
-                out_ref[peer, :, at : at + HALF] = tile.astype(BF16)
+    def some_peers(step, carry):
+        for turn in range(SENDS):
+            peer = step * SENDS + turn
+            for group in range(ROWS // GROUP):
+                parts = []
+                for pos in range(GROUP):
+                    start = peer * 2 * ROWS + group * GROUP + pos
+                    real_part = sums_ref[pl.ds(start, ROWS, stride=PITCH), :]
+                    imag_part = sums_ref[pl.ds(start + ROWS, ROWS, stride=PITCH), :]
+                    parts.append(jnp.concatenate([real_part, imag_part], axis=0))
+                if group == 0:
+                    parts[0] = parts[0] + line
+                for k, tile in enumerate(packed_four(parts)):
+                    at = (group * 3 + k) * HALF
+                    out_ref[peer, :, at : at + HALF] = tile.astype(BF16)
         return carry
 
-    lax.fori_loop(0, PEERS, one_peer, 0)
+    lax.fori_loop(0, PEERS // SENDS, some_peers, 0)
 
 
 def tendency(came_ref, table_ref, group):
@@ -219,17 +290,31 @@
 def middle_kernel(
     bound_ref,
     species_ref,
+    base_ref,
     came_ref,
+    state_hbm,
+    z_fwd_hbm,
+    z_inv_hbm,
+    out_ref,
+    kept_hbm,
+    kappa_ref,
     state_ref,
-    base_ref,
     z_fwd_ref,
     z_inv_ref,
-    out_ref,
     kept_ref,
-    kappa_ref,
     whole_ref,
     deriv_ref,
+    in_sems,
+    out_sems,
 ):
+    loads = [
+        copy_of(source, target, in_sems.at[k])
+        for k, (source, target) in enumerate(
+            ((z_fwd_hbm, z_fwd_ref), (state_hbm, state_ref), (z_inv_hbm, z_inv_ref))
+        )
+    ]
+    for load in loads:
+        load.start()
     shape = (PEERS, 2 * ROWS, HALF)
     found = jnp.where(iota(shape, 1) == 0, came_ref[:, :, :HALF].astype(F32), 0.0)
     lane = iota(shape, 2)
@@ -245,13 +330,18 @@
     variance = spread(jnp.sum(piece(0), axis=0, keepdims=True)) / CELLS
     mean_grad = spread(jnp.sum(piece(1), axis=0, keepdims=True)) / CELLS
     peak = spread(jnp.max(piece(2), axis=0, keepdims=True))
-    match = iota(base_ref.shape, 1) == species_ref[0]
-    base = spread(jnp.sum(jnp.where(match, base_ref[...], 0.0), axis=1, keepdims=True))
-    kappa_ref[...] = base * peak * jnp.sqrt(variance) / (mean_grad + 1e-06)
-    kappa = kappa_ref[0:1, :]
+    base = base_ref[species_ref[0]]
+    found = base * peak * jnp.sqrt(variance) / (mean_grad + 1e-06)
+    kappa_ref[0] = jnp.max(found)
+    kappa = found[0:1, :]
     bound = (bound_ref[0] * bound_ref[0]).astype(F32)
+    loads[0].wait()
+    saves = []
     for group in range(ROWS // GROUP):
-        for pos, (sum_real, sum_imag) in enumerate(tendency(came_ref, z_fwd_ref, group)):
+        parts = tendency(came_ref, z_fwd_ref, group)
+        if group == 0:
+            loads[1].wait()
+        for pos, (sum_real, sum_imag) in enumerate(parts):
             local = group * GROUP + pos
             kz_wave, ksquare = waves_of(local)
             factor = jnp.exp(-kappa * ksquare * STEP)
@@ -262,28 +352,50 @@
                 start = state_ref[part, local]
                 middle.append(factor * (start + STEP * first[part]))
                 kept_ref[part, local] = factor * start + (0.5 * STEP) * (factor * first[part])
+            if local == 0:
+                loads[2].wait()
             z_inverse(local, z_rows(*middle, kz_wave), z_inv_ref, whole_ref, deriv_ref)
-    send_planes(out_ref, whole_ref, deriv_ref)
-
-
-def final_kernel(bound_ref, came_ref, kept_ref, z_fwd_ref, out_ref):
+        rows = pl.ds(group * GROUP, GROUP)
+        saves.append(copy_of(kept_ref.at[:, rows], kept_hbm.at[:, rows], out_sems.at[group]))
+        saves[-1].start()
+    send_planes(0, PEERS, out_ref, whole_ref, deriv_ref)
+    for save in saves:
+        save.wait()
+
+
+def final_kernel(bound_ref, came_ref, kept_hbm, z_fwd_hbm, out_hbm, kept_ref, z_fwd_ref, out_ref, in_sems, out_sems):
+    loads = [copy_of(z_fwd_hbm, z_fwd_ref, in_sems.at[0]), copy_of(kept_hbm, kept_ref, in_sems.at[1])]
+    for load in loads:
+        load.start()
     bound = (bound_ref[0] * bound_ref[0]).astype(F32)
+    loads[0].wait()
+    saves = []
     for group in range(ROWS // GROUP):
-        for pos, sums in enumerate(tendency(came_ref, z_fwd_ref, group)):
+        parts = tendency(came_ref, z_fwd_ref, group)
+        if group == 0:
+            loads[1].wait()
+        for pos, sums in enumerate(parts):
             local = group * GROUP + pos
             _, ksquare = waves_of(local)
             for part in (0, 1):
                 second = jnp.where(ksquare <= bound, -sums[part], 0.0)
                 out_ref[part, local] = kept_ref[part, local] + (0.5 * STEP) * second
+            saves.append(copy_of(out_ref.at[:, local], out_hbm.at[:, local], out_sems.at[local]))
+            saves[-1].start()
+    for save in saves:
+        save.wait()
 
 
 SCALARS = pl.BlockSpec(memory_space=pltpu.SMEM)
 NEAR = pl.BlockSpec(memory_space=pltpu.VMEM)
+FAR = pl.BlockSpec(memory_space=pltpu.HBM)
 PLANES = (PEERS, ROWS, 2 * ROWS, N)
 SENT = (PEERS, 2 * ROWS, PACKED)
 STATE = (2, ROWS, N, HALF)
-PAIR = 2
-AHEAD = 2
+PAIR = 4
+CHUNK = 8
+UNROLL = 2
+SENDS = 4
 
 
 def params(mebibytes):
@@ -298,8 +410,21 @@
     return pltpu.with_memory_space_constraint(x, pltpu.VMEM)
 
 
+def far(x):
+    return pltpu.with_memory_space_constraint(x, pltpu.HBM)
+
+
+def sems(count):
+    return pltpu.SemaphoreType.DMA((count,))
+
+
 def turned():
     return pltpu.VMEM((ROWS * PITCH, HALF), F32)
+
+
+BIG = pltpu.VMEM((2 * N, 2 * N), BF16)
+SMALL = pltpu.VMEM((N, N), BF16)
+HELD = pltpu.VMEM(STATE, F32)
 
 
 def gathered(velocity):
@@ -342,60 +467,58 @@
 def start_call(state, table):
     return pl.pallas_call(
         start_kernel,
-        grid=(ROWS // AHEAD,),
-        in_specs=[pl.BlockSpec((2, AHEAD, N, HALF), lambda step: (0, step, 0, 0)), NEAR],
-        out_specs=[NEAR, NEAR],
-        out_shape=[pltpu.VMEM(PLANES, BF16), pltpu.VMEM((2, 8, HALF), F32)],
-        scratch_shapes=[turned(), turned()],
+        in_specs=[FAR, FAR],
+        out_specs=[FAR, NEAR],
+        out_shape=[pltpu.HBM(PLANES, BF16), pltpu.VMEM((2, 8, HALF), F32)],
+        scratch_shapes=[HELD, BIG, pltpu.VMEM(PLANES, BF16), turned(), turned(), sems(ROWS + 1), sems(PEERS // CHUNK)],
         compiler_params=params(24),
         name="start",
-    )(state, near(table["z_inv"]))
-
-
-def grid_call(planes, speeds, stats, table):
+    )(far(state), far(table["z_inv"]))
+
+
+def grid_call(scalars, planes, speeds, stats, table, apart):
+    scratch = [BIG, SMALL, SMALL, BIG, turned(), pltpu.VMEM((8, N), F32), sems(4)]
+    if apart:
+        scratch += [pltpu.VMEM(PLANES, BF16), sems(ROWS // PAIR)]
     return pl.pallas_call(
         grid_kernel,
-        in_specs=[NEAR] * 7,
+        in_specs=[(SCALARS,) * len(scalars), FAR if apart else NEAR, NEAR, NEAR] + [FAR] * 4,
         out_specs=NEAR,
         out_shape=pltpu.VMEM(SENT, BF16),
-        scratch_shapes=[turned(), pltpu.VMEM((8, N), F32)],
+        scratch_shapes=scratch,
         compiler_params=params(24),
         name="grid",
     )(
-        *(near(x) for x in (planes, speeds, stats)),
-        *(near(table[name]) for name in ("y_inv", "x_inv", "x_fwd", "y_fwd")),
+        scalars,
+        far(planes) if apart else near(planes),
+        near(speeds),
+        near(stats),
+        *(far(table[name]) for name in ("y_inv", "x_inv", "x_fwd", "y_fwd")),
     )
 
 
-def middle_call(bound, species, came, state, kappa_table, table):
+def middle_call(bound, species, kappa_table, came, state, table):
     return pl.pallas_call(
         middle_kernel,
-        in_specs=[SCALARS, SCALARS] + [NEAR] * 5,
-        out_specs=[NEAR] * 3,
-        out_shape=[pltpu.VMEM(PLANES, BF16), pltpu.VMEM(STATE, F32), shaped((8, HALF), F32)],
-        scratch_shapes=[turned(), turned()],
+        in_specs=[SCALARS] * 3 + [NEAR] + [FAR] * 3,
+        out_specs=[NEAR, FAR, SCALARS],
+        out_shape=[pltpu.VMEM(PLANES, BF16), pltpu.HBM(STATE, F32), shaped((1,), F32)],
+        scratch_shapes=[HELD, BIG, BIG, HELD, turned(), turned(), sems(3), sems(ROWS // GROUP)],
         compiler_params=params(24),
         name="middle",
-    )(
-        bound,
-        species,
-        near(came),
-        near(state),
-        kappa_table[None],
-        near(table["z_fwd"]),
-        near(table["z_inv"]),
-    )
+    )(bound, species, kappa_table, near(came), far(state), far(table["z_fwd"]), far(table["z_inv"]))
 
 
 def final_call(bound, came, kept, table):
     return pl.pallas_call(
         final_kernel,
-        in_specs=[SCALARS] + [NEAR] * 3,
-        out_specs=NEAR,
-        out_shape=shaped(STATE, F32),
-        compiler_params=params(16),
+        in_specs=[SCALARS, NEAR, FAR, FAR],
+        out_specs=FAR,
+        out_shape=pltpu.HBM(STATE, F32),
+        scratch_shapes=[HELD, BIG, HELD, sems(2), sems(ROWS)],
+        compiler_params=params(24),
         name="final",
-    )(bound, near(came), near(kept), near(table["z_fwd"]))
+    )(bound, near(came), far(kept), far(table["z_fwd"]))
 
 
 def body(scalar_state, velocity, species, kappa_table, dealias_bound):
@@ -403,10 +526,11 @@
     state = scalar_state[0]
     speeds = gathered(velocity)
     planes, stats = start_call(state, table)
-    came = exchanged(grid_call(exchanged(planes), speeds, stats, table))
-    planes, kept, kappa = middle_call(dealias_bound, species, came, state, kappa_table, table)
-    came = exchanged(grid_call(exchanged(planes), speeds, stats, table))
-    return (final_call(dealias_bound, came, kept, table)[None], kappa[0, :1])
+    scalars = (dealias_bound, species, kappa_table)
+    came = exchanged(grid_call(scalars, exchanged(planes), speeds, stats, table, True))
+    planes, kept, kappa = middle_call(dealias_bound, species, kappa_table, came, state, table)
+    came = exchanged(grid_call((), exchanged(planes), speeds, stats, table, False))
+    return (final_call(dealias_bound, came, kept, table)[None], kappa)
 
 
 def solution(mesh):

time: 216 us -> 202 us (0.935)
  blocking collectives: 54.3 us -> 108 us
  waiting for transfers between devices: 69.8 us -> 29.6 us
  local copies, waits for them, and re-layouts: 21.1 us -> 4.59 us
  starting transfers between devices: 36.4 us -> 24.8 us
    all_to_all x1 -> x3, blocking collectives: 54.3 us -> 108 us  [exchanged(): return lax.all_to_all(x, 'fft', 0, 0, tiled=True)]
    all_to_all x3 -> x1, waiting for transfers between devices: 51.1 us -> 10.3 us  [exchanged(): return lax.all_to_all(x, 'fft', 0, 0, tiled=True)]
    unnamed x34 -> x2, local copies, waits for them, and re-layouts: 14.1 us -> 0.01 us
    all_to_all x3 -> x1, starting transfers between devices: 22.7 us -> 11.1 us  [exchanged(): return lax.all_to_all(x, 'fft', 0, 0, tiled=True)]
  transfers between devices with their start and end apart: 12 -> 10, of which waited for: 7 -> 5; matrix products, arithmetic and copies ran while one was open for 3% -> 2% of each run, Pallas kernels for 0% -> 0%
where the time goes in v3:
time: 202 us; the launch traced here: 201 us
  blocking collectives  108 us (53%)
  Pallas kernels  31.5 us (16%)
  waiting for transfers between devices  29.6 us (15%)
  starting transfers between devices  24.8 us (12%)
  local copies, waits for them, and re-layouts  4.59 us (2%)
  between operations  2.32 us (1%)
    all_to_all x3, blocking collectives, exchanged(): return lax.all_to_all(x, 'fft', 0, 0, tiled=True)  108 us
    ppermute x9, waiting for transfers between devices, moved(): return lax.ppermute(x, 'scal', [(s, change(s)) for s in range(groups)])  19.3 us
    pallas_call x2, Pallas kernels, grid_call(): pl.pallas_call(grid_kernel, in_specs=[(SCALARS,) * len(scalars), FAR if a...  16 us
    ppermute x9, starting transfers between devices, moved(): return lax.ppermute(x, 'scal', [(s, change(s)) for s in range(groups)])  13.7 us
    all_to_all x1, starting transfers between devices, exchanged(): return lax.all_to_all(x, 'fft', 0, 0, tiled=True)  11.1 us
    all_to_all x1, waiting for transfers between devices, exchanged(): return lax.all_to_all(x, 'fft', 0, 0, tiled=True)  10.3 us
    pallas_call x1, Pallas kernels, start_call(): pl.pallas_call(start_kernel, in_specs=[FAR, FAR], out_specs=[FAR, NEAR],...  6.34 us
    pallas_call x1, Pallas kernels, middle_call(): pl.pallas_call(middle_kernel, in_specs=[SCALARS] * 3 + [NEAR] + [FAR] * 3...  5.66 us
  transfers between devices with their start and end apart: 10, of which 5 were waited for; matrix products, arithmetic and copies ran while one was open for 2% of the time, Pallas kernels for 0%

profile of v3, /device:TPU:1, one launch (start us, length us, event | category | flops | bytes accessed | tf_op | source)
XLA Modules:
  0.0 200.7 jit_solution(16945169568492010352)
XLA Ops:
  0.6 6.3 %start.1 = (bf16[32,8,16,256]{3,2,1,0:T(8,128)(2,1)}, f32[2,8,128]{2,1,0:T(8,128)S(1)}) custom-call(f32[2,8,256,128]{3,2,1,0:T(8,128)} %bitcast.2, bf16[512,512]{1,0:T(8,128)(2,1)} %constant.85.table_hbm.z_inv_hbm), custom_call_target="tpu_custom_call" | custom-call | tf_op jit(solution)/shard_map/start/pallas_call | solution.py:468
  7.0 11.1 %all-to-all-start = ((bf16[32,8,16,256]{3,2,1,0:T(8,128)(2,1)}), bf16[32,8,16,256]{3,2,1,0:T(8,128)(2,1)}, u32[]{:S(2)}, u32[]{:S(2)}) async-start(bf16[32,8,16,256]{3,2,1,0:T(8,128)(2,1)} %get-tuple-element.7), calls=%async_computation | async-start | bytes 4194304 | tf_op jit(solution)/shard_map/all_to_all | solution.py:464
  18.1 1.4 collective-permute-start
  19.5 1.5 collective-permute-start.1
  21.0 2.5 %collective-permute-start.4 = (bf16[3,8,32,256]{3,2,1,0:T(8,128)(2,1)}, bf16[3,8,32,256]{3,2,1,0:T(8,128)(2,1)}, u32[]{:S(2)}, u32[]{:S(2)}) collective-permute-start(bf16[3,8,32,256]{3,2,1,0:T(8,128)(2,1)} %param.12), channel_id=1, source_target_pairs={{0,4},{1,5},{2,6},{3,7},{4,0},{5,1},{6,2},{7,3},{8,12},{9,13},{10,... | collective-permute-start | bytes 1179656 | tf_op jit(solution)/shard_map/ppermute | solution.py:436
  24.8 0.3 broadcast_in_dim.6
  25.1 1.0 constant_dynamic-update-slice_fusion.9
  26.1 4.0 %collective-permute-done = bf16[3,8,32,256]{3,2,1,0:T(8,128)(2,1)S(1)} collective-permute-done((bf16[3,8,32,256]{3,2,1,0:T(8,128)(2,1)}, bf16[3,8,32,256]{3,2,1,0:T(8,128)(2,1)S(1)}, u32[]{:S(2)}, u32[]{:S(2)}) %collective-permute-start) | collective-permute-done | bytes 393248 | tf_op jit(solution)/shard_map/ppermute | solution.py:436
  30.2 0.1 collective-permute-start.2
  30.3 0.0 collective-permute-done.1
  30.3 0.9 slice.17
  31.3 0.0 copy-start
  31.3 2.7 %collective-permute-start.3 = (bf16[3,4,32,256]{3,2,1,0:T(8,128)(2,1)S(1)}, bf16[3,4,32,256]{3,2,1,0:T(8,128)(2,1)S(1)}, u32[]{:S(2)}, u32[]{:S(2)}) collective-permute-start(bf16[3,4,32,256]{3,2,1,0:T(8,128)(2,1)S(1)} %slice.17), channel_id=1, source_target_pairs={{0,3},{1,0},{2,1},{3,2},{4,7},{5,4},{6,5},{7,6},{8,11},{9,8},{10,9... | collective-permute-start | bytes 589832 | tf_op jit(solution)/shard_map/ppermute | solution.py:436
  34.0 5.7 %collective-permute-done.4 = bf16[3,8,32,256]{3,2,1,0:T(8,128)(2,1)} collective-permute-done((bf16[3,8,32,256]{3,2,1,0:T(8,128)(2,1)}, bf16[3,8,32,256]{3,2,1,0:T(8,128)(2,1)}, u32[]{:S(2)}, u32[]{:S(2)}) %collective-permute-start.4) | collective-permute-done | bytes 393248 | tf_op jit(solution)/shard_map/ppermute | solution.py:436
  39.7 0.9 collective-permute-start.5
  40.7 1.7 collective-permute-start.6
  42.4 1.0 constant_dynamic-update-slice_fusion.7
  43.5 0.0 collective-permute-done.2
  43.5 0.0 collective-permute-done.3
  43.6 1.0 constant_dynamic-update-slice_fusion.4
  44.6 6.2 %collective-permute-done.5 = bf16[3,8,32,256]{3,2,1,0:T(8,128)(2,1)S(1)} collective-permute-done((bf16[3,8,32,256]{3,2,1,0:T(8,128)(2,1)}, bf16[3,8,32,256]{3,2,1,0:T(8,128)(2,1)S(1)}, u32[]{:S(2)}, u32[]{:S(2)}) %collective-permute-start.5) | collective-permute-done | bytes 393248 | tf_op jit(solution)/shard_map/ppermute | solution.py:436
  50.8 0.1 collective-permute-start.7
  50.9 0.0 collective-permute-done.6
  50.9 2.7 %collective-permute-start.8 = (bf16[3,4,32,256]{3,2,1,0:T(8,128)(2,1)S(1)}, bf16[3,4,32,256]{3,2,1,0:T(8,128)(2,1)S(1)}, u32[]{:S(2)}, u32[]{:S(2)}) collective-permute-start(bf16[3,4,32,256]{3,2,1,0:T(8,128)(2,1)S(1)} %slice.19), channel_id=1, source_target_pairs={{0,3},{1,0},{2,1},{3,2},{4,7},{5,4},{6,5},{7,6},{8,11},{9,8},{10,9... | collective-permute-start | bytes 589832 | tf_op jit(solution)/shard_map/ppermute | solution.py:436
  53.8 3.3 %collective-permute-done.7 = bf16[3,4,32,256]{3,2,1,0:T(8,128)(2,1)S(1)} collective-permute-done((bf16[3,4,32,256]{3,2,1,0:T(8,128)(2,1)S(1)}, bf16[3,4,32,256]{3,2,1,0:T(8,128)(2,1)S(1)}, u32[]{:S(2)}, u32[]{:S(2)}) %collective-permute-start.7) | collective-permute-done | bytes 196640 | tf_op jit(solution)/shard_map/ppermute | solution.py:436
  57.1 0.0 collective-permute-done.8
  57.1 10.3 %all-to-all-done.planes_hbm = bf16[32,8,16,256]{3,2,1,0:T(8,128)(2,1)} async-done(((bf16[32,8,16,256]{3,2,1,0:T(8,128)(2,1)}), bf16[32,8,16,256]{3,2,1,0:T(8,128)(2,1)}, u32[]{:S(2)}, u32[]{:S(2)}) %all-to-all-start) | async-done | bytes 2097184 | tf_op jit(solution)/shard_map/all_to_all | solution.py:464
  67.4 0.0 copy-done
  67.4 8.5 %grid.2 = bf16[32,16,768]{2,1,0:T(8,128)(2,1)S(1)} custom-call(s32[1]{0:T(128)S(6)} %copy.24.scalars_0_.bound_ref, s32[1]{0:T(128)S(6)} %copy.23.scalars_1_.species_ref, f32[64]{0:T(128)S(1)} %copy-done, bf16[32,8,16,256]{3,2,1,0:T(8,128)(2,1)} %all-to-all-done.planes_hbm, bf16[3,8,256,256]{3,2,1,0:T(8,128)(2,1)S(1)} %constant_dynamic-update-slice_fusion.speed_ref, ...), custom_call_target="tpu_custom_call" | custom-call | tf_op jit(solution)/shard_map/grid/pallas_call | solution.py:483
  75.9 26.7 %all_to_all.20.came_ref = bf16[32,16,768]{2,1,0:T(8,128)(2,1)S(1)} all-to-all(bf16[32,16,768]{2,1,0:T(8,128)(2,1)S(1)} %grid.2), channel_id=1, replica_groups=mesh['fft'=32,'scal'=8] {'fft'}, dimensions={0} | all-to-all | bytes 1572864 | tf_op jit(solution)/shard_map/all_to_all | solution.py:464
  102.6 5.7 %middle.1 = (bf16[32,8,16,256]{3,2,1,0:T(8,128)(2,1)S(1)}, f32[2,8,256,128]{3,2,1,0:T(8,128)}, f32[1]{0:T(128)}) custom-call(s32[1]{0:T(128)S(6)} %copy.24.scalars_0_.bound_ref, s32[1]{0:T(128)S(6)} %copy.23.scalars_1_.species_ref, f32[64]{0:T(128)S(1)} %copy-done, bf16[32,16,768]{2,1,0:T(8,128)(2,1)S(1)} %all_to_all.20.came_ref, ...), custom_call_target="tpu_custom_call" | custom-call | tf_op jit(solution)/shard_map/middle/pallas_call | solution.py:501
  108.3 54.3 %all_to_all.21.planes_hbm = bf16[32,8,16,256]{3,2,1,0:T(8,128)(2,1)S(1)} all-to-all(bf16[32,8,16,256]{3,2,1,0:T(8,128)(2,1)S(1)} %get-tuple-element.9), channel_id=1, replica_groups=mesh['fft'=32,'scal'=8] {'fft'}, dimensions={0} | all-to-all | bytes 4194304 | tf_op jit(solution)/shard_map/all_to_all | solution.py:464
  162.6 7.4 %grid.3 = bf16[32,16,768]{2,1,0:T(8,128)(2,1)S(1)} custom-call(bf16[32,8,16,256]{3,2,1,0:T(8,128)(2,1)S(1)} %all_to_all.21.planes_hbm, bf16[3,8,256,256]{3,2,1,0:T(8,128)(2,1)S(1)} %constant_dynamic-update-slice_fusion.speed_ref, f32[2,8,128]{2,1,0:T(8,128)S(1)} %get-tuple-element.8.stats_ref, bf16[512,512]{1,0:T(8,128)(2,1)} %constant.86.y_inv_hbm, ...), custom_call_target="tpu_custom_call" | custom-call | tf_op jit(solution)/shard_map/grid/pallas_call | solution.py:483
  170.1 27.0 %all_to_all.22.came_ref = bf16[32,16,768]{2,1,0:T(8,128)(2,1)S(1)} all-to-all(bf16[32,16,768]{2,1,0:T(8,128)(2,1)S(1)} %grid.3), channel_id=1, replica_groups=mesh['fft'=32,'scal'=8] {'fft'}, dimensions={0} | all-to-all | bytes 1572864 | tf_op jit(solution)/shard_map/all_to_all | solution.py:464
  197.0 3.5 %final.1 = f32[2,8,256,128]{3,2,1,0:T(8,128)} custom-call(s32[1]{0:T(128)S(6)} %copy.24.scalars_0_.bound_ref, bf16[32,16,768]{2,1,0:T(8,128)(2,1)S(1)} %all_to_all.22.came_ref, f32[2,8,256,128]{3,2,1,0:T(8,128)} %get-tuple-element.10.kept_hbm, bf16[512,512]{1,0:T(8,128)(2,1)} %constant.90.z_fwd_hbm), custom_call_target="tpu_custom_call" | custom-call | tf_op jit(solution)/shard_map/final/pallas_call | solution.py:513
  (10 shorter events, 0.2 us)
Async XLA Ops:
  7.0 60.4 %all-to-all-start = ((bf16[32,8,16,256]{3,2,1,0:T(8,128)(2,1)}), bf16[32,8,16,256]{3,2,1,0:T(8,128)(2,1)}, u32[]{:S(2)}, u32[]{:S(2)}) async-start(bf16[32,8,16,256]{3,2,1,0:T(8,128)(2,1)} %get-tuple-element.7), calls=%async_computation | async-start | bytes 4194304 | tf_op jit(solution)/shard_map/all_to_all | solution.py:464
  18.1 12.1 %collective-permute-start = (bf16[3,8,32,256]{3,2,1,0:T(8,128)(2,1)}, bf16[3,8,32,256]{3,2,1,0:T(8,128)(2,1)S(1)}, u32[]{:S(2)}, u32[]{:S(2)}) collective-permute-start(bf16[3,8,32,256]{3,2,1,0:T(8,128)(2,1)} %param.12), channel_id=1, source_target_pairs={{0,1},{1,2},{2,3},{3,0},{4,5},{5,6},{6,7},{7,4},{8,9},{9,10},{10,1... | collective-permute-start | bytes 1179656 | tf_op jit(solution)/shard_map/ppermute | solution.py:436
  19.5 10.8 %collective-permute-start.1 = (bf16[3,8,32,256]{3,2,1,0:T(8,128)(2,1)}, bf16[3,8,32,256]{3,2,1,0:T(8,128)(2,1)}, u32[]{:S(2)}, u32[]{:S(2)}) collective-permute-start(bf16[3,8,32,256]{3,2,1,0:T(8,128)(2,1)} %param.12), channel_id=1, source_target_pairs={{0,3},{1,0},{2,1},{3,2},{4,7},{5,4},{6,5},{7,6},{8,11},{9,8},{10,9... | collective-permute-start | bytes 1179656 | tf_op jit(solution)/shard_map/ppermute | solution.py:436
  21.0 18.7 %collective-permute-start.4 = (bf16[3,8,32,256]{3,2,1,0:T(8,128)(2,1)}, bf16[3,8,32,256]{3,2,1,0:T(8,128)(2,1)}, u32[]{:S(2)}, u32[]{:S(2)}) collective-permute-start(bf16[3,8,32,256]{3,2,1,0:T(8,128)(2,1)} %param.12), channel_id=1, source_target_pairs={{0,4},{1,5},{2,6},{3,7},{4,0},{5,1},{6,2},{7,3},{8,12},{9,13},{10,... | collective-permute-start | bytes 1179656 | tf_op jit(solution)/shard_map/ppermute | solution.py:436
  30.2 13.3 %collective-permute-start.2 = (bf16[3,4,32,256]{3,2,1,0:T(8,128)(2,1)S(1)}, bf16[3,4,32,256]{3,2,1,0:T(8,128)(2,1)S(1)}, u32[]{:S(2)}, u32[]{:S(2)}) collective-permute-start(bf16[3,4,32,256]{3,2,1,0:T(8,128)(2,1)S(1)} %slice.16), channel_id=1, source_target_pairs={{0,1},{1,2},{2,3},{3,0},{4,5},{5,6},{6,7},{7,4},{8,9},{9,10},{10,1... | collective-permute-start | bytes 589832 | tf_op jit(solution)/shard_map/ppermute | solution.py:436
  31.3 36.1 %copy-start = (f32[64]{0:T(128)S(1)}, f32[64]{0:T(128)}, u32[]{:S(2)}) copy-start(f32[64]{0:T(128)} %base_ref.1) | copy-start | bytes 772
  31.3 12.3 %collective-permute-start.3 = (bf16[3,4,32,256]{3,2,1,0:T(8,128)(2,1)S(1)}, bf16[3,4,32,256]{3,2,1,0:T(8,128)(2,1)S(1)}, u32[]{:S(2)}, u32[]{:S(2)}) collective-permute-start(bf16[3,4,32,256]{3,2,1,0:T(8,128)(2,1)S(1)} %slice.17), channel_id=1, source_target_pairs={{0,3},{1,0},{2,1},{3,2},{4,7},{5,4},{6,5},{7,6},{8,11},{9,8},{10,9... | collective-permute-start | bytes 589832 | tf_op jit(solution)/shard_map/ppermute | solution.py:436
  39.7 11.1 %collective-permute-start.5 = (bf16[3,8,32,256]{3,2,1,0:T(8,128)(2,1)}, bf16[3,8,32,256]{3,2,1,0:T(8,128)(2,1)S(1)}, u32[]{:S(2)}, u32[]{:S(2)}) collective-permute-start(bf16[3,8,32,256]{3,2,1,0:T(8,128)(2,1)} %collective-permute-done.4), channel_id=1, source_target_pairs={{0,1},{1,2},{2,3},{3,0},{4,5},{5,6},{6,7},{7,4},{8,9},{9,10},{10,1... | collective-permute-start | bytes 1179656 | tf_op jit(solution)/shard_map/ppermute | solution.py:436
  40.7 10.2 %collective-permute-start.6 = (bf16[3,8,32,256]{3,2,1,0:T(8,128)(2,1)}, bf16[3,8,32,256]{3,2,1,0:T(8,128)(2,1)S(1)}, u32[]{:S(2)}, u32[]{:S(2)}) collective-permute-start(bf16[3,8,32,256]{3,2,1,0:T(8,128)(2,1)} %collective-permute-done.4), channel_id=1, source_target_pairs={{0,3},{1,0},{2,1},{3,2},{4,7},{5,4},{6,5},{7,6},{8,11},{9,8},{10,9... | collective-permute-start | bytes 1179656 | tf_op jit(solution)/shard_map/ppermute | solution.py:436
  50.8 6.2 %collective-permute-start.7 = (bf16[3,4,32,256]{3,2,1,0:T(8,128)(2,1)S(1)}, bf16[3,4,32,256]{3,2,1,0:T(8,128)(2,1)S(1)}, u32[]{:S(2)}, u32[]{:S(2)}) collective-permute-start(bf16[3,4,32,256]{3,2,1,0:T(8,128)(2,1)S(1)} %slice.18), channel_id=1, source_target_pairs={{0,1},{1,2},{2,3},{3,0},{4,5},{5,6},{6,7},{7,4},{8,9},{9,10},{10,1... | collective-permute-start | bytes 589832 | tf_op jit(solution)/shard_map/ppermute | solution.py:436
  50.9 6.1 %collective-permute-start.8 = (bf16[3,4,32,256]{3,2,1,0:T(8,128)(2,1)S(1)}, bf16[3,4,32,256]{3,2,1,0:T(8,128)(2,1)S(1)}, u32[]{:S(2)}, u32[]{:S(2)}) collective-permute-start(bf16[3,4,32,256]{3,2,1,0:T(8,128)(2,1)S(1)} %slice.19), channel_id=1, source_target_pairs={{0,3},{1,0},{2,1},{3,2},{4,7},{5,4},{6,5},{7,6},{8,11},{9,8},{10,9... | collective-permute-start | bytes 589832 | tf_op jit(solution)/shard_map/ppermute | solution.py:436

commit v4 on v3

--- a/solution.py
+++ b/solution.py
@@ -120,7 +120,7 @@
         z_inverse(local, z_rows(real_part, imag_part, kz_wave), table_ref, whole_ref, deriv_ref)
         return carry
 
-    lax.fori_loop(0, ROWS, one_row, 0, unroll=2)
+    lax.fori_loop(0, ROWS, one_row, 0)
 
     def leaving(k):
         part = pl.ds(k * CHUNK, CHUNK)
@@ -160,65 +160,41 @@
     ]
 
 
-def grid_kernel(
-    scalars,
-    planes_hbm,
-    speed_ref,
-    stats_ref,
-    y_inv_hbm,
-    x_inv_hbm,
-    x_fwd_hbm,
-    y_fwd_hbm,
-    out_ref,
-    y_inv_ref,
-    x_inv_ref,
-    x_fwd_ref,
-    y_fwd_ref,
-    sums_ref,
-    peak_ref,
-    sems,
-    planes_ref=None,
-    planes_sems=None,
-):
+def grid_kernel(scalars, planes_hbm, speed_ref, stats_ref, held, out_ref, passed, sums_ref, peak_ref, *apart):
     count = 2 * N
-
-    def came_pair(step):
-        part = pl.ds(step * PAIR, PAIR)
-        return copy_of(planes_hbm.at[:, part], planes_ref.at[:, part], planes_sems.at[step])
-
-    loads = [
-        copy_of(source, target, sems.at[k])
-        for k, (source, target) in enumerate(
-            (
-                (y_inv_hbm, y_inv_ref),
-                (x_inv_hbm, x_inv_ref),
-                (x_fwd_hbm, x_fwd_ref),
-                (y_fwd_hbm, y_fwd_ref),
-            )
-        )
-    ]
-    far = planes_ref is not None
-    loads[0].start()
-    if far:
-        came_pair(0).start()
-    for load in loads[1:]:
-        load.start()
-    if far:
-        for k in range(1, ROWS // PAIR):
-            came_pair(k).start()
+    if apart:
+        planes_ref, planes_sems, sems = apart
+
+        def came_plane(k):
+            return copy_of(planes_hbm.at[:, k], planes_ref.at[:, k], planes_sems.at[k])
+
+        loads = [copy_of(source, target, sems.at[k]) for k, (source, target) in enumerate(zip(held, passed))]
+        loads[0].start()
+        for k in range(PAIR):
+            came_plane(k).start()
+        for load in loads[1:4]:
+            load.start()
+        for k in range(PAIR, ROWS):
+            came_plane(k).start()
+        for load in loads[4:]:
+            load.start()
+        held = passed
     else:
         planes_ref = planes_hbm
+    y_inv_ref, x_inv_ref, x_fwd_ref, y_fwd_ref = held[:4]
     peak_ref[...] = jnp.zeros_like(peak_ref)
     row = iota((count, HALF), 0)
     ky_wave = signed(row // (2 * ROWS) * ROWS + row % ROWS)
     kx_wave = iota((N, HALF), 1).astype(F32)
 
     def one_pair(step, carry):
-        if far:
-            came_pair(step).wait()
+        if apart:
+            for k in range(PAIR):
+                came_plane(step * PAIR + k).wait()
         came = [planes_ref[:, step * PAIR + k].reshape(count, N) for k in range(PAIR)]
         scaled = [(ky_wave * part[:, :HALF].astype(F32)).astype(BF16) for part in came]
-        pl.when(step == 0)(loads[0].wait)
+        if apart:
+            pl.when(step == 0)(loads[0].wait)
         y_section = dot(y_inv_ref[...], jnp.concatenate(came + scaled, axis=1))
         x_rows = []
         for k in range(PAIR):
@@ -228,8 +204,9 @@
                 if which == 0:
                     halves = [kx_wave * half for half in halves]
                 x_rows.append(jnp.concatenate(halves, axis=1).astype(BF16))
-        for load in loads[1:]:
-            pl.when(step == 0)(load.wait)
+        if apart:
+            for load in loads[1:4]:
+                pl.when(step == 0)(load.wait)
         gradients = dot(jnp.concatenate(x_rows, axis=0), x_inv_ref[...])
         fields = []
         for k in range(PAIR):
@@ -279,6 +256,9 @@
         return carry
 
     lax.fori_loop(0, PEERS // SENDS, some_peers, 0)
+    if apart:
+        for load in loads[4:]:
+            load.wait()
 
 
 def tendency(came_ref, table_ref, group):
@@ -292,29 +272,15 @@
     species_ref,
     base_ref,
     came_ref,
-    state_hbm,
-    z_fwd_hbm,
-    z_inv_hbm,
-    out_ref,
-    kept_hbm,
-    kappa_ref,
     state_ref,
     z_fwd_ref,
     z_inv_ref,
+    out_ref,
     kept_ref,
+    kappa_ref,
     whole_ref,
     deriv_ref,
-    in_sems,
-    out_sems,
 ):
-    loads = [
-        copy_of(source, target, in_sems.at[k])
-        for k, (source, target) in enumerate(
-            ((z_fwd_hbm, z_fwd_ref), (state_hbm, state_ref), (z_inv_hbm, z_inv_ref))
-        )
-    ]
-    for load in loads:
-        load.start()
     shape = (PEERS, 2 * ROWS, HALF)
     found = jnp.where(iota(shape, 1) == 0, came_ref[:, :, :HALF].astype(F32), 0.0)
     lane = iota(shape, 2)
@@ -335,12 +301,8 @@
     kappa_ref[0] = jnp.max(found)
     kappa = found[0:1, :]
     bound = (bound_ref[0] * bound_ref[0]).astype(F32)
-    loads[0].wait()
-    saves = []
     for group in range(ROWS // GROUP):
         parts = tendency(came_ref, z_fwd_ref, group)
-        if group == 0:
-            loads[1].wait()
         for pos, (sum_real, sum_imag) in enumerate(parts):
             local = group * GROUP + pos
             kz_wave, ksquare = waves_of(local)
@@ -352,28 +314,15 @@
                 start = state_ref[part, local]
                 middle.append(factor * (start + STEP * first[part]))
                 kept_ref[part, local] = factor * start + (0.5 * STEP) * (factor * first[part])
-            if local == 0:
-                loads[2].wait()
             z_inverse(local, z_rows(*middle, kz_wave), z_inv_ref, whole_ref, deriv_ref)
-        rows = pl.ds(group * GROUP, GROUP)
-        saves.append(copy_of(kept_ref.at[:, rows], kept_hbm.at[:, rows], out_sems.at[group]))
-        saves[-1].start()
     send_planes(0, PEERS, out_ref, whole_ref, deriv_ref)
-    for save in saves:
-        save.wait()
-
-
-def final_kernel(bound_ref, came_ref, kept_hbm, z_fwd_hbm, out_hbm, kept_ref, z_fwd_ref, out_ref, in_sems, out_sems):
-    loads = [copy_of(z_fwd_hbm, z_fwd_ref, in_sems.at[0]), copy_of(kept_hbm, kept_ref, in_sems.at[1])]
-    for load in loads:
-        load.start()
+
+
+def final_kernel(bound_ref, came_ref, kept_ref, z_fwd_ref, out_hbm, out_ref, out_sems):
     bound = (bound_ref[0] * bound_ref[0]).astype(F32)
-    loads[0].wait()
     saves = []
     for group in range(ROWS // GROUP):
         parts = tendency(came_ref, z_fwd_ref, group)
-        if group == 0:
-            loads[1].wait()
         for pos, sums in enumerate(parts):
             local = group * GROUP + pos
             _, ksquare = waves_of(local)
@@ -476,49 +425,45 @@
     )(far(state), far(table["z_inv"]))
 
 
-def grid_call(scalars, planes, speeds, stats, table, apart):
-    scratch = [BIG, SMALL, SMALL, BIG, turned(), pltpu.VMEM((8, N), F32), sems(4)]
+def grid_call(scalars, planes, speeds, stats, held, apart):
+    scratch = [turned(), pltpu.VMEM((8, N), F32)]
+    passed = held if apart else ()
     if apart:
-        scratch += [pltpu.VMEM(PLANES, BF16), sems(ROWS // PAIR)]
+        scratch += [pltpu.VMEM(PLANES, BF16), sems(ROWS), sems(len(held))]
+    spec, place = (FAR, far) if apart else (NEAR, near)
     return pl.pallas_call(
         grid_kernel,
-        in_specs=[(SCALARS,) * len(scalars), FAR if apart else NEAR, NEAR, NEAR] + [FAR] * 4,
-        out_specs=NEAR,
-        out_shape=pltpu.VMEM(SENT, BF16),
+        in_specs=[(SCALARS,) * len(scalars), spec, NEAR, NEAR, (spec,) * len(held)],
+        out_specs=[NEAR, (NEAR,) * len(passed)],
+        out_shape=[pltpu.VMEM(SENT, BF16), tuple(pltpu.VMEM(x.shape, x.dtype) for x in passed)],
         scratch_shapes=scratch,
         compiler_params=params(24),
         name="grid",
-    )(
-        scalars,
-        far(planes) if apart else near(planes),
-        near(speeds),
-        near(stats),
-        *(far(table[name]) for name in ("y_inv", "x_inv", "x_fwd", "y_fwd")),
-    )
-
-
-def middle_call(bound, species, kappa_table, came, state, table):
+    )(scalars, place(planes), near(speeds), near(stats), tuple(place(x) for x in held))
+
+
+def middle_call(scalars, came, state, z_fwd, z_inv):
     return pl.pallas_call(
         middle_kernel,
-        in_specs=[SCALARS] * 3 + [NEAR] + [FAR] * 3,
-        out_specs=[NEAR, FAR, SCALARS],
-        out_shape=[pltpu.VMEM(PLANES, BF16), pltpu.HBM(STATE, F32), shaped((1,), F32)],
-        scratch_shapes=[HELD, BIG, BIG, HELD, turned(), turned(), sems(3), sems(ROWS // GROUP)],
+        in_specs=[SCALARS] * 3 + [NEAR] * 4,
+        out_specs=[NEAR, NEAR, SCALARS],
+        out_shape=[pltpu.VMEM(PLANES, BF16), pltpu.VMEM(STATE, F32), shaped((1,), F32)],
+        scratch_shapes=[turned(), turned()],
         compiler_params=params(24),
         name="middle",
-    )(bound, species, kappa_table, near(came), far(state), far(table["z_fwd"]), far(table["z_inv"]))
-
-
-def final_call(bound, came, kept, table):
+    )(*scalars, *(near(x) for x in (came, state, z_fwd, z_inv)))
+
+
+def final_call(bound, came, kept, z_fwd):
     return pl.pallas_call(
         final_kernel,
-        in_specs=[SCALARS, NEAR, FAR, FAR],
+        in_specs=[SCALARS, NEAR, NEAR, NEAR],
         out_specs=FAR,
         out_shape=pltpu.HBM(STATE, F32),
-        scratch_shapes=[HELD, BIG, HELD, sems(2), sems(ROWS)],
+        scratch_shapes=[HELD, sems(ROWS)],
         compiler_params=params(24),
         name="final",
-    )(bound, near(came), far(kept), far(table["z_fwd"]))
+    )(bound, near(came), near(kept), near(z_fwd))
 
 
 def body(scalar_state, velocity, species, kappa_table, dealias_bound):
@@ -527,10 +472,12 @@
     speeds = gathered(velocity)
     planes, stats = start_call(state, table)
     scalars = (dealias_bound, species, kappa_table)
-    came = exchanged(grid_call(scalars, exchanged(planes), speeds, stats, table, True))
-    planes, kept, kappa = middle_call(dealias_bound, species, kappa_table, came, state, table)
-    came = exchanged(grid_call((), exchanged(planes), speeds, stats, table, False))
-    return (final_call(dealias_bound, came, kept, table)[None], kappa)
+    held = tuple(table[name] for name in ("y_inv", "x_inv", "x_fwd", "y_fwd", "z_fwd", "z_inv")) + (state,)
+    sent, held = grid_call(scalars, exchanged(planes), speeds, stats, held, True)
+    *grid_tables, z_fwd, z_inv, state = held
+    planes, kept, kappa = middle_call(scalars, exchanged(sent), state, z_fwd, z_inv)
+    sent, _ = grid_call((), exchanged(planes), speeds, stats, tuple(grid_tables), False)
+    return (final_call(dealias_bound, exchanged(sent), kept, z_fwd)[None], kappa)
 
 
 def solution(mesh):

time: 202 us -> 197 us (0.975)
  Pallas kernels: 31.5 us -> 26.3 us
    pallas_call x4, Pallas kernels: 25.1 us -> 20.8 us  [the longest x2 14.6 us: grid_call(): pl.pallas_call(grid_kernel, in_specs=[(SCALARS,) * len(scalars), spec, NE...]
    all_to_all x1, waiting for transfers between devices: 10.3 us -> 7.63 us  [exchanged(): return lax.all_to_all(x, 'fft', 0, 0, tiled=True)]
    ppermute x9, waiting for transfers between devices: 19.3 us -> 21.5 us  [moved(): return lax.ppermute(x, 'scal', [(s, change(s)) for s in range(groups)])]
where the time goes in v4:
time: 197 us; the launch traced here: 196 us
  blocking collectives  108 us (55%)
  waiting for transfers between devices  29.1 us (15%)
  Pallas kernels  26.3 us (13%)
  starting transfers between devices  25.2 us (13%)
  local copies, waits for them, and re-layouts  4.59 us (2%)
  between operations  2.3 us (1%)
    all_to_all x3, blocking collectives, exchanged(): return lax.all_to_all(x, 'fft', 0, 0, tiled=True)  108 us
    ppermute x9, waiting for transfers between devices, moved(): return lax.ppermute(x, 'scal', [(s, change(s)) for s in range(groups)])  21.5 us
    pallas_call x2, Pallas kernels, grid_call(): pl.pallas_call(grid_kernel, in_specs=[(SCALARS,) * len(scalars), spec, NE...  14.6 us
    ppermute x9, starting transfers between devices, moved(): return lax.ppermute(x, 'scal', [(s, change(s)) for s in range(groups)])  14.1 us
    all_to_all x1, starting transfers between devices, exchanged(): return lax.all_to_all(x, 'fft', 0, 0, tiled=True)  11.1 us
    all_to_all x1, waiting for transfers between devices, exchanged(): return lax.all_to_all(x, 'fft', 0, 0, tiled=True)  7.63 us
    pallas_call x1, Pallas kernels, start_call(): pl.pallas_call(start_kernel, in_specs=[FAR, FAR], out_specs=[FAR, NEAR],...  5.58 us
    pallas_call x1, Pallas kernels, middle_call(): pl.pallas_call(middle_kernel, in_specs=[SCALARS] * 3 + [NEAR] * 4, out_sp...  4.25 us
  transfers between devices with their start and end apart: 10, of which 5 were waited for; matrix products, arithmetic and copies ran while one was open for 2% of the time, Pallas kernels for 0%

profile of v4, /device:TPU:1, one launch (start us, length us, event | category | flops | bytes accessed | tf_op | source)
XLA Modules:
  0.0 195.8 jit_solution(965326947175473212)
XLA Ops:
  0.6 5.6 %start.1 = (bf16[32,8,16,256]{3,2,1,0:T(8,128)(2,1)}, f32[2,8,128]{2,1,0:T(8,128)S(1)}) custom-call(f32[2,8,256,128]{3,2,1,0:T(8,128)} %bitcast.2, bf16[512,512]{1,0:T(8,128)(2,1)} %constant.85.table_hbm.held_5_), custom_call_target="tpu_custom_call" | custom-call | tf_op jit(solution)/shard_map/start/pallas_call | solution.py:417
  6.2 11.1 %all-to-all-start = ((bf16[32,8,16,256]{3,2,1,0:T(8,128)(2,1)}), bf16[32,8,16,256]{3,2,1,0:T(8,128)(2,1)}, u32[]{:S(2)}, u32[]{:S(2)}) async-start(bf16[32,8,16,256]{3,2,1,0:T(8,128)(2,1)} %get-tuple-element.15), calls=%async_computation | async-start | bytes 4194304 | tf_op jit(solution)/shard_map/all_to_all | solution.py:413
  17.3 1.4 collective-permute-start
  18.7 1.5 collective-permute-start.1
  20.2 2.4 %collective-permute-start.4 = (bf16[3,8,32,256]{3,2,1,0:T(8,128)(2,1)}, bf16[3,8,32,256]{3,2,1,0:T(8,128)(2,1)}, u32[]{:S(2)}, u32[]{:S(2)}) collective-permute-start(bf16[3,8,32,256]{3,2,1,0:T(8,128)(2,1)} %param.12), channel_id=1, source_target_pairs={{0,4},{1,5},{2,6},{3,7},{4,0},{5,1},{6,2},{7,3},{8,12},{9,13},{10,... | collective-permute-start | bytes 1179656 | tf_op jit(solution)/shard_map/ppermute | solution.py:385
  24.0 0.3 broadcast_in_dim.6
  24.3 1.0 constant_dynamic-update-slice_fusion.9
  25.4 4.1 %collective-permute-done = bf16[3,8,32,256]{3,2,1,0:T(8,128)(2,1)S(1)} collective-permute-done((bf16[3,8,32,256]{3,2,1,0:T(8,128)(2,1)}, bf16[3,8,32,256]{3,2,1,0:T(8,128)(2,1)S(1)}, u32[]{:S(2)}, u32[]{:S(2)}) %collective-permute-start) | collective-permute-done | bytes 393248 | tf_op jit(solution)/shard_map/ppermute | solution.py:385
  29.5 0.1 collective-permute-start.2
  29.5 0.0 collective-permute-done.1
  29.6 0.9 slice.17
  30.5 0.0 copy-start
  30.5 2.7 %collective-permute-start.3 = (bf16[3,4,32,256]{3,2,1,0:T(8,128)(2,1)S(1)}, bf16[3,4,32,256]{3,2,1,0:T(8,128)(2,1)S(1)}, u32[]{:S(2)}, u32[]{:S(2)}) collective-permute-start(bf16[3,4,32,256]{3,2,1,0:T(8,128)(2,1)S(1)} %slice.17), channel_id=1, source_target_pairs={{0,3},{1,0},{2,1},{3,2},{4,7},{5,4},{6,5},{7,6},{8,11},{9,8},{10,9... | collective-permute-start | bytes 589832 | tf_op jit(solution)/shard_map/ppermute | solution.py:385
  33.2 5.7 %collective-permute-done.4 = bf16[3,8,32,256]{3,2,1,0:T(8,128)(2,1)} collective-permute-done((bf16[3,8,32,256]{3,2,1,0:T(8,128)(2,1)}, bf16[3,8,32,256]{3,2,1,0:T(8,128)(2,1)}, u32[]{:S(2)}, u32[]{:S(2)}) %collective-permute-start.4) | collective-permute-done | bytes 393248 | tf_op jit(solution)/shard_map/ppermute | solution.py:385
  39.0 2.4 %collective-permute-start.6 = (bf16[3,8,32,256]{3,2,1,0:T(8,128)(2,1)}, bf16[3,8,32,256]{3,2,1,0:T(8,128)(2,1)S(1)}, u32[]{:S(2)}, u32[]{:S(2)}) collective-permute-start(bf16[3,8,32,256]{3,2,1,0:T(8,128)(2,1)} %collective-permute-done.4), channel_id=1, source_target_pairs={{0,3},{1,0},{2,1},{3,2},{4,7},{5,4},{6,5},{7,6},{8,11},{9,8},{10,9... | collective-permute-start | bytes 1179656 | tf_op jit(solution)/shard_map/ppermute | solution.py:385
  41.4 0.0 collective-permute-start.5
  41.4 1.0 constant_dynamic-update-slice_fusion.7
  42.4 0.0 collective-permute-done.2
  42.5 0.0 collective-permute-done.3
  42.5 1.0 constant_dynamic-update-slice_fusion.4
  43.5 5.7 %collective-permute-done.6 = bf16[3,8,32,256]{3,2,1,0:T(8,128)(2,1)S(1)} collective-permute-done((bf16[3,8,32,256]{3,2,1,0:T(8,128)(2,1)}, bf16[3,8,32,256]{3,2,1,0:T(8,128)(2,1)S(1)}, u32[]{:S(2)}, u32[]{:S(2)}) %collective-permute-start.6) | collective-permute-done | bytes 393248 | tf_op jit(solution)/shard_map/ppermute | solution.py:385
  49.2 3.5 %collective-permute-start.8 = (bf16[3,4,32,256]{3,2,1,0:T(8,128)(2,1)S(1)}, bf16[3,4,32,256]{3,2,1,0:T(8,128)(2,1)S(1)}, u32[]{:S(2)}, u32[]{:S(2)}) collective-permute-start(bf16[3,4,32,256]{3,2,1,0:T(8,128)(2,1)S(1)} %slice.19), channel_id=1, source_target_pairs={{0,3},{1,0},{2,1},{3,2},{4,7},{5,4},{6,5},{7,6},{8,11},{9,8},{10,9... | collective-permute-start | bytes 589832 | tf_op jit(solution)/shard_map/ppermute | solution.py:385
  52.7 0.0 collective-permute-done.5
  52.7 0.1 collective-permute-start.7
  52.9 6.0 %collective-permute-done.7 = bf16[3,4,32,256]{3,2,1,0:T(8,128)(2,1)S(1)} collective-permute-done((bf16[3,4,32,256]{3,2,1,0:T(8,128)(2,1)S(1)}, bf16[3,4,32,256]{3,2,1,0:T(8,128)(2,1)S(1)}, u32[]{:S(2)}, u32[]{:S(2)}) %collective-permute-start.7) | collective-permute-done | bytes 196640 | tf_op jit(solution)/shard_map/ppermute | solution.py:385
  59.0 0.0 collective-permute-done.8
  59.0 7.6 %all-to-all-done.planes_hbm = bf16[32,8,16,256]{3,2,1,0:T(8,128)(2,1)} async-done(((bf16[32,8,16,256]{3,2,1,0:T(8,128)(2,1)}), bf16[32,8,16,256]{3,2,1,0:T(8,128)(2,1)}, u32[]{:S(2)}, u32[]{:S(2)}) %all-to-all-start) | async-done | bytes 2097184 | tf_op jit(solution)/shard_map/all_to_all | solution.py:413
  66.6 0.0 copy-done
  66.6 8.6 %grid.2 = (bf16[32,16,768]{2,1,0:T(8,128)(2,1)S(1)}, bf16[512,512]{1,0:T(8,128)(2,1)S(1)}, bf16[256,256]{1,0:T(8,128)(2,1)S(1)}, bf16[256,256]{1,0:T(8,128)(2,1)...) custom-call(s32[1]{0:T(128)S(6)} %copy.24.scalars_0_.bound_ref, ...), custom_call_target="tpu_custom_call" | custom-call | tf_op jit(solution)/shard_map/grid/pallas_call | solution.py:434
  75.2 26.9 %all_to_all.20.came_ref = bf16[32,16,768]{2,1,0:T(8,128)(2,1)S(1)} all-to-all(bf16[32,16,768]{2,1,0:T(8,128)(2,1)S(1)} %get-tuple-element.17), channel_id=1, replica_groups=mesh['fft'=32,'scal'=8] {'fft'}, dimensions={0} | all-to-all | bytes 1572864 | tf_op jit(solution)/shard_map/all_to_all | solution.py:413
  102.1 4.2 %middle.1 = (bf16[32,8,16,256]{3,2,1,0:T(8,128)(2,1)S(1)}, f32[2,8,256,128]{3,2,1,0:T(8,128)S(1)}, f32[1]{0:T(128)}) custom-call(s32[1]{0:T(128)S(6)} %copy.24.scalars_0_.bound_ref, s32[1]{0:T(128)S(6)} %copy.23.scalars_1_.species_ref, f32[64]{0:T(128)S(1)} %copy-done, bf16[32,16,768]{2,1,0:T(8,128)(2,1)S(1)} %all_to_all.20.came_ref, ...), custom_call_target="tpu_custom_call" | custom-call | tf_op jit(solution)/shard_map/middle/pallas_call | solution.py:446
  106.4 54.3 %all_to_all.21.planes_hbm = bf16[32,8,16,256]{3,2,1,0:T(8,128)(2,1)S(1)} all-to-all(bf16[32,8,16,256]{3,2,1,0:T(8,128)(2,1)S(1)} %get-tuple-element.21), channel_id=1, replica_groups=mesh['fft'=32,'scal'=8] {'fft'}, dimensions={0} | all-to-all | bytes 4194304 | tf_op jit(solution)/shard_map/all_to_all | solution.py:413
  160.7 6.0 %grid.3 = bf16[32,16,768]{2,1,0:T(8,128)(2,1)S(1)} custom-call(bf16[32,8,16,256]{3,2,1,0:T(8,128)(2,1)S(1)} %all_to_all.21.planes_hbm, bf16[3,8,256,256]{3,2,1,0:T(8,128)(2,1)S(1)} %constant_dynamic-update-slice_fusion.speed_ref, f32[2,8,128]{2,1,0:T(8,128)S(1)} %get-tuple-element.16.stats_ref, bf16[512,512]{1,0:T(8,128)(2,1)S(1)} %get-tuple-element.22.held_0_, ...), custom_call_target="tpu_custom_call" | custom-call | tf_op jit(solution)/shard_map/grid/pallas_call | solution.py:434
  166.7 27.0 %all_to_all.22.came_ref = bf16[32,16,768]{2,1,0:T(8,128)(2,1)S(1)} all-to-all(bf16[32,16,768]{2,1,0:T(8,128)(2,1)S(1)} %grid.3), channel_id=1, replica_groups=mesh['fft'=32,'scal'=8] {'fft'}, dimensions={0} | all-to-all | bytes 1572864 | tf_op jit(solution)/shard_map/all_to_all | solution.py:413
  193.7 1.9 final.1
  (10 shorter events, 0.2 us)
Async XLA Ops:
  6.2 60.4 %all-to-all-start = ((bf16[32,8,16,256]{3,2,1,0:T(8,128)(2,1)}), bf16[32,8,16,256]{3,2,1,0:T(8,128)(2,1)}, u32[]{:S(2)}, u32[]{:S(2)}) async-start(bf16[32,8,16,256]{3,2,1,0:T(8,128)(2,1)} %get-tuple-element.15), calls=%async_computation | async-start | bytes 4194304 | tf_op jit(solution)/shard_map/all_to_all | solution.py:413
  17.3 12.1 %collective-permute-start = (bf16[3,8,32,256]{3,2,1,0:T(8,128)(2,1)}, bf16[3,8,32,256]{3,2,1,0:T(8,128)(2,1)S(1)}, u32[]{:S(2)}, u32[]{:S(2)}) collective-permute-start(bf16[3,8,32,256]{3,2,1,0:T(8,128)(2,1)} %param.12), channel_id=1, source_target_pairs={{0,1},{1,2},{2,3},{3,0},{4,5},{5,6},{6,7},{7,4},{8,9},{9,10},{10,1... | collective-permute-start | bytes 1179656 | tf_op jit(solution)/shard_map/ppermute | solution.py:385
  18.7 10.8 %collective-permute-start.1 = (bf16[3,8,32,256]{3,2,1,0:T(8,128)(2,1)}, bf16[3,8,32,256]{3,2,1,0:T(8,128)(2,1)}, u32[]{:S(2)}, u32[]{:S(2)}) collective-permute-start(bf16[3,8,32,256]{3,2,1,0:T(8,128)(2,1)} %param.12), channel_id=1, source_target_pairs={{0,3},{1,0},{2,1},{3,2},{4,7},{5,4},{6,5},{7,6},{8,11},{9,8},{10,9... | collective-permute-start | bytes 1179656 | tf_op jit(solution)/shard_map/ppermute | solution.py:385
  20.2 18.7 %collective-permute-start.4 = (bf16[3,8,32,256]{3,2,1,0:T(8,128)(2,1)}, bf16[3,8,32,256]{3,2,1,0:T(8,128)(2,1)}, u32[]{:S(2)}, u32[]{:S(2)}) collective-permute-start(bf16[3,8,32,256]{3,2,1,0:T(8,128)(2,1)} %param.12), channel_id=1, source_target_pairs={{0,4},{1,5},{2,6},{3,7},{4,0},{5,1},{6,2},{7,3},{8,12},{9,13},{10,... | collective-permute-start | bytes 1179656 | tf_op jit(solution)/shard_map/ppermute | solution.py:385
  29.5 13.0 %collective-permute-start.2 = (bf16[3,4,32,256]{3,2,1,0:T(8,128)(2,1)S(1)}, bf16[3,4,32,256]{3,2,1,0:T(8,128)(2,1)S(1)}, u32[]{:S(2)}, u32[]{:S(2)}) collective-permute-start(bf16[3,4,32,256]{3,2,1,0:T(8,128)(2,1)S(1)} %slice.16), channel_id=1, source_target_pairs={{0,1},{1,2},{2,3},{3,0},{4,5},{5,6},{6,7},{7,4},{8,9},{9,10},{10,1... | collective-permute-start | bytes 589832 | tf_op jit(solution)/shard_map/ppermute | solution.py:385
  30.5 36.1 %copy-start = (f32[64]{0:T(128)S(1)}, f32[64]{0:T(128)}, u32[]{:S(2)}) copy-start(f32[64]{0:T(128)} %base_ref.1) | copy-start | bytes 772
  30.5 12.0 %collective-permute-start.3 = (bf16[3,4,32,256]{3,2,1,0:T(8,128)(2,1)S(1)}, bf16[3,4,32,256]{3,2,1,0:T(8,128)(2,1)S(1)}, u32[]{:S(2)}, u32[]{:S(2)}) collective-permute-start(bf16[3,4,32,256]{3,2,1,0:T(8,128)(2,1)S(1)} %slice.17), channel_id=1, source_target_pairs={{0,3},{1,0},{2,1},{3,2},{4,7},{5,4},{6,5},{7,6},{8,11},{9,8},{10,9... | collective-permute-start | bytes 589832 | tf_op jit(solution)/shard_map/ppermute | solution.py:385
  39.0 10.2 %collective-permute-start.6 = (bf16[3,8,32,256]{3,2,1,0:T(8,128)(2,1)}, bf16[3,8,32,256]{3,2,1,0:T(8,128)(2,1)S(1)}, u32[]{:S(2)}, u32[]{:S(2)}) collective-permute-start(bf16[3,8,32,256]{3,2,1,0:T(8,128)(2,1)} %collective-permute-done.4), channel_id=1, source_target_pairs={{0,3},{1,0},{2,1},{3,2},{4,7},{5,4},{6,5},{7,6},{8,11},{9,8},{10,9... | collective-permute-start | bytes 1179656 | tf_op jit(solution)/shard_map/ppermute | solution.py:385
  41.4 11.4 %collective-permute-start.5 = (bf16[3,8,32,256]{3,2,1,0:T(8,128)(2,1)}, bf16[3,8,32,256]{3,2,1,0:T(8,128)(2,1)S(1)}, u32[]{:S(2)}, u32[]{:S(2)}) collective-permute-start(bf16[3,8,32,256]{3,2,1,0:T(8,128)(2,1)} %collective-permute-done.4), channel_id=1, source_target_pairs={{0,1},{1,2},{2,3},{3,0},{4,5},{5,6},{6,7},{7,4},{8,9},{9,10},{10,1... | collective-permute-start | bytes 1179656 | tf_op jit(solution)/shard_map/ppermute | solution.py:385
  49.2 9.7 %collective-permute-start.8 = (bf16[3,4,32,256]{3,2,1,0:T(8,128)(2,1)S(1)}, bf16[3,4,32,256]{3,2,1,0:T(8,128)(2,1)S(1)}, u32[]{:S(2)}, u32[]{:S(2)}) collective-permute-start(bf16[3,4,32,256]{3,2,1,0:T(8,128)(2,1)S(1)} %slice.19), channel_id=1, source_target_pairs={{0,3},{1,0},{2,1},{3,2},{4,7},{5,4},{6,5},{7,6},{8,11},{9,8},{10,9... | collective-permute-start | bytes 589832 | tf_op jit(solution)/shard_map/ppermute | solution.py:385
  52.7 6.2 %collective-permute-start.7 = (bf16[3,4,32,256]{3,2,1,0:T(8,128)(2,1)S(1)}, bf16[3,4,32,256]{3,2,1,0:T(8,128)(2,1)S(1)}, u32[]{:S(2)}, u32[]{:S(2)}) collective-permute-start(bf16[3,4,32,256]{3,2,1,0:T(8,128)(2,1)S(1)} %slice.18), channel_id=1, source_target_pairs={{0,1},{1,2},{2,3},{3,0},{4,5},{5,6},{6,7},{7,4},{8,9},{9,10},{10,1... | collective-permute-start | bytes 589832 | tf_op jit(solution)/shard_map/ppermute | solution.py:385

commit v5 on v4

--- a/solution.py
+++ b/solution.py
@@ -16,7 +16,7 @@
 KEPT = 96
 LIMIT = 86
 PACKED = ROWS * KEPT
-PITCH = 2 * N + 8
+PITCH = 2 * N + 4
 STEP = 0.2 * 2.0 * math.pi / N
 CELLS = float(N) ** 3
 F32 = jnp.float32
@@ -24,28 +24,43 @@
 
 
 def tables():
-    index = np.arange(N)
-    angles = (index[:, None] * index[None, :] % N).astype(np.float32) * np.float32(2.0 * math.pi / N)
-    cos = np.cos(angles) * np.float32(1.0 / math.sqrt(N))
-    sin = np.sin(angles) * np.float32(1.0 / math.sqrt(N))
-    weight = np.where(np.arange(HALF) == 0, 1.0, 2.0).astype(np.float32)[:, None]
-    inverse = np.block([[cos, -sin], [sin, cos]])
-    forward = np.block([[cos, sin], [-sin, cos]])
-    order = np.arange(2 * N).reshape(2, PEERS, ROWS).transpose(1, 0, 2).reshape(-1)
-    x_inv = np.concatenate([-weight * sin[:HALF], -weight * cos[:HALF]], axis=0)
-    keep = (np.arange(HALF) < LIMIT).astype(np.float32)[None, :]
-    x_fwd = np.concatenate([cos[:, :HALF] * keep, -sin[:, :HALF] * keep], axis=1)
+    def cos_sin(rows, columns):
+        angles = (rows[:, None] * columns[None, :] % N).astype(np.float32) * np.float32(2.0 * math.pi / N)
+        scale = np.float32(1.0 / math.sqrt(N))
+        return np.cos(angles) * scale, np.sin(angles) * scale
+
+    def inverse(rows, columns):
+        cos, sin = cos_sin(rows, columns)
+        return np.block([[cos, -sin], [sin, cos]])
+
+    def forward(rows, columns):
+        cos, sin = cos_sin(rows, columns)
+        return np.block([[cos, sin], [-sin, cos]])
+
+    def order(peers):
+        return np.arange(2 * peers * ROWS).reshape(2, peers, ROWS).transpose(1, 0, 2).reshape(-1)
+
+    index, low = np.arange(N), np.arange(HALF)
+    cos, sin = cos_sin(index, low)
+    weight = np.where(low == 0, 1.0, 2.0).astype(np.float32)[:, None]
+    keep = (low < LIMIT).astype(np.float32)[None, :]
+    halves = order(PEERS // 2)
     listed = {
-        "z_inv": inverse,
-        "y_inv": inverse[:, order],
-        "x_inv": x_inv,
-        "x_fwd": x_fwd,
-        "y_fwd": forward[order, :],
-        "z_fwd": forward[:, order],
+        "z_inv": np.stack([inverse(2 * low + turn, low) for turn in (0, 1)]),
+        "y_inv": np.stack([inverse(2 * low + turn, low)[:, halves] for turn in (0, 1)]),
+        "x_inv": np.concatenate([-weight * sin.T, -weight * cos.T], axis=0),
+        "x_fwd": np.concatenate([cos * keep, -sin * keep], axis=1),
+        "y_fwd": np.stack([forward(low, 2 * low + turn)[halves] for turn in (0, 1)]),
+        "z_fwd": forward(index, index)[:, order(PEERS)],
     }
     return {name: jnp.asarray(value.astype(np.float32)).astype(BF16) for name, value in listed.items()}
 
 
+def both_turns(x):
+    low, high = x[: x.shape[0] // 2], x[x.shape[0] // 2 :]
+    return low + high, low - high
+
+
 def dot(left, right):
     return jnp.dot(left, right, preferred_element_type=F32)
 
@@ -59,9 +74,11 @@
 
 
 def z_rows(real_part, imag_part, kz_wave):
-    both = jnp.concatenate([real_part, imag_part], axis=0)
-    waves = jnp.concatenate([kz_wave, kz_wave], axis=0)
-    return jnp.concatenate([both.astype(BF16), (waves * both).astype(BF16)], axis=1)
+    columns = [
+        [jnp.concatenate(pair, axis=0).astype(BF16) for pair in zip(both_turns(real), both_turns(imag))]
+        for real, imag in ((real_part, imag_part), (kz_wave * real_part, kz_wave * imag_part))
+    ]
+    return [jnp.concatenate(pair, axis=1) for pair in zip(*columns)]
 
 
 def send_planes(first, count, planes_ref, whole_ref, deriv_ref):
@@ -70,9 +87,9 @@
             peer = first + step * UNROLL + turn
             for local in range(ROWS):
                 for at, ref in ((0, whole_ref), (HALF, deriv_ref)):
-                    start = peer * ROWS + local
+                    start = local % 2 * N + peer * (ROWS // 2) + local // 2
                     real_part = ref[pl.ds(start, ROWS, stride=PITCH), :]
-                    imag_part = ref[pl.ds(start + N, ROWS, stride=PITCH), :]
+                    imag_part = ref[pl.ds(start + HALF, ROWS, stride=PITCH), :]
                     tile = jnp.concatenate([real_part, imag_part], axis=0).astype(BF16)
                     planes_ref[peer, local, :, at : at + HALF] = tile
         return carry
@@ -80,11 +97,16 @@
     lax.fori_loop(0, count // UNROLL, some_peers, 0)
 
 
+def row_of(block, shift=0):
+    return block * PITCH + shift if isinstance(block, int) else pl.multiple_of(block * PITCH + shift, 4)
+
+
 def z_inverse(local, rows, table_ref, whole_ref, deriv_ref):
-    found = dot(table_ref[...], rows)
-    start = pl.multiple_of(local * PITCH, 8)
-    whole_ref[pl.ds(start, 2 * N), :] = found[:, :HALF]
-    deriv_ref[pl.ds(start, 2 * N), :] = found[:, HALF:]
+    for turn in (0, 1):
+        found = dot(table_ref[turn], rows[turn])
+        part = pl.ds(row_of(local, turn * N), N)
+        whole_ref[part, :] = found[:, :HALF]
+        deriv_ref[part, :] = found[:, HALF:]
 
 
 def waves_of(local):
@@ -184,29 +206,28 @@
     y_inv_ref, x_inv_ref, x_fwd_ref, y_fwd_ref = held[:4]
     peak_ref[...] = jnp.zeros_like(peak_ref)
     row = iota((count, HALF), 0)
-    ky_wave = signed(row // (2 * ROWS) * ROWS + row % ROWS)
-    kx_wave = iota((N, HALF), 1).astype(F32)
+    ky_wave = signed(row // (2 * ROWS) * ROWS + row % ROWS).astype(BF16)
+    kx_wave = iota((HALF, HALF), 1).astype(F32)
 
     def one_pair(step, carry):
         if apart:
             for k in range(PAIR):
                 came_plane(step * PAIR + k).wait()
+            for load in loads[:4]:
+                pl.when(step == 0)(load.wait)
         came = [planes_ref[:, step * PAIR + k].reshape(count, N) for k in range(PAIR)]
-        scaled = [(ky_wave * part[:, :HALF].astype(F32)).astype(BF16) for part in came]
-        if apart:
-            pl.when(step == 0)(loads[0].wait)
-        y_section = dot(y_inv_ref[...], jnp.concatenate(came + scaled, axis=1))
+        scaled = [ky_wave * part[:, :HALF] for part in came]
+        pairs = both_turns(jnp.concatenate(came + scaled, axis=1))
+        y_section = [dot(y_inv_ref[turn], pairs[turn]) for turn in (0, 1)]
         x_rows = []
         for k in range(PAIR):
             starts = (k * N, PAIR * N + k * HALF, k * N + HALF)
             for which, at in enumerate(starts):
-                halves = [y_section[part * N : (part + 1) * N, at : at + HALF] for part in (0, 1)]
-                if which == 0:
-                    halves = [kx_wave * half for half in halves]
-                x_rows.append(jnp.concatenate(halves, axis=1).astype(BF16))
-        if apart:
-            for load in loads[1:4]:
-                pl.when(step == 0)(load.wait)
+                for found in y_section:
+                    halves = [found[part * HALF : (part + 1) * HALF, at : at + HALF] for part in (0, 1)]
+                    if which == 0:
+                        halves = [kx_wave * half for half in halves]
+                    x_rows.append(jnp.concatenate(halves, axis=1).astype(BF16))
         gradients = dot(jnp.concatenate(x_rows, axis=0), x_inv_ref[...])
         fields = []
         for k in range(PAIR):
@@ -218,14 +239,17 @@
             square = parts[0] * parts[0] + parts[1] * parts[1] + parts[2] * parts[2]
             peak_ref[...] = jnp.maximum(peak_ref[...], jnp.max(square.reshape(N // 8, 8, N), axis=0))
         x_section = dot(jnp.concatenate(fields, axis=0), x_fwd_ref[...]).astype(BF16)
-        columns = []
+        sums = []
+        for turn in (0, 1):
+            columns = []
+            for k in range(PAIR):
+                part = x_section[k * N + turn * HALF : k * N + (turn + 1) * HALF]
+                columns.append(jnp.concatenate([part[:, :HALF], part[:, HALF:]], axis=0))
+            sums.append(dot(y_fwd_ref[turn], jnp.concatenate(columns, axis=1)))
         for k in range(PAIR):
-            part = x_section[k * N : (k + 1) * N]
-            columns.append(jnp.concatenate([part[:, :HALF], part[:, HALF:]], axis=0))
-        sums = dot(y_fwd_ref[...], jnp.concatenate(columns, axis=1))
-        for k in range(PAIR):
-            start = pl.multiple_of((step * PAIR + k) * PITCH, 8)
-            sums_ref[pl.ds(start, count), :] = sums[:, k * HALF : (k + 1) * HALF]
+            even, odd = (found[:, k * HALF : (k + 1) * HALF] for found in sums)
+            sums_ref[pl.ds(row_of(step * PAIR + k), N), :] = even + odd
+            sums_ref[pl.ds(row_of(step * PAIR + k, N), N), :] = even - odd
         return carry
 
     lax.fori_loop(0, ROWS // PAIR, one_pair, 0)
@@ -371,8 +395,7 @@
     return pltpu.VMEM((ROWS * PITCH, HALF), F32)
 
 
-BIG = pltpu.VMEM((2 * N, 2 * N), BF16)
-SMALL = pltpu.VMEM((N, N), BF16)
+BIG = pltpu.VMEM((2, N, N), BF16)
 HELD = pltpu.VMEM(STATE, F32)
 
 
@@ -380,6 +403,9 @@
     groups = lax.axis_size("scal")
     me = lax.axis_index("scal")
     ring = 4
+    high, low = me // ring, me % ring
+    planes, rows = velocity.shape[1], velocity.shape[2] // 2
+    velocity = velocity.reshape(3, planes, rows, 2, N).swapaxes(2, 3)
 
     def moved(x, change):
         return lax.ppermute(x, "scal", [(s, change(s)) for s in range(groups)])
@@ -388,12 +414,11 @@
         return lambda s: s // ring * ring + (s + shift) % ring
 
     across = moved(velocity, lambda s: (s + ring) % groups)
-    out = jnp.zeros((*velocity.shape[:2], N, N), velocity.dtype)
-    high, low = me // ring, me % ring
-    half = velocity.shape[1] // 2
+    out = jnp.zeros((3, planes, 2, HALF, N), velocity.dtype)
+    half = planes // 2
 
     def placed(out, x, owner, first=0):
-        return lax.dynamic_update_slice(out, x, (0, first, owner * x.shape[2], 0))
+        return lax.dynamic_update_slice(out, x, (0, first, 0, owner * rows, 0))
 
     for x, own in ((velocity, high), (across, 1 - high)):
         up = moved(x, beside(1))
@@ -406,7 +431,7 @@
         out = placed(out, down, start + (low + 1) % ring)
         out = placed(out, far_up, start + (low + 2) % ring)
         out = placed(out, far_down, start + (low + 2) % ring, half)
-    return out
+    return out.reshape(3, planes, N, N)
 
 
 def exchanged(x):

time: 197 us -> 192 us (0.975)
  Pallas kernels: 26.3 us -> 21.8 us
  waiting for transfers between devices: 29.1 us -> 26.2 us
  local copies, waits for them, and re-layouts: 4.59 us -> 6.61 us
    pallas_call x2, Pallas kernels: 14.6 us -> 11.3 us  [grid_call(): pl.pallas_call(grid_kernel, in_specs=[(SCALARS,) * len(scalars), spec, NE...]
    all_to_all x1, waiting for transfers between devices: 7.63 us -> 5.42 us  [exchanged(): return lax.all_to_all(x, 'fft', 0, 0, tiled=True)]
  transfers between devices with their start and end apart: 10 -> 10, of which waited for: 5 -> 5; matrix products, arithmetic and copies ran while one was open for 2% -> 3% of each run, Pallas kernels for 0% -> 0%
where the time goes in v5:
time: 192 us; the launch traced here: 191 us
  blocking collectives  108 us (56%)
  waiting for transfers between devices  26.2 us (14%)
  starting transfers between devices  26.1 us (14%)
  Pallas kernels  21.8 us (11%)
  local copies, waits for them, and re-layouts  6.61 us (3%)
  between operations  2.33 us (1%)
    all_to_all x3, blocking collectives, exchanged(): return lax.all_to_all(x, 'fft', 0, 0, tiled=True)  108 us
    ppermute x9, waiting for transfers between devices, moved(): return lax.ppermute(x, 'scal', [(s, change(s)) for s in range(groups)])  20.8 us
    ppermute x9, starting transfers between devices, moved(): return lax.ppermute(x, 'scal', [(s, change(s)) for s in range(groups)])  15 us
    pallas_call x2, Pallas kernels, grid_call(): pl.pallas_call(grid_kernel, in_specs=[(SCALARS,) * len(scalars), spec, NE...  11.3 us
    all_to_all x1, starting transfers between devices, exchanged(): return lax.all_to_all(x, 'fft', 0, 0, tiled=True)  11.1 us
    all_to_all x1, waiting for transfers between devices, exchanged(): return lax.all_to_all(x, 'fft', 0, 0, tiled=True)  5.42 us
    pallas_call x1, Pallas kernels, start_call(): pl.pallas_call(start_kernel, in_specs=[FAR, FAR], out_specs=[FAR, NEAR],...  4.88 us
  transfers between devices with their start and end apart: 10, of which 5 were waited for; matrix products, arithmetic and copies ran while one was open for 3% of the time, Pallas kernels for 0%

profile of v5, /device:TPU:1, one launch (start us, length us, event | category | flops | bytes accessed | tf_op | source)
XLA Modules:
  0.0 191.1 jit_solution(15915313144457940084)
XLA Ops:
  0.6 0.0 copy-start.1
  0.6 4.9 %start.1 = (bf16[32,8,16,256]{3,2,1,0:T(8,128)(2,1)}, f32[2,8,128]{2,1,0:T(8,128)S(1)}) custom-call(f32[2,8,256,128]{3,2,1,0:T(8,128)} %bitcast.12, bf16[2,256,256]{2,1,0:T(8,128)(2,1)} %constant.85.table_hbm.held_5_), custom_call_target="tpu_custom_call" | custom-call | tf_op jit(solution)/shard_map/start/pallas_call | solution.py:442
  5.5 11.1 %all-to-all-start = ((bf16[32,8,16,256]{3,2,1,0:T(8,128)(2,1)}), bf16[32,8,16,256]{3,2,1,0:T(8,128)(2,1)}, u32[]{:S(2)}, u32[]{:S(2)}) async-start(bf16[32,8,16,256]{3,2,1,0:T(8,128)(2,1)} %get-tuple-element.15), calls=%async_computation | async-start | bytes 4194304 | tf_op jit(solution)/shard_map/all_to_all | solution.py:438
  16.6 0.0 copy-done.1
  16.7 0.2 reshape.10
  16.8 0.8 copy.17
  17.6 2.7 %collective-permute-start.1 = (bf16[3,8,2,16,256]{4,3,2,1,0:T(8,128)(2,1)}, bf16[3,8,2,16,256]{4,3,2,1,0:T(8,128)(2,1)}, u32[]{:S(2)}, u32[]{:S(2)}) collective-permute-start(bf16[3,8,2,16,256]{4,3,2,1,0:T(8,128)(2,1)} %bitcast.9), channel_id=1, source_target_pairs={{0,3},{1,0},{2,1},{3,2},{4,7},{5,4},{6,5},{7,6},{8,11},{9,8},{10,9... | collective-permute-start | bytes 1179656 | tf_op jit(solution)/shard_map/ppermute | solution.py:411
  20.4 0.0 collective-permute-start
  20.4 2.5 %collective-permute-start.4 = (bf16[3,8,2,16,256]{4,3,2,1,0:T(8,128)(2,1)}, bf16[3,8,2,16,256]{4,3,2,1,0:T(8,128)(2,1)}, u32[]{:S(2)}, u32[]{:S(2)}) collective-permute-start(bf16[3,8,2,16,256]{4,3,2,1,0:T(8,128)(2,1)} %bitcast.9), channel_id=1, source_target_pairs={{0,4},{1,5},{2,6},{3,7},{4,0},{5,1},{6,2},{7,3},{8,12},{9,13},{10,... | collective-permute-start | bytes 1179656 | tf_op jit(solution)/shard_map/ppermute | solution.py:411
  24.1 0.4 broadcast_in_dim.6
  24.5 0.1 constant_dynamic-update-slice_fusion.9
  24.6 4.3 %collective-permute-done.1 = bf16[3,8,2,16,256]{4,3,2,1,0:T(8,128)(2,1)} collective-permute-done((bf16[3,8,2,16,256]{4,3,2,1,0:T(8,128)(2,1)}, bf16[3,8,2,16,256]{4,3,2,1,0:T(8,128)(2,1)}, u32[]{:S(2)}, u32[]{:S(2)}) %collective-permute-start.1) | collective-permute-done | bytes 393248 | tf_op jit(solution)/shard_map/ppermute | solution.py:411
  28.8 0.9 slice.17
  29.8 3.5 %collective-permute-start.3 = (bf16[3,4,2,16,256]{4,3,2,1,0:T(8,128)(2,1)S(1)}, bf16[3,4,2,16,256]{4,3,2,1,0:T(8,128)(2,1)S(1)}, u32[]{:S(2)}, u32[]{:S(2)}) collective-permute-start(bf16[3,4,2,16,256]{4,3,2,1,0:T(8,128)(2,1)S(1)} %slice.17), channel_id=1, source_target_pairs={{0,3},{1,0},{2,1},{3,2},{4,7},{5,4},{6,5},{7,6},{8,11},{9,8},{10,9... | collective-permute-start | bytes 589832 | tf_op jit(solution)/shard_map/ppermute | solution.py:411
  33.3 0.0 collective-permute-done
  33.3 0.9 slice.16
  34.2 0.0 copy-start
  34.2 0.1 collective-permute-start.2
  34.3 5.5 %collective-permute-done.4 = bf16[3,8,2,16,256]{4,3,2,1,0:T(8,128)(2,1)} collective-permute-done((bf16[3,8,2,16,256]{4,3,2,1,0:T(8,128)(2,1)}, bf16[3,8,2,16,256]{4,3,2,1,0:T(8,128)(2,1)}, u32[]{:S(2)}, u32[]{:S(2)}) %collective-permute-start.4) | collective-permute-done | bytes 393248 | tf_op jit(solution)/shard_map/ppermute | solution.py:411
  39.8 2.7 %collective-permute-start.6 = (bf16[3,8,2,16,256]{4,3,2,1,0:T(8,128)(2,1)}, bf16[3,8,2,16,256]{4,3,2,1,0:T(8,128)(2,1)S(1)}, u32[]{:S(2)}, u32[]{:S(2)}) collective-permute-start(bf16[3,8,2,16,256]{4,3,2,1,0:T(8,128)(2,1)} %collective-permute-done.4), channel_id=1, source_target_pairs={{0,3},{1,0},{2,1},{3,2},{4,7},{5,4},{6,5},{7,6},{8,11},{9,8},{10,9... | collective-permute-start | bytes 1179656 | tf_op jit(solution)/shard_map/ppermute | solution.py:411
  42.5 0.0 collective-permute-start.5
  42.5 1.0 constant_dynamic-update-slice_fusion.8
  43.5 1.0 constant_dynamic-update-slice_fusion.7
  44.6 0.0 collective-permute-done.2
  44.6 0.0 collective-permute-done.3
  44.7 1.0 constant_dynamic-update-slice_fusion.4
  45.7 5.0 %collective-permute-done.6 = bf16[3,8,2,16,256]{4,3,2,1,0:T(8,128)(2,1)S(1)} collective-permute-done((bf16[3,8,2,16,256]{4,3,2,1,0:T(8,128)(2,1)}, bf16[3,8,2,16,256]{4,3,2,1,0:T(8,128)(2,1)S(1)}, u32[]{:S(2)}, u32[]{:S(2)}) %collective-permute-start.6) | collective-permute-done | bytes 393248 | tf_op jit(solution)/shard_map/ppermute | solution.py:411
  50.7 3.5 %collective-permute-start.8 = (bf16[3,4,2,16,256]{4,3,2,1,0:T(8,128)(2,1)S(1)}, bf16[3,4,2,16,256]{4,3,2,1,0:T(8,128)(2,1)S(1)}, u32[]{:S(2)}, u32[]{:S(2)}) collective-permute-start(bf16[3,4,2,16,256]{4,3,2,1,0:T(8,128)(2,1)S(1)} %slice.19), channel_id=1, source_target_pairs={{0,3},{1,0},{2,1},{3,2},{4,7},{5,4},{6,5},{7,6},{8,11},{9,8},{10,9... | collective-permute-start | bytes 589832 | tf_op jit(solution)/shard_map/ppermute | solution.py:411
  54.2 0.0 collective-permute-done.5
  54.2 0.1 collective-permute-start.7
  54.4 6.0 %collective-permute-done.7 = bf16[3,4,2,16,256]{4,3,2,1,0:T(8,128)(2,1)S(1)} collective-permute-done((bf16[3,4,2,16,256]{4,3,2,1,0:T(8,128)(2,1)S(1)}, bf16[3,4,2,16,256]{4,3,2,1,0:T(8,128)(2,1)S(1)}, u32[]{:S(2)}, u32[]{:S(2)}) %collective-permute-start.7) | collective-permute-done | bytes 196640 | tf_op jit(solution)/shard_map/ppermute | solution.py:411
  60.5 0.0 collective-permute-done.8
  60.5 5.4 %all-to-all-done.planes_hbm = bf16[32,8,16,256]{3,2,1,0:T(8,128)(2,1)} async-done(((bf16[32,8,16,256]{3,2,1,0:T(8,128)(2,1)}), bf16[32,8,16,256]{3,2,1,0:T(8,128)(2,1)}, u32[]{:S(2)}, u32[]{:S(2)}) %all-to-all-start) | async-done | bytes 2097184 | tf_op jit(solution)/shard_map/all_to_all | solution.py:438
  65.9 0.0 copy-done
  66.0 6.7 %grid.2 = (bf16[32,16,768]{2,1,0:T(8,128)(2,1)S(1)}, bf16[2,256,256]{2,1,0:T(8,128)(2,1)S(1)}, bf16[256,256]{1,0:T(8,128)(2,1)S(1)}, bf16[256,256]{1,0:T(8,128)(...) custom-call(s32[1]{0:T(128)S(6)} %copy.29.scalars_0_.bound_ref, ...), custom_call_target="tpu_custom_call" | custom-call | tf_op jit(solution)/shard_map/grid/pallas_call | solution.py:459
  72.6 26.7 %all_to_all.20.came_ref = bf16[32,16,768]{2,1,0:T(8,128)(2,1)S(1)} all-to-all(bf16[32,16,768]{2,1,0:T(8,128)(2,1)S(1)} %get-tuple-element.17), channel_id=1, replica_groups=mesh['fft'=32,'scal'=8] {'fft'}, dimensions={0} | all-to-all | bytes 1572864 | tf_op jit(solution)/shard_map/all_to_all | solution.py:438
  99.3 3.7 %middle.1 = (bf16[32,8,16,256]{3,2,1,0:T(8,128)(2,1)S(1)}, f32[2,8,256,128]{3,2,1,0:T(8,128)S(1)}, f32[1]{0:T(128)}) custom-call(s32[1]{0:T(128)S(6)} %copy.29.scalars_0_.bound_ref, s32[1]{0:T(128)S(6)} %copy.28.scalars_1_.species_ref, f32[64]{0:T(128)S(1)} %copy-done, bf16[32,16,768]{2,1,0:T(8,128)(2,1)S(1)} %all_to_all.20.came_ref, ...), custom_call_target="tpu_custom_call" | custom-call | tf_op jit(solution)/shard_map/middle/pallas_call | solution.py:471
  103.1 54.3 %all_to_all.21.planes_hbm = bf16[32,8,16,256]{3,2,1,0:T(8,128)(2,1)S(1)} all-to-all(bf16[32,8,16,256]{3,2,1,0:T(8,128)(2,1)S(1)} %get-tuple-element.21), channel_id=1, replica_groups=mesh['fft'=32,'scal'=8] {'fft'}, dimensions={0} | all-to-all | bytes 4194304 | tf_op jit(solution)/shard_map/all_to_all | solution.py:438
  157.4 4.7 %grid.3 = bf16[32,16,768]{2,1,0:T(8,128)(2,1)S(1)} custom-call(bf16[32,8,16,256]{3,2,1,0:T(8,128)(2,1)S(1)} %all_to_all.21.planes_hbm, bf16[3,8,256,256]{3,2,1,0:T(8,128)(2,1)S(1)} %bitcast.11, f32[2,8,128]{2,1,0:T(8,128)S(1)} %get-tuple-element.16.stats_ref, bf16[2,256,256]{2,1,0:T(8,128)(2,1)S(1)} %get-tuple-element.22.held_0_, ...), custom_call_target="tpu_custom_call" | custom-call | tf_op jit(solution)/shard_map/grid/pallas_call | solution.py:459
  162.0 27.0 %all_to_all.22.came_ref = bf16[32,16,768]{2,1,0:T(8,128)(2,1)S(1)} all-to-all(bf16[32,16,768]{2,1,0:T(8,128)(2,1)S(1)} %grid.3), channel_id=1, replica_groups=mesh['fft'=32,'scal'=8] {'fft'}, dimensions={0} | all-to-all | bytes 1572864 | tf_op jit(solution)/shard_map/all_to_all | solution.py:438
  189.0 1.9 %final.1 = f32[2,8,256,128]{3,2,1,0:T(8,128)} custom-call(s32[1]{0:T(128)S(6)} %copy.29.scalars_0_.bound_ref, bf16[32,16,768]{2,1,0:T(8,128)(2,1)S(1)} %all_to_all.22.came_ref, f32[2,8,256,128]{3,2,1,0:T(8,128)S(1)} %get-tuple-element.26.kept_ref, bf16[512,512]{1,0:T(8,128)(2,1)S(1)} %get-tuple-element.19.z_fwd_ref), custom_call_target="tpu_custom_call" | custom-call | tf_op jit(solution)/shard_map/final/pallas_call | solution.py:483
  (8 shorter events, 0.2 us)
Async XLA Ops:
  0.6 16.0 %copy-start.1 = (bf16[3,8,32,256]{3,2,1,0:T(8,128)(2,1)S(1)}, bf16[3,8,32,256]{3,2,1,0:T(8,128)(2,1)}, u32[]{:S(2)}) copy-start(bf16[3,8,32,256]{3,2,1,0:T(8,128)(2,1)} %param.12) | copy-start | bytes 1179652
  5.5 60.4 %all-to-all-start = ((bf16[32,8,16,256]{3,2,1,0:T(8,128)(2,1)}), bf16[32,8,16,256]{3,2,1,0:T(8,128)(2,1)}, u32[]{:S(2)}, u32[]{:S(2)}) async-start(bf16[32,8,16,256]{3,2,1,0:T(8,128)(2,1)} %get-tuple-element.15), calls=%async_computation | async-start | bytes 4194304 | tf_op jit(solution)/shard_map/all_to_all | solution.py:438
  17.6 11.2 %collective-permute-start.1 = (bf16[3,8,2,16,256]{4,3,2,1,0:T(8,128)(2,1)}, bf16[3,8,2,16,256]{4,3,2,1,0:T(8,128)(2,1)}, u32[]{:S(2)}, u32[]{:S(2)}) collective-permute-start(bf16[3,8,2,16,256]{4,3,2,1,0:T(8,128)(2,1)} %bitcast.9), channel_id=1, source_target_pairs={{0,3},{1,0},{2,1},{3,2},{4,7},{5,4},{6,5},{7,6},{8,11},{9,8},{10,9... | collective-permute-start | bytes 1179656 | tf_op jit(solution)/shard_map/ppermute | solution.py:411
  20.4 12.9 %collective-permute-start = (bf16[3,8,2,16,256]{4,3,2,1,0:T(8,128)(2,1)}, bf16[3,8,2,16,256]{4,3,2,1,0:T(8,128)(2,1)}, u32[]{:S(2)}, u32[]{:S(2)}) collective-permute-start(bf16[3,8,2,16,256]{4,3,2,1,0:T(8,128)(2,1)} %bitcast.9), channel_id=1, source_target_pairs={{0,1},{1,2},{2,3},{3,0},{4,5},{5,6},{6,7},{7,4},{8,9},{9,10},{10,1... | collective-permute-start | bytes 1179656 | tf_op jit(solution)/shard_map/ppermute | solution.py:411
  20.4 19.5 %collective-permute-start.4 = (bf16[3,8,2,16,256]{4,3,2,1,0:T(8,128)(2,1)}, bf16[3,8,2,16,256]{4,3,2,1,0:T(8,128)(2,1)}, u32[]{:S(2)}, u32[]{:S(2)}) collective-permute-start(bf16[3,8,2,16,256]{4,3,2,1,0:T(8,128)(2,1)} %bitcast.9), channel_id=1, source_target_pairs={{0,4},{1,5},{2,6},{3,7},{4,0},{5,1},{6,2},{7,3},{8,12},{9,13},{10,... | collective-permute-start | bytes 1179656 | tf_op jit(solution)/shard_map/ppermute | solution.py:411
  29.8 14.8 %collective-permute-start.3 = (bf16[3,4,2,16,256]{4,3,2,1,0:T(8,128)(2,1)S(1)}, bf16[3,4,2,16,256]{4,3,2,1,0:T(8,128)(2,1)S(1)}, u32[]{:S(2)}, u32[]{:S(2)}) collective-permute-start(bf16[3,4,2,16,256]{4,3,2,1,0:T(8,128)(2,1)S(1)} %slice.17), channel_id=1, source_target_pairs={{0,3},{1,0},{2,1},{3,2},{4,7},{5,4},{6,5},{7,6},{8,11},{9,8},{10,9... | collective-permute-start | bytes 589832 | tf_op jit(solution)/shard_map/ppermute | solution.py:411
  34.2 31.7 %copy-start = (f32[64]{0:T(128)S(1)}, f32[64]{0:T(128)}, u32[]{:S(2)}) copy-start(f32[64]{0:T(128)} %base_ref.1) | copy-start | bytes 772
  34.2 10.4 %collective-permute-start.2 = (bf16[3,4,2,16,256]{4,3,2,1,0:T(8,128)(2,1)S(1)}, bf16[3,4,2,16,256]{4,3,2,1,0:T(8,128)(2,1)S(1)}, u32[]{:S(2)}, u32[]{:S(2)}) collective-permute-start(bf16[3,4,2,16,256]{4,3,2,1,0:T(8,128)(2,1)S(1)} %slice.16), channel_id=1, source_target_pairs={{0,1},{1,2},{2,3},{3,0},{4,5},{5,6},{6,7},{7,4},{8,9},{9,10},{10,1... | collective-permute-start | bytes 589832 | tf_op jit(solution)/shard_map/ppermute | solution.py:411
  39.8 10.9 %collective-permute-start.6 = (bf16[3,8,2,16,256]{4,3,2,1,0:T(8,128)(2,1)}, bf16[3,8,2,16,256]{4,3,2,1,0:T(8,128)(2,1)S(1)}, u32[]{:S(2)}, u32[]{:S(2)}) collective-permute-start(bf16[3,8,2,16,256]{4,3,2,1,0:T(8,128)(2,1)} %collective-permute-done.4), channel_id=1, source_target_pairs={{0,3},{1,0},{2,1},{3,2},{4,7},{5,4},{6,5},{7,6},{8,11},{9,8},{10,9... | collective-permute-start | bytes 1179656 | tf_op jit(solution)/shard_map/ppermute | solution.py:411
  42.5 11.7 %collective-permute-start.5 = (bf16[3,8,2,16,256]{4,3,2,1,0:T(8,128)(2,1)}, bf16[3,8,2,16,256]{4,3,2,1,0:T(8,128)(2,1)S(1)}, u32[]{:S(2)}, u32[]{:S(2)}) collective-permute-start(bf16[3,8,2,16,256]{4,3,2,1,0:T(8,128)(2,1)} %collective-permute-done.4), channel_id=1, source_target_pairs={{0,1},{1,2},{2,3},{3,0},{4,5},{5,6},{6,7},{7,4},{8,9},{9,10},{10,1... | collective-permute-start | bytes 1179656 | tf_op jit(solution)/shard_map/ppermute | solution.py:411
  50.7 9.8 %collective-permute-start.8 = (bf16[3,4,2,16,256]{4,3,2,1,0:T(8,128)(2,1)S(1)}, bf16[3,4,2,16,256]{4,3,2,1,0:T(8,128)(2,1)S(1)}, u32[]{:S(2)}, u32[]{:S(2)}) collective-permute-start(bf16[3,4,2,16,256]{4,3,2,1,0:T(8,128)(2,1)S(1)} %slice.19), channel_id=1, source_target_pairs={{0,3},{1,0},{2,1},{3,2},{4,7},{5,4},{6,5},{7,6},{8,11},{9,8},{10,9... | collective-permute-start | bytes 589832 | tf_op jit(solution)/shard_map/ppermute | solution.py:411
  54.2 6.2 %collective-permute-start.7 = (bf16[3,4,2,16,256]{4,3,2,1,0:T(8,128)(2,1)S(1)}, bf16[3,4,2,16,256]{4,3,2,1,0:T(8,128)(2,1)S(1)}, u32[]{:S(2)}, u32[]{:S(2)}) collective-permute-start(bf16[3,4,2,16,256]{4,3,2,1,0:T(8,128)(2,1)S(1)} %slice.18), channel_id=1, source_target_pairs={{0,1},{1,2},{2,3},{3,0},{4,5},{5,6},{6,7},{7,4},{8,9},{9,10},{10,1... | collective-permute-start | bytes 589832 | tf_op jit(solution)/shard_map/ppermute | solution.py:411

commit v6 on v5

--- a/solution.py
+++ b/solution.py
@@ -12,10 +12,9 @@
 HALF = 128
 PEERS = 32
 ROWS = N // PEERS
-GROUP = 4
-KEPT = 96
+KEPT = 88
 LIMIT = 86
-PACKED = ROWS * KEPT
+BLOCKS = ROWS * KEPT // HALF
 PITCH = 2 * N + 4
 STEP = 0.2 * 2.0 * math.pi / N
 CELLS = float(N) ** 3
@@ -165,21 +164,34 @@
     return high, middle, (rest - middle).astype(BF16).astype(F32)
 
 
-def packed_four(parts):
+def place_of(row):
+    return row * KEPT // HALF, row * KEPT % HALF
+
+
+def packed(parts):
     lane = iota((2 * ROWS, HALF), 1)
-    turned = [parts[0]] + [pltpu.roll(parts[k], HALF - 32 * k, 1) for k in (1, 2, 3)]
-    return [jnp.where(lane < HALF - 32 * (k + 1), turned[k], turned[k + 1]) for k in (0, 1, 2)]
-
-
-def unpacked_four(packed):
+    blocks = [None] * (BLOCKS + 1)
+    for row, part in enumerate(parts):
+        block, shift = place_of(row)
+        turned = pltpu.roll(part, shift, 1) if shift else part
+        blocks[block] = turned if shift == 0 else jnp.where(lane < shift, blocks[block], turned)
+        if shift + KEPT > HALF:
+            blocks[block + 1] = turned
+    real_part, imag_part = blocks[BLOCKS][:ROWS], blocks[BLOCKS][ROWS:]
+    blocks[BLOCKS] = jnp.where(lane[:ROWS] < HALF // 2, real_part, pltpu.roll(imag_part, HALF // 2, 1))
+    return blocks
+
+
+def unpacked(blocks):
     lane = iota((2 * N, HALF), 1)
-    first, second, third = (packed[:, k * HALF : (k + 1) * HALF] for k in (0, 1, 2))
-    return [
-        first,
-        pltpu.roll(jnp.where(lane >= 96, first, second), 32, 1),
-        pltpu.roll(jnp.where(lane >= 64, second, third), 64, 1),
-        pltpu.roll(third, 96, 1),
-    ]
+    parts = []
+    for row in range(ROWS):
+        block, shift = place_of(row)
+        part = blocks[block]
+        if shift + KEPT > HALF:
+            part = jnp.where(lane >= shift, part, blocks[block + 1])
+        parts.append(pltpu.roll(part, HALF - shift, 1) if shift else part)
+    return parts
 
 
 def grid_kernel(scalars, planes_hbm, speed_ref, stats_ref, held, out_ref, passed, sums_ref, peak_ref, *apart):
@@ -260,23 +272,21 @@
         pieces.extend(in_three(jnp.broadcast_to(value, shape)))
     line = jnp.zeros(shape, F32)
     for k, piece in enumerate(pieces):
-        line = jnp.where((iota(shape, 0) == 0) & (iota(shape, 1) == LIMIT + k), piece, line)
+        line = jnp.where((iota(shape, 0) == k) & (iota(shape, 1) == LIMIT), piece, line)
 
     def some_peers(step, carry):
         for turn in range(SENDS):
             peer = step * SENDS + turn
-            for group in range(ROWS // GROUP):
-                parts = []
-                for pos in range(GROUP):
-                    start = peer * 2 * ROWS + group * GROUP + pos
-                    real_part = sums_ref[pl.ds(start, ROWS, stride=PITCH), :]
-                    imag_part = sums_ref[pl.ds(start + ROWS, ROWS, stride=PITCH), :]
-                    parts.append(jnp.concatenate([real_part, imag_part], axis=0))
-                if group == 0:
-                    parts[0] = parts[0] + line
-                for k, tile in enumerate(packed_four(parts)):
-                    at = (group * 3 + k) * HALF
-                    out_ref[peer, :, at : at + HALF] = tile.astype(BF16)
+            parts = []
+            for row in range(ROWS):
+                start = peer * 2 * ROWS + row
+                real_part = sums_ref[pl.ds(start, ROWS, stride=PITCH), :]
+                imag_part = sums_ref[pl.ds(start + ROWS, ROWS, stride=PITCH), :]
+                parts.append(jnp.concatenate([real_part, imag_part], axis=0))
+            parts[0] = parts[0] + line
+            for k, block in enumerate(packed(parts)):
+                at = 2 * ROWS * k
+                out_ref[peer, at : at + block.shape[0], :] = block.astype(BF16)
         return carry
 
     lax.fori_loop(0, PEERS // SENDS, some_peers, 0)
@@ -285,10 +295,14 @@
             load.wait()
 
 
-def tendency(came_ref, table_ref, group):
-    at = group * GROUP * KEPT
-    packed = dot(table_ref[...], came_ref[:, :, at : at + GROUP * KEPT].reshape(2 * N, GROUP * KEPT))
-    return [(part[:N], part[N:]) for part in unpacked_four(packed)]
+def tendency(came_ref, table_ref):
+    count = 2 * ROWS
+    blocks = [came_ref[:, k * count : (k + 1) * count, :] for k in range(BLOCKS)]
+    last = came_ref[:, BLOCKS * count :, :].astype(F32)
+    blocks.append(jnp.concatenate([last, pltpu.roll(last, HALF // 2, 2)], axis=1).astype(BF16))
+    sums = dot(table_ref[...], jnp.concatenate([block.reshape(2 * N, HALF) for block in blocks], axis=1))
+    parts = unpacked([sums[:, k * HALF : (k + 1) * HALF] for k in range(BLOCKS + 1)])
+    return [(part[:N], part[N:]) for part in parts]
 
 
 def middle_kernel(
@@ -306,12 +320,11 @@
     deriv_ref,
 ):
     shape = (PEERS, 2 * ROWS, HALF)
-    found = jnp.where(iota(shape, 1) == 0, came_ref[:, :, :HALF].astype(F32), 0.0)
-    lane = iota(shape, 2)
+    found = jnp.where(iota(shape, 2) == LIMIT, came_ref[:, : 2 * ROWS, :].astype(F32), 0.0)
+    piece_row = iota(shape, 1)
 
     def piece(which):
-        low = LIMIT + 3 * which
-        inside = jnp.where((lane >= low) & (lane < low + 3), found, 0.0)
+        inside = jnp.where((piece_row >= 3 * which) & (piece_row < 3 * which + 3), found, 0.0)
         return jnp.sum(jnp.sum(inside, axis=1), axis=1, keepdims=True)
 
     def spread(value):
@@ -325,36 +338,30 @@
     kappa_ref[0] = jnp.max(found)
     kappa = found[0:1, :]
     bound = (bound_ref[0] * bound_ref[0]).astype(F32)
-    for group in range(ROWS // GROUP):
-        parts = tendency(came_ref, z_fwd_ref, group)
-        for pos, (sum_real, sum_imag) in enumerate(parts):
-            local = group * GROUP + pos
-            kz_wave, ksquare = waves_of(local)
-            factor = jnp.exp(-kappa * ksquare * STEP)
-            inside = ksquare <= bound
-            first = [jnp.where(inside, -part, 0.0) for part in (sum_real, sum_imag)]
-            middle = []
-            for part in (0, 1):
-                start = state_ref[part, local]
-                middle.append(factor * (start + STEP * first[part]))
-                kept_ref[part, local] = factor * start + (0.5 * STEP) * (factor * first[part])
-            z_inverse(local, z_rows(*middle, kz_wave), z_inv_ref, whole_ref, deriv_ref)
+    for local, (sum_real, sum_imag) in enumerate(tendency(came_ref, z_fwd_ref)):
+        kz_wave, ksquare = waves_of(local)
+        factor = jnp.exp(-kappa * ksquare * STEP)
+        inside = ksquare <= bound
+        first = [jnp.where(inside, -part, 0.0) for part in (sum_real, sum_imag)]
+        middle = []
+        for part in (0, 1):
+            start = state_ref[part, local]
+            middle.append(factor * (start + STEP * first[part]))
+            kept_ref[part, local] = factor * start + (0.5 * STEP) * (factor * first[part])
+        z_inverse(local, z_rows(*middle, kz_wave), z_inv_ref, whole_ref, deriv_ref)
     send_planes(0, PEERS, out_ref, whole_ref, deriv_ref)
 
 
 def final_kernel(bound_ref, came_ref, kept_ref, z_fwd_ref, out_hbm, out_ref, out_sems):
     bound = (bound_ref[0] * bound_ref[0]).astype(F32)
     saves = []
-    for group in range(ROWS // GROUP):
-        parts = tendency(came_ref, z_fwd_ref, group)
-        for pos, sums in enumerate(parts):
-            local = group * GROUP + pos
-            _, ksquare = waves_of(local)
-            for part in (0, 1):
-                second = jnp.where(ksquare <= bound, -sums[part], 0.0)
-                out_ref[part, local] = kept_ref[part, local] + (0.5 * STEP) * second
-            saves.append(copy_of(out_ref.at[:, local], out_hbm.at[:, local], out_sems.at[local]))
-            saves[-1].start()
+    for local, sums in enumerate(tendency(came_ref, z_fwd_ref)):
+        _, ksquare = waves_of(local)
+        for part in (0, 1):
+            second = jnp.where(ksquare <= bound, -sums[part], 0.0)
+            out_ref[part, local] = kept_ref[part, local] + (0.5 * STEP) * second
+        saves.append(copy_of(out_ref.at[:, local], out_hbm.at[:, local], out_sems.at[local]))
+        saves[-1].start()
     for save in saves:
         save.wait()
 
@@ -363,12 +370,12 @@
 NEAR = pl.BlockSpec(memory_space=pltpu.VMEM)
 FAR = pl.BlockSpec(memory_space=pltpu.HBM)
 PLANES = (PEERS, ROWS, 2 * ROWS, N)
-SENT = (PEERS, 2 * ROWS, PACKED)
+SENT = (PEERS, 2 * ROWS * KEPT * ROWS // HALF, HALF)
 STATE = (2, ROWS, N, HALF)
 PAIR = 4
 CHUNK = 8
-UNROLL = 2
-SENDS = 4
+UNROLL = 4
+SENDS = 32
 
 
 def params(mebibytes):

time: 192 us -> 189 us (0.984)
  blocking collectives: 108 us -> 105 us
    all_to_all x3, blocking collectives: 108 us -> 105 us  [exchanged(): return lax.all_to_all(x, 'fft', 0, 0, tiled=True)]
  transfers between devices with their start and end apart: 10 -> 10, of which waited for: 5 -> 5; matrix products, arithmetic and copies ran while one was open for 3% -> 4% of each run, Pallas kernels for 0% -> 0%
where the time goes in v6:
time: 189 us; the launch traced here: 188 us
  blocking collectives  105 us (56%)
  waiting for transfers between devices  26.2 us (14%)
  starting transfers between devices  26.1 us (14%)
  Pallas kernels  21.1 us (11%)
  local copies, waits for them, and re-layouts  6.61 us (3%)
  between operations  2.33 us (1%)
    all_to_all x3, blocking collectives, exchanged(): return lax.all_to_all(x, 'fft', 0, 0, tiled=True)  105 us
    ppermute x9, waiting for transfers between devices, moved(): return lax.ppermute(x, 'scal', [(s, change(s)) for s in range(groups)])  20.8 us
    ppermute x9, starting transfers between devices, moved(): return lax.ppermute(x, 'scal', [(s, change(s)) for s in range(groups)])  15 us
    all_to_all x1, starting transfers between devices, exchanged(): return lax.all_to_all(x, 'fft', 0, 0, tiled=True)  11.1 us
    pallas_call x2, Pallas kernels, grid_call(): pl.pallas_call(grid_kernel, in_specs=[(SCALARS,) * len(scalars), spec, NE...  10.5 us
    all_to_all x1, waiting for transfers between devices, exchanged(): return lax.all_to_all(x, 'fft', 0, 0, tiled=True)  5.42 us
    pallas_call x1, Pallas kernels, start_call(): pl.pallas_call(start_kernel, in_specs=[FAR, FAR], out_specs=[FAR, NEAR],...  4.87 us
  transfers between devices with their start and end apart: 10, of which 5 were waited for; matrix products, arithmetic and copies ran while one was open for 4% of the time, Pallas kernels for 0%

profile of v6, /device:TPU:1, one launch (start us, length us, event | category | flops | bytes accessed | tf_op | source)
XLA Modules:
  0.0 187.8 jit_solution(11308789223724891153)
XLA Ops:
  0.6 0.0 copy-start.1
  0.6 4.9 %start.1 = (bf16[32,8,16,256]{3,2,1,0:T(8,128)(2,1)}, f32[2,8,128]{2,1,0:T(8,128)S(1)}) custom-call(f32[2,8,256,128]{3,2,1,0:T(8,128)} %bitcast.12, bf16[2,256,256]{2,1,0:T(8,128)(2,1)} %constant.85.table_hbm.held_5_), custom_call_target="tpu_custom_call" | custom-call | tf_op jit(solution)/shard_map/start/pallas_call | solution.py:449
  5.5 11.1 %all-to-all-start = ((bf16[32,8,16,256]{3,2,1,0:T(8,128)(2,1)}), bf16[32,8,16,256]{3,2,1,0:T(8,128)(2,1)}, u32[]{:S(2)}, u32[]{:S(2)}) async-start(bf16[32,8,16,256]{3,2,1,0:T(8,128)(2,1)} %get-tuple-element.15), calls=%async_computation | async-start | bytes 4194304 | tf_op jit(solution)/shard_map/all_to_all | solution.py:445
  16.6 0.0 copy-done.1
  16.6 0.2 reshape.10
  16.8 0.8 copy.17
  17.6 2.7 %collective-permute-start.1 = (bf16[3,8,2,16,256]{4,3,2,1,0:T(8,128)(2,1)}, bf16[3,8,2,16,256]{4,3,2,1,0:T(8,128)(2,1)}, u32[]{:S(2)}, u32[]{:S(2)}) collective-permute-start(bf16[3,8,2,16,256]{4,3,2,1,0:T(8,128)(2,1)} %bitcast.9), channel_id=1, source_target_pairs={{0,3},{1,0},{2,1},{3,2},{4,7},{5,4},{6,5},{7,6},{8,11},{9,8},{10,9... | collective-permute-start | bytes 1179656 | tf_op jit(solution)/shard_map/ppermute | solution.py:418
  20.4 0.0 collective-permute-start
  20.4 2.5 %collective-permute-start.4 = (bf16[3,8,2,16,256]{4,3,2,1,0:T(8,128)(2,1)}, bf16[3,8,2,16,256]{4,3,2,1,0:T(8,128)(2,1)}, u32[]{:S(2)}, u32[]{:S(2)}) collective-permute-start(bf16[3,8,2,16,256]{4,3,2,1,0:T(8,128)(2,1)} %bitcast.9), channel_id=1, source_target_pairs={{0,4},{1,5},{2,6},{3,7},{4,0},{5,1},{6,2},{7,3},{8,12},{9,13},{10,... | collective-permute-start | bytes 1179656 | tf_op jit(solution)/shard_map/ppermute | solution.py:418
  24.1 0.4 broadcast_in_dim.6
  24.5 0.1 constant_dynamic-update-slice_fusion.9
  24.6 4.3 %collective-permute-done.1 = bf16[3,8,2,16,256]{4,3,2,1,0:T(8,128)(2,1)} collective-permute-done((bf16[3,8,2,16,256]{4,3,2,1,0:T(8,128)(2,1)}, bf16[3,8,2,16,256]{4,3,2,1,0:T(8,128)(2,1)}, u32[]{:S(2)}, u32[]{:S(2)}) %collective-permute-start.1) | collective-permute-done | bytes 393248 | tf_op jit(solution)/shard_map/ppermute | solution.py:418
  28.8 0.9 slice.17
  29.8 3.5 %collective-permute-start.3 = (bf16[3,4,2,16,256]{4,3,2,1,0:T(8,128)(2,1)S(1)}, bf16[3,4,2,16,256]{4,3,2,1,0:T(8,128)(2,1)S(1)}, u32[]{:S(2)}, u32[]{:S(2)}) collective-permute-start(bf16[3,4,2,16,256]{4,3,2,1,0:T(8,128)(2,1)S(1)} %slice.17), channel_id=1, source_target_pairs={{0,3},{1,0},{2,1},{3,2},{4,7},{5,4},{6,5},{7,6},{8,11},{9,8},{10,9... | collective-permute-start | bytes 589832 | tf_op jit(solution)/shard_map/ppermute | solution.py:418
  33.3 0.0 collective-permute-done
  33.3 0.9 slice.16
  34.2 0.0 copy-start
  34.2 0.1 collective-permute-start.2
  34.3 5.5 %collective-permute-done.4 = bf16[3,8,2,16,256]{4,3,2,1,0:T(8,128)(2,1)} collective-permute-done((bf16[3,8,2,16,256]{4,3,2,1,0:T(8,128)(2,1)}, bf16[3,8,2,16,256]{4,3,2,1,0:T(8,128)(2,1)}, u32[]{:S(2)}, u32[]{:S(2)}) %collective-permute-start.4) | collective-permute-done | bytes 393248 | tf_op jit(solution)/shard_map/ppermute | solution.py:418
  39.8 2.7 %collective-permute-start.6 = (bf16[3,8,2,16,256]{4,3,2,1,0:T(8,128)(2,1)}, bf16[3,8,2,16,256]{4,3,2,1,0:T(8,128)(2,1)S(1)}, u32[]{:S(2)}, u32[]{:S(2)}) collective-permute-start(bf16[3,8,2,16,256]{4,3,2,1,0:T(8,128)(2,1)} %collective-permute-done.4), channel_id=1, source_target_pairs={{0,3},{1,0},{2,1},{3,2},{4,7},{5,4},{6,5},{7,6},{8,11},{9,8},{10,9... | collective-permute-start | bytes 1179656 | tf_op jit(solution)/shard_map/ppermute | solution.py:418
  42.5 0.0 collective-permute-start.5
  42.5 1.0 constant_dynamic-update-slice_fusion.8
  43.5 1.0 constant_dynamic-update-slice_fusion.7
  44.6 0.0 collective-permute-done.2
  44.6 0.0 collective-permute-done.3
  44.7 1.0 constant_dynamic-update-slice_fusion.4
  45.7 5.0 %collective-permute-done.6 = bf16[3,8,2,16,256]{4,3,2,1,0:T(8,128)(2,1)S(1)} collective-permute-done((bf16[3,8,2,16,256]{4,3,2,1,0:T(8,128)(2,1)}, bf16[3,8,2,16,256]{4,3,2,1,0:T(8,128)(2,1)S(1)}, u32[]{:S(2)}, u32[]{:S(2)}) %collective-permute-start.6) | collective-permute-done | bytes 393248 | tf_op jit(solution)/shard_map/ppermute | solution.py:418
  50.7 3.5 %collective-permute-start.8 = (bf16[3,4,2,16,256]{4,3,2,1,0:T(8,128)(2,1)S(1)}, bf16[3,4,2,16,256]{4,3,2,1,0:T(8,128)(2,1)S(1)}, u32[]{:S(2)}, u32[]{:S(2)}) collective-permute-start(bf16[3,4,2,16,256]{4,3,2,1,0:T(8,128)(2,1)S(1)} %slice.19), channel_id=1, source_target_pairs={{0,3},{1,0},{2,1},{3,2},{4,7},{5,4},{6,5},{7,6},{8,11},{9,8},{10,9... | collective-permute-start | bytes 589832 | tf_op jit(solution)/shard_map/ppermute | solution.py:418
  54.2 0.0 collective-permute-done.5
  54.2 0.1 collective-permute-start.7
  54.4 6.0 %collective-permute-done.7 = bf16[3,4,2,16,256]{4,3,2,1,0:T(8,128)(2,1)S(1)} collective-permute-done((bf16[3,4,2,16,256]{4,3,2,1,0:T(8,128)(2,1)S(1)}, bf16[3,4,2,16,256]{4,3,2,1,0:T(8,128)(2,1)S(1)}, u32[]{:S(2)}, u32[]{:S(2)}) %collective-permute-start.7) | collective-permute-done | bytes 196640 | tf_op jit(solution)/shard_map/ppermute | solution.py:418
  60.5 0.0 collective-permute-done.8
  60.5 5.4 %all-to-all-done.planes_hbm = bf16[32,8,16,256]{3,2,1,0:T(8,128)(2,1)} async-done(((bf16[32,8,16,256]{3,2,1,0:T(8,128)(2,1)}), bf16[32,8,16,256]{3,2,1,0:T(8,128)(2,1)}, u32[]{:S(2)}, u32[]{:S(2)}) %all-to-all-start) | async-done | bytes 2097184 | tf_op jit(solution)/shard_map/all_to_all | solution.py:445
  65.9 0.0 copy-done
  65.9 6.2 %grid.2 = (bf16[32,88,128]{2,1,0:T(8,128)(2,1)S(1)}, bf16[2,256,256]{2,1,0:T(8,128)(2,1)S(1)}, bf16[256,256]{1,0:T(8,128)(2,1)S(1)}, bf16[256,256]{1,0:T(8,128)(...) custom-call(s32[1]{0:T(128)S(6)} %copy.29.scalars_0_.bound_ref, ...), custom_call_target="tpu_custom_call" | custom-call | tf_op jit(solution)/shard_map/grid/pallas_call | solution.py:466
  72.2 25.5 %all_to_all.20.came_ref = bf16[32,88,128]{2,1,0:T(8,128)(2,1)S(1)} all-to-all(bf16[32,88,128]{2,1,0:T(8,128)(2,1)S(1)} %get-tuple-element.17), channel_id=1, replica_groups=mesh['fft'=32,'scal'=8] {'fft'}, dimensions={0} | all-to-all | bytes 1441792 | tf_op jit(solution)/shard_map/all_to_all | solution.py:445
  97.7 3.5 %middle.1 = (bf16[32,8,16,256]{3,2,1,0:T(8,128)(2,1)S(1)}, f32[2,8,256,128]{3,2,1,0:T(8,128)S(1)}, f32[1]{0:T(128)}) custom-call(s32[1]{0:T(128)S(6)} %copy.29.scalars_0_.bound_ref, s32[1]{0:T(128)S(6)} %copy.28.scalars_1_.species_ref, f32[64]{0:T(128)S(1)} %copy-done, bf16[32,88,128]{2,1,0:T(8,128)(2,1)S(1)} %all_to_all.20.came_ref, ...), custom_call_target="tpu_custom_call" | custom-call | tf_op jit(solution)/shard_map/middle/pallas_call | solution.py:478
  101.2 54.1 %all_to_all.21.planes_hbm = bf16[32,8,16,256]{3,2,1,0:T(8,128)(2,1)S(1)} all-to-all(bf16[32,8,16,256]{3,2,1,0:T(8,128)(2,1)S(1)} %get-tuple-element.21), channel_id=1, replica_groups=mesh['fft'=32,'scal'=8] {'fft'}, dimensions={0} | all-to-all | bytes 4194304 | tf_op jit(solution)/shard_map/all_to_all | solution.py:445
  155.3 4.2 %grid.3 = bf16[32,88,128]{2,1,0:T(8,128)(2,1)S(1)} custom-call(bf16[32,8,16,256]{3,2,1,0:T(8,128)(2,1)S(1)} %all_to_all.21.planes_hbm, bf16[3,8,256,256]{3,2,1,0:T(8,128)(2,1)S(1)} %bitcast.11, f32[2,8,128]{2,1,0:T(8,128)S(1)} %get-tuple-element.16.stats_ref, bf16[2,256,256]{2,1,0:T(8,128)(2,1)S(1)} %get-tuple-element.22.held_0_, ...), custom_call_target="tpu_custom_call" | custom-call | tf_op jit(solution)/shard_map/grid/pallas_call | solution.py:466
  159.6 25.8 %all_to_all.22.came_ref = bf16[32,88,128]{2,1,0:T(8,128)(2,1)S(1)} all-to-all(bf16[32,88,128]{2,1,0:T(8,128)(2,1)S(1)} %grid.3), channel_id=1, replica_groups=mesh['fft'=32,'scal'=8] {'fft'}, dimensions={0} | all-to-all | bytes 1441792 | tf_op jit(solution)/shard_map/all_to_all | solution.py:445
  185.4 2.2 %final.1 = f32[2,8,256,128]{3,2,1,0:T(8,128)} custom-call(s32[1]{0:T(128)S(6)} %copy.29.scalars_0_.bound_ref, bf16[32,88,128]{2,1,0:T(8,128)(2,1)S(1)} %all_to_all.22.came_ref, f32[2,8,256,128]{3,2,1,0:T(8,128)S(1)} %get-tuple-element.26.kept_ref, bf16[512,512]{1,0:T(8,128)(2,1)S(1)} %get-tuple-element.19.z_fwd_ref), custom_call_target="tpu_custom_call" | custom-call | tf_op jit(solution)/shard_map/final/pallas_call | solution.py:490
  (8 shorter events, 0.2 us)
Async XLA Ops:
  0.6 16.0 %copy-start.1 = (bf16[3,8,32,256]{3,2,1,0:T(8,128)(2,1)S(1)}, bf16[3,8,32,256]{3,2,1,0:T(8,128)(2,1)}, u32[]{:S(2)}) copy-start(bf16[3,8,32,256]{3,2,1,0:T(8,128)(2,1)} %param.12) | copy-start | bytes 1179652
  5.5 60.4 %all-to-all-start = ((bf16[32,8,16,256]{3,2,1,0:T(8,128)(2,1)}), bf16[32,8,16,256]{3,2,1,0:T(8,128)(2,1)}, u32[]{:S(2)}, u32[]{:S(2)}) async-start(bf16[32,8,16,256]{3,2,1,0:T(8,128)(2,1)} %get-tuple-element.15), calls=%async_computation | async-start | bytes 4194304 | tf_op jit(solution)/shard_map/all_to_all | solution.py:445
  17.6 11.2 %collective-permute-start.1 = (bf16[3,8,2,16,256]{4,3,2,1,0:T(8,128)(2,1)}, bf16[3,8,2,16,256]{4,3,2,1,0:T(8,128)(2,1)}, u32[]{:S(2)}, u32[]{:S(2)}) collective-permute-start(bf16[3,8,2,16,256]{4,3,2,1,0:T(8,128)(2,1)} %bitcast.9), channel_id=1, source_target_pairs={{0,3},{1,0},{2,1},{3,2},{4,7},{5,4},{6,5},{7,6},{8,11},{9,8},{10,9... | collective-permute-start | bytes 1179656 | tf_op jit(solution)/shard_map/ppermute | solution.py:418
  20.4 12.9 %collective-permute-start = (bf16[3,8,2,16,256]{4,3,2,1,0:T(8,128)(2,1)}, bf16[3,8,2,16,256]{4,3,2,1,0:T(8,128)(2,1)}, u32[]{:S(2)}, u32[]{:S(2)}) collective-permute-start(bf16[3,8,2,16,256]{4,3,2,1,0:T(8,128)(2,1)} %bitcast.9), channel_id=1, source_target_pairs={{0,1},{1,2},{2,3},{3,0},{4,5},{5,6},{6,7},{7,4},{8,9},{9,10},{10,1... | collective-permute-start | bytes 1179656 | tf_op jit(solution)/shard_map/ppermute | solution.py:418
  20.4 19.5 %collective-permute-start.4 = (bf16[3,8,2,16,256]{4,3,2,1,0:T(8,128)(2,1)}, bf16[3,8,2,16,256]{4,3,2,1,0:T(8,128)(2,1)}, u32[]{:S(2)}, u32[]{:S(2)}) collective-permute-start(bf16[3,8,2,16,256]{4,3,2,1,0:T(8,128)(2,1)} %bitcast.9), channel_id=1, source_target_pairs={{0,4},{1,5},{2,6},{3,7},{4,0},{5,1},{6,2},{7,3},{8,12},{9,13},{10,... | collective-permute-start | bytes 1179656 | tf_op jit(solution)/shard_map/ppermute | solution.py:418
  29.8 14.8 %collective-permute-start.3 = (bf16[3,4,2,16,256]{4,3,2,1,0:T(8,128)(2,1)S(1)}, bf16[3,4,2,16,256]{4,3,2,1,0:T(8,128)(2,1)S(1)}, u32[]{:S(2)}, u32[]{:S(2)}) collective-permute-start(bf16[3,4,2,16,256]{4,3,2,1,0:T(8,128)(2,1)S(1)} %slice.17), channel_id=1, source_target_pairs={{0,3},{1,0},{2,1},{3,2},{4,7},{5,4},{6,5},{7,6},{8,11},{9,8},{10,9... | collective-permute-start | bytes 589832 | tf_op jit(solution)/shard_map/ppermute | solution.py:418
  34.2 31.7 %copy-start = (f32[64]{0:T(128)S(1)}, f32[64]{0:T(128)}, u32[]{:S(2)}) copy-start(f32[64]{0:T(128)} %base_ref.1) | copy-start | bytes 772
  34.2 10.4 %collective-permute-start.2 = (bf16[3,4,2,16,256]{4,3,2,1,0:T(8,128)(2,1)S(1)}, bf16[3,4,2,16,256]{4,3,2,1,0:T(8,128)(2,1)S(1)}, u32[]{:S(2)}, u32[]{:S(2)}) collective-permute-start(bf16[3,4,2,16,256]{4,3,2,1,0:T(8,128)(2,1)S(1)} %slice.16), channel_id=1, source_target_pairs={{0,1},{1,2},{2,3},{3,0},{4,5},{5,6},{6,7},{7,4},{8,9},{9,10},{10,1... | collective-permute-start | bytes 589832 | tf_op jit(solution)/shard_map/ppermute | solution.py:418
  39.8 10.9 %collective-permute-start.6 = (bf16[3,8,2,16,256]{4,3,2,1,0:T(8,128)(2,1)}, bf16[3,8,2,16,256]{4,3,2,1,0:T(8,128)(2,1)S(1)}, u32[]{:S(2)}, u32[]{:S(2)}) collective-permute-start(bf16[3,8,2,16,256]{4,3,2,1,0:T(8,128)(2,1)} %collective-permute-done.4), channel_id=1, source_target_pairs={{0,3},{1,0},{2,1},{3,2},{4,7},{5,4},{6,5},{7,6},{8,11},{9,8},{10,9... | collective-permute-start | bytes 1179656 | tf_op jit(solution)/shard_map/ppermute | solution.py:418
  42.5 11.7 %collective-permute-start.5 = (bf16[3,8,2,16,256]{4,3,2,1,0:T(8,128)(2,1)}, bf16[3,8,2,16,256]{4,3,2,1,0:T(8,128)(2,1)S(1)}, u32[]{:S(2)}, u32[]{:S(2)}) collective-permute-start(bf16[3,8,2,16,256]{4,3,2,1,0:T(8,128)(2,1)} %collective-permute-done.4), channel_id=1, source_target_pairs={{0,1},{1,2},{2,3},{3,0},{4,5},{5,6},{6,7},{7,4},{8,9},{9,10},{10,1... | collective-permute-start | bytes 1179656 | tf_op jit(solution)/shard_map/ppermute | solution.py:418
  50.7 9.8 %collective-permute-start.8 = (bf16[3,4,2,16,256]{4,3,2,1,0:T(8,128)(2,1)S(1)}, bf16[3,4,2,16,256]{4,3,2,1,0:T(8,128)(2,1)S(1)}, u32[]{:S(2)}, u32[]{:S(2)}) collective-permute-start(bf16[3,4,2,16,256]{4,3,2,1,0:T(8,128)(2,1)S(1)} %slice.19), channel_id=1, source_target_pairs={{0,3},{1,0},{2,1},{3,2},{4,7},{5,4},{6,5},{7,6},{8,11},{9,8},{10,9... | collective-permute-start | bytes 589832 | tf_op jit(solution)/shard_map/ppermute | solution.py:418
  54.2 6.2 %collective-permute-start.7 = (bf16[3,4,2,16,256]{4,3,2,1,0:T(8,128)(2,1)S(1)}, bf16[3,4,2,16,256]{4,3,2,1,0:T(8,128)(2,1)S(1)}, u32[]{:S(2)}, u32[]{:S(2)}) collective-permute-start(bf16[3,4,2,16,256]{4,3,2,1,0:T(8,128)(2,1)S(1)} %slice.18), channel_id=1, source_target_pairs={{0,1},{1,2},{2,3},{3,0},{4,5},{5,6},{6,7},{7,4},{8,9},{9,10},{10,1... | collective-permute-start | bytes 589832 | tf_op jit(solution)/shard_map/ppermute | solution.py:418

commit v7 on v6

--- a/solution.py
+++ b/solution.py
@@ -50,7 +50,7 @@
         "x_inv": np.concatenate([-weight * sin.T, -weight * cos.T], axis=0),
         "x_fwd": np.concatenate([cos * keep, -sin * keep], axis=1),
         "y_fwd": np.stack([forward(low, 2 * low + turn)[halves] for turn in (0, 1)]),
-        "z_fwd": forward(index, index)[:, order(PEERS)],
+        "z_fwd": forward(np.concatenate([index[:KEPT], index[-KEPT:]]), index)[:, order(PEERS)],
     }
     return {name: jnp.asarray(value.astype(np.float32)).astype(BF16) for name, value in listed.items()}
 
@@ -183,7 +183,7 @@
 
 
 def unpacked(blocks):
-    lane = iota((2 * N, HALF), 1)
+    lane = iota(blocks[0].shape, 1)
     parts = []
     for row in range(ROWS):
         block, shift = place_of(row)
@@ -221,15 +221,15 @@
     ky_wave = signed(row // (2 * ROWS) * ROWS + row % ROWS).astype(BF16)
     kx_wave = iota((HALF, HALF), 1).astype(F32)
 
-    def one_pair(step, carry):
+    def one_pair(step):
         if apart:
             for k in range(PAIR):
                 came_plane(step * PAIR + k).wait()
-            for load in loads[:4]:
-                pl.when(step == 0)(load.wait)
         came = [planes_ref[:, step * PAIR + k].reshape(count, N) for k in range(PAIR)]
         scaled = [ky_wave * part[:, :HALF] for part in came]
         pairs = both_turns(jnp.concatenate(came + scaled, axis=1))
+        if apart and step == 0:
+            loads[0].wait()
         y_section = [dot(y_inv_ref[turn], pairs[turn]) for turn in (0, 1)]
         x_rows = []
         for k in range(PAIR):
@@ -240,6 +240,9 @@
                     if which == 0:
                         halves = [kx_wave * half for half in halves]
                     x_rows.append(jnp.concatenate(halves, axis=1).astype(BF16))
+        if apart and step == 0:
+            for load in loads[1:4]:
+                load.wait()
         gradients = dot(jnp.concatenate(x_rows, axis=0), x_inv_ref[...])
         fields = []
         for k in range(PAIR):
@@ -262,9 +265,9 @@
             even, odd = (found[:, k * HALF : (k + 1) * HALF] for found in sums)
             sums_ref[pl.ds(row_of(step * PAIR + k), N), :] = even + odd
             sums_ref[pl.ds(row_of(step * PAIR + k, N), N), :] = even - odd
-        return carry
-
-    lax.fori_loop(0, ROWS // PAIR, one_pair, 0)
+
+    for step in range(ROWS // PAIR):
+        one_pair(step)
     shape = (2 * ROWS, HALF)
     peak = jnp.sqrt(jnp.max(peak_ref[...], keepdims=True))
     pieces = []
@@ -302,7 +305,9 @@
     blocks.append(jnp.concatenate([last, pltpu.roll(last, HALF // 2, 2)], axis=1).astype(BF16))
     sums = dot(table_ref[...], jnp.concatenate([block.reshape(2 * N, HALF) for block in blocks], axis=1))
     parts = unpacked([sums[:, k * HALF : (k + 1) * HALF] for k in range(BLOCKS + 1)])
-    return [(part[:N], part[N:]) for part in parts]
+    between = jnp.zeros((N - 2 * KEPT, HALF), F32)
+    cut = [[part[k * KEPT : (k + 1) * KEPT] for k in range(4)] for part in parts]
+    return [tuple(jnp.concatenate([c[k], between, c[k + 1]], axis=0) for k in (0, 2)) for c in cut]
 
 
 def middle_kernel(

time: 189 us -> 188 us (level)
  no operation moved by 1% of the time
where the time goes in v7:
time: 188 us; the launch traced here: 187 us
  blocking collectives  105 us (56%)
  starting transfers between devices  26.3 us (14%)
  waiting for transfers between devices  26 us (14%)
  Pallas kernels  20.4 us (11%)
  local copies, waits for them, and re-layouts  6.61 us (4%)
  between operations  2.32 us (1%)
    all_to_all x3, blocking collectives, exchanged(): return lax.all_to_all(x, 'fft', 0, 0, tiled=True)  105 us
    ppermute x9, waiting for transfers between devices, moved(): return lax.ppermute(x, 'scal', [(s, change(s)) for s in range(groups)])  20.8 us
    ppermute x9, starting transfers between devices, moved(): return lax.ppermute(x, 'scal', [(s, change(s)) for s in range(groups)])  15.2 us
    all_to_all x1, starting transfers between devices, exchanged(): return lax.all_to_all(x, 'fft', 0, 0, tiled=True)  11.1 us
    pallas_call x2, Pallas kernels, grid_call(): pl.pallas_call(grid_kernel, in_specs=[(SCALARS,) * len(scalars), spec, NE...  10.1 us
    all_to_all x1, waiting for transfers between devices, exchanged(): return lax.all_to_all(x, 'fft', 0, 0, tiled=True)  5.24 us
    pallas_call x1, Pallas kernels, start_call(): pl.pallas_call(start_kernel, in_specs=[FAR, FAR], out_specs=[FAR, NEAR],...  4.87 us
  transfers between devices with their start and end apart: 10, of which 5 were waited for; matrix products, arithmetic and copies ran while one was open for 4% of the time, Pallas kernels for 0%

profile of v7, /device:TPU:1, one launch (start us, length us, event | category | flops | bytes accessed | tf_op | source)
XLA Modules:
  0.0 187.0 jit_solution(3331626915961225384)
XLA Ops:
  0.6 0.0 copy-start.1
  0.6 4.9 %start.1 = (bf16[32,8,16,256]{3,2,1,0:T(8,128)(2,1)}, f32[2,8,128]{2,1,0:T(8,128)S(1)}) custom-call(f32[2,8,256,128]{3,2,1,0:T(8,128)} %bitcast.12, bf16[2,256,256]{2,1,0:T(8,128)(2,1)} %constant.85.table_hbm.held_5_), custom_call_target="tpu_custom_call" | custom-call | tf_op jit(solution)/shard_map/start/pallas_call | solution.py:454
  5.5 11.1 %all-to-all-start = ((bf16[32,8,16,256]{3,2,1,0:T(8,128)(2,1)}), bf16[32,8,16,256]{3,2,1,0:T(8,128)(2,1)}, u32[]{:S(2)}, u32[]{:S(2)}) async-start(bf16[32,8,16,256]{3,2,1,0:T(8,128)(2,1)} %get-tuple-element.15), calls=%async_computation | async-start | bytes 4194304 | tf_op jit(solution)/shard_map/all_to_all | solution.py:450
  16.6 0.0 copy-done.1
  16.6 0.2 reshape.10
  16.8 0.8 copy.17
  17.6 2.7 %collective-permute-start.1 = (bf16[3,8,2,16,256]{4,3,2,1,0:T(8,128)(2,1)}, bf16[3,8,2,16,256]{4,3,2,1,0:T(8,128)(2,1)}, u32[]{:S(2)}, u32[]{:S(2)}) collective-permute-start(bf16[3,8,2,16,256]{4,3,2,1,0:T(8,128)(2,1)} %bitcast.9), channel_id=1, source_target_pairs={{0,3},{1,0},{2,1},{3,2},{4,7},{5,4},{6,5},{7,6},{8,11},{9,8},{10,9... | collective-permute-start | bytes 1179656 | tf_op jit(solution)/shard_map/ppermute | solution.py:423
  20.4 0.0 collective-permute-start
  20.4 2.5 %collective-permute-start.4 = (bf16[3,8,2,16,256]{4,3,2,1,0:T(8,128)(2,1)}, bf16[3,8,2,16,256]{4,3,2,1,0:T(8,128)(2,1)}, u32[]{:S(2)}, u32[]{:S(2)}) collective-permute-start(bf16[3,8,2,16,256]{4,3,2,1,0:T(8,128)(2,1)} %bitcast.9), channel_id=1, source_target_pairs={{0,4},{1,5},{2,6},{3,7},{4,0},{5,1},{6,2},{7,3},{8,12},{9,13},{10,... | collective-permute-start | bytes 1179656 | tf_op jit(solution)/shard_map/ppermute | solution.py:423
  24.1 0.4 broadcast_in_dim.6
  24.5 0.1 constant_dynamic-update-slice_fusion.9
  24.6 4.3 %collective-permute-done.1 = bf16[3,8,2,16,256]{4,3,2,1,0:T(8,128)(2,1)} collective-permute-done((bf16[3,8,2,16,256]{4,3,2,1,0:T(8,128)(2,1)}, bf16[3,8,2,16,256]{4,3,2,1,0:T(8,128)(2,1)}, u32[]{:S(2)}, u32[]{:S(2)}) %collective-permute-start.1) | collective-permute-done | bytes 393248 | tf_op jit(solution)/shard_map/ppermute | solution.py:423
  28.8 0.9 slice.17
  29.8 3.5 %collective-permute-start.3 = (bf16[3,4,2,16,256]{4,3,2,1,0:T(8,128)(2,1)S(1)}, bf16[3,4,2,16,256]{4,3,2,1,0:T(8,128)(2,1)S(1)}, u32[]{:S(2)}, u32[]{:S(2)}) collective-permute-start(bf16[3,4,2,16,256]{4,3,2,1,0:T(8,128)(2,1)S(1)} %slice.17), channel_id=1, source_target_pairs={{0,3},{1,0},{2,1},{3,2},{4,7},{5,4},{6,5},{7,6},{8,11},{9,8},{10,9... | collective-permute-start | bytes 589832 | tf_op jit(solution)/shard_map/ppermute | solution.py:423
  33.3 0.0 collective-permute-done
  33.3 0.9 slice.16
  34.2 0.0 copy-start
  34.2 0.1 collective-permute-start.2
  34.3 5.5 %collective-permute-done.4 = bf16[3,8,2,16,256]{4,3,2,1,0:T(8,128)(2,1)} collective-permute-done((bf16[3,8,2,16,256]{4,3,2,1,0:T(8,128)(2,1)}, bf16[3,8,2,16,256]{4,3,2,1,0:T(8,128)(2,1)}, u32[]{:S(2)}, u32[]{:S(2)}) %collective-permute-start.4) | collective-permute-done | bytes 393248 | tf_op jit(solution)/shard_map/ppermute | solution.py:423
  39.8 2.7 %collective-permute-start.6 = (bf16[3,8,2,16,256]{4,3,2,1,0:T(8,128)(2,1)}, bf16[3,8,2,16,256]{4,3,2,1,0:T(8,128)(2,1)S(1)}, u32[]{:S(2)}, u32[]{:S(2)}) collective-permute-start(bf16[3,8,2,16,256]{4,3,2,1,0:T(8,128)(2,1)} %collective-permute-done.4), channel_id=1, source_target_pairs={{0,3},{1,0},{2,1},{3,2},{4,7},{5,4},{6,5},{7,6},{8,11},{9,8},{10,9... | collective-permute-start | bytes 1179656 | tf_op jit(solution)/shard_map/ppermute | solution.py:423
  42.5 0.0 collective-permute-start.5
  42.5 1.0 constant_dynamic-update-slice_fusion.8
  43.5 1.0 constant_dynamic-update-slice_fusion.7
  44.6 0.0 collective-permute-done.2
  44.6 0.0 collective-permute-done.3
  44.7 1.0 constant_dynamic-update-slice_fusion.4
  45.7 5.0 %collective-permute-done.6 = bf16[3,8,2,16,256]{4,3,2,1,0:T(8,128)(2,1)S(1)} collective-permute-done((bf16[3,8,2,16,256]{4,3,2,1,0:T(8,128)(2,1)}, bf16[3,8,2,16,256]{4,3,2,1,0:T(8,128)(2,1)S(1)}, u32[]{:S(2)}, u32[]{:S(2)}) %collective-permute-start.6) | collective-permute-done | bytes 393248 | tf_op jit(solution)/shard_map/ppermute | solution.py:423
  50.7 3.5 %collective-permute-start.8 = (bf16[3,4,2,16,256]{4,3,2,1,0:T(8,128)(2,1)S(1)}, bf16[3,4,2,16,256]{4,3,2,1,0:T(8,128)(2,1)S(1)}, u32[]{:S(2)}, u32[]{:S(2)}) collective-permute-start(bf16[3,4,2,16,256]{4,3,2,1,0:T(8,128)(2,1)S(1)} %slice.19), channel_id=1, source_target_pairs={{0,3},{1,0},{2,1},{3,2},{4,7},{5,4},{6,5},{7,6},{8,11},{9,8},{10,9... | collective-permute-start | bytes 589832 | tf_op jit(solution)/shard_map/ppermute | solution.py:423
  54.2 0.0 collective-permute-done.5
  54.2 0.3 collective-permute-start.7
  54.6 6.0 %collective-permute-done.7 = bf16[3,4,2,16,256]{4,3,2,1,0:T(8,128)(2,1)S(1)} collective-permute-done((bf16[3,4,2,16,256]{4,3,2,1,0:T(8,128)(2,1)S(1)}, bf16[3,4,2,16,256]{4,3,2,1,0:T(8,128)(2,1)S(1)}, u32[]{:S(2)}, u32[]{:S(2)}) %collective-permute-start.7) | collective-permute-done | bytes 196640 | tf_op jit(solution)/shard_map/ppermute | solution.py:423
  60.7 0.0 collective-permute-done.8
  60.7 5.2 %all-to-all-done.planes_hbm = bf16[32,8,16,256]{3,2,1,0:T(8,128)(2,1)} async-done(((bf16[32,8,16,256]{3,2,1,0:T(8,128)(2,1)}), bf16[32,8,16,256]{3,2,1,0:T(8,128)(2,1)}, u32[]{:S(2)}, u32[]{:S(2)}) %all-to-all-start) | async-done | bytes 2097184 | tf_op jit(solution)/shard_map/all_to_all | solution.py:450
  65.9 0.0 copy-done
  65.9 6.3 %grid.2 = (bf16[32,88,128]{2,1,0:T(8,128)(2,1)S(1)}, bf16[2,256,256]{2,1,0:T(8,128)(2,1)S(1)}, bf16[256,256]{1,0:T(8,128)(2,1)S(1)}, bf16[256,256]{1,0:T(8,128)(...) custom-call(s32[1]{0:T(128)S(6)} %copy.29.scalars_0_.bound_ref, ...), custom_call_target="tpu_custom_call" | custom-call | tf_op jit(solution)/shard_map/grid/pallas_call | solution.py:471
  72.3 25.5 %all_to_all.20.came_ref = bf16[32,88,128]{2,1,0:T(8,128)(2,1)S(1)} all-to-all(bf16[32,88,128]{2,1,0:T(8,128)(2,1)S(1)} %get-tuple-element.17), channel_id=1, replica_groups=mesh['fft'=32,'scal'=8] {'fft'}, dimensions={0} | all-to-all | bytes 1441792 | tf_op jit(solution)/shard_map/all_to_all | solution.py:450
  97.8 3.4 %middle.1 = (bf16[32,8,16,256]{3,2,1,0:T(8,128)(2,1)S(1)}, f32[2,8,256,128]{3,2,1,0:T(8,128)S(1)}, f32[1]{0:T(128)}) custom-call(s32[1]{0:T(128)S(6)} %copy.29.scalars_0_.bound_ref, s32[1]{0:T(128)S(6)} %copy.28.scalars_1_.species_ref, f32[64]{0:T(128)S(1)} %copy-done, bf16[32,88,128]{2,1,0:T(8,128)(2,1)S(1)} %all_to_all.20.came_ref, ...), custom_call_target="tpu_custom_call" | custom-call | tf_op jit(solution)/shard_map/middle/pallas_call | solution.py:483
  101.2 54.1 %all_to_all.21.planes_hbm = bf16[32,8,16,256]{3,2,1,0:T(8,128)(2,1)S(1)} all-to-all(bf16[32,8,16,256]{3,2,1,0:T(8,128)(2,1)S(1)} %get-tuple-element.21), channel_id=1, replica_groups=mesh['fft'=32,'scal'=8] {'fft'}, dimensions={0} | all-to-all | bytes 4194304 | tf_op jit(solution)/shard_map/all_to_all | solution.py:450
  155.2 3.8 %grid.3 = bf16[32,88,128]{2,1,0:T(8,128)(2,1)S(1)} custom-call(bf16[32,8,16,256]{3,2,1,0:T(8,128)(2,1)S(1)} %all_to_all.21.planes_hbm, bf16[3,8,256,256]{3,2,1,0:T(8,128)(2,1)S(1)} %bitcast.11, f32[2,8,128]{2,1,0:T(8,128)S(1)} %get-tuple-element.16.stats_ref, bf16[2,256,256]{2,1,0:T(8,128)(2,1)S(1)} %get-tuple-element.22.held_0_, ...), custom_call_target="tpu_custom_call" | custom-call | tf_op jit(solution)/shard_map/grid/pallas_call | solution.py:471
  159.1 25.8 %all_to_all.22.came_ref = bf16[32,88,128]{2,1,0:T(8,128)(2,1)S(1)} all-to-all(bf16[32,88,128]{2,1,0:T(8,128)(2,1)S(1)} %grid.3), channel_id=1, replica_groups=mesh['fft'=32,'scal'=8] {'fft'}, dimensions={0} | all-to-all | bytes 1441792 | tf_op jit(solution)/shard_map/all_to_all | solution.py:450
  184.9 2.0 %final.1 = f32[2,8,256,128]{3,2,1,0:T(8,128)} custom-call(s32[1]{0:T(128)S(6)} %copy.29.scalars_0_.bound_ref, bf16[32,88,128]{2,1,0:T(8,128)(2,1)S(1)} %all_to_all.22.came_ref, f32[2,8,256,128]{3,2,1,0:T(8,128)S(1)} %get-tuple-element.26.kept_ref, bf16[352,512]{1,0:T(8,128)(2,1)S(1)} %get-tuple-element.19.z_fwd_ref), custom_call_target="tpu_custom_call" | custom-call | tf_op jit(solution)/shard_map/final/pallas_call | solution.py:495
  (8 shorter events, 0.2 us)
Async XLA Ops:
  0.6 16.0 %copy-start.1 = (bf16[3,8,32,256]{3,2,1,0:T(8,128)(2,1)S(1)}, bf16[3,8,32,256]{3,2,1,0:T(8,128)(2,1)}, u32[]{:S(2)}) copy-start(bf16[3,8,32,256]{3,2,1,0:T(8,128)(2,1)} %param.12) | copy-start | bytes 1179652
  5.5 60.4 %all-to-all-start = ((bf16[32,8,16,256]{3,2,1,0:T(8,128)(2,1)}), bf16[32,8,16,256]{3,2,1,0:T(8,128)(2,1)}, u32[]{:S(2)}, u32[]{:S(2)}) async-start(bf16[32,8,16,256]{3,2,1,0:T(8,128)(2,1)} %get-tuple-element.15), calls=%async_computation | async-start | bytes 4194304 | tf_op jit(solution)/shard_map/all_to_all | solution.py:450
  17.6 11.2 %collective-permute-start.1 = (bf16[3,8,2,16,256]{4,3,2,1,0:T(8,128)(2,1)}, bf16[3,8,2,16,256]{4,3,2,1,0:T(8,128)(2,1)}, u32[]{:S(2)}, u32[]{:S(2)}) collective-permute-start(bf16[3,8,2,16,256]{4,3,2,1,0:T(8,128)(2,1)} %bitcast.9), channel_id=1, source_target_pairs={{0,3},{1,0},{2,1},{3,2},{4,7},{5,4},{6,5},{7,6},{8,11},{9,8},{10,9... | collective-permute-start | bytes 1179656 | tf_op jit(solution)/shard_map/ppermute | solution.py:423
  20.4 12.9 %collective-permute-start = (bf16[3,8,2,16,256]{4,3,2,1,0:T(8,128)(2,1)}, bf16[3,8,2,16,256]{4,3,2,1,0:T(8,128)(2,1)}, u32[]{:S(2)}, u32[]{:S(2)}) collective-permute-start(bf16[3,8,2,16,256]{4,3,2,1,0:T(8,128)(2,1)} %bitcast.9), channel_id=1, source_target_pairs={{0,1},{1,2},{2,3},{3,0},{4,5},{5,6},{6,7},{7,4},{8,9},{9,10},{10,1... | collective-permute-start | bytes 1179656 | tf_op jit(solution)/shard_map/ppermute | solution.py:423
  20.4 19.5 %collective-permute-start.4 = (bf16[3,8,2,16,256]{4,3,2,1,0:T(8,128)(2,1)}, bf16[3,8,2,16,256]{4,3,2,1,0:T(8,128)(2,1)}, u32[]{:S(2)}, u32[]{:S(2)}) collective-permute-start(bf16[3,8,2,16,256]{4,3,2,1,0:T(8,128)(2,1)} %bitcast.9), channel_id=1, source_target_pairs={{0,4},{1,5},{2,6},{3,7},{4,0},{5,1},{6,2},{7,3},{8,12},{9,13},{10,... | collective-permute-start | bytes 1179656 | tf_op jit(solution)/shard_map/ppermute | solution.py:423
  29.8 14.8 %collective-permute-start.3 = (bf16[3,4,2,16,256]{4,3,2,1,0:T(8,128)(2,1)S(1)}, bf16[3,4,2,16,256]{4,3,2,1,0:T(8,128)(2,1)S(1)}, u32[]{:S(2)}, u32[]{:S(2)}) collective-permute-start(bf16[3,4,2,16,256]{4,3,2,1,0:T(8,128)(2,1)S(1)} %slice.17), channel_id=1, source_target_pairs={{0,3},{1,0},{2,1},{3,2},{4,7},{5,4},{6,5},{7,6},{8,11},{9,8},{10,9... | collective-permute-start | bytes 589832 | tf_op jit(solution)/shard_map/ppermute | solution.py:423
  34.2 31.7 %copy-start = (f32[64]{0:T(128)S(1)}, f32[64]{0:T(128)}, u32[]{:S(2)}) copy-start(f32[64]{0:T(128)} %base_ref.1) | copy-start | bytes 772
  34.2 10.4 %collective-permute-start.2 = (bf16[3,4,2,16,256]{4,3,2,1,0:T(8,128)(2,1)S(1)}, bf16[3,4,2,16,256]{4,3,2,1,0:T(8,128)(2,1)S(1)}, u32[]{:S(2)}, u32[]{:S(2)}) collective-permute-start(bf16[3,4,2,16,256]{4,3,2,1,0:T(8,128)(2,1)S(1)} %slice.16), channel_id=1, source_target_pairs={{0,1},{1,2},{2,3},{3,0},{4,5},{5,6},{6,7},{7,4},{8,9},{9,10},{10,1... | collective-permute-start | bytes 589832 | tf_op jit(solution)/shard_map/ppermute | solution.py:423
  39.8 10.9 %collective-permute-start.6 = (bf16[3,8,2,16,256]{4,3,2,1,0:T(8,128)(2,1)}, bf16[3,8,2,16,256]{4,3,2,1,0:T(8,128)(2,1)S(1)}, u32[]{:S(2)}, u32[]{:S(2)}) collective-permute-start(bf16[3,8,2,16,256]{4,3,2,1,0:T(8,128)(2,1)} %collective-permute-done.4), channel_id=1, source_target_pairs={{0,3},{1,0},{2,1},{3,2},{4,7},{5,4},{6,5},{7,6},{8,11},{9,8},{10,9... | collective-permute-start | bytes 1179656 | tf_op jit(solution)/shard_map/ppermute | solution.py:423
  42.5 11.7 %collective-permute-start.5 = (bf16[3,8,2,16,256]{4,3,2,1,0:T(8,128)(2,1)}, bf16[3,8,2,16,256]{4,3,2,1,0:T(8,128)(2,1)S(1)}, u32[]{:S(2)}, u32[]{:S(2)}) collective-permute-start(bf16[3,8,2,16,256]{4,3,2,1,0:T(8,128)(2,1)} %collective-permute-done.4), channel_id=1, source_target_pairs={{0,1},{1,2},{2,3},{3,0},{4,5},{5,6},{6,7},{7,4},{8,9},{9,10},{10,1... | collective-permute-start | bytes 1179656 | tf_op jit(solution)/shard_map/ppermute | solution.py:423
  50.7 10.0 %collective-permute-start.8 = (bf16[3,4,2,16,256]{4,3,2,1,0:T(8,128)(2,1)S(1)}, bf16[3,4,2,16,256]{4,3,2,1,0:T(8,128)(2,1)S(1)}, u32[]{:S(2)}, u32[]{:S(2)}) collective-permute-start(bf16[3,4,2,16,256]{4,3,2,1,0:T(8,128)(2,1)S(1)} %slice.19), channel_id=1, source_target_pairs={{0,3},{1,0},{2,1},{3,2},{4,7},{5,4},{6,5},{7,6},{8,11},{9,8},{10,9... | collective-permute-start | bytes 589832 | tf_op jit(solution)/shard_map/ppermute | solution.py:423
  54.2 6.4 %collective-permute-start.7 = (bf16[3,4,2,16,256]{4,3,2,1,0:T(8,128)(2,1)S(1)}, bf16[3,4,2,16,256]{4,3,2,1,0:T(8,128)(2,1)S(1)}, u32[]{:S(2)}, u32[]{:S(2)}) collective-permute-start(bf16[3,4,2,16,256]{4,3,2,1,0:T(8,128)(2,1)S(1)} %slice.18), channel_id=1, source_target_pairs={{0,1},{1,2},{2,3},{3,0},{4,5},{5,6},{6,7},{7,4},{8,9},{9,10},{10,1... | collective-permute-start | bytes 589832 | tf_op jit(solution)/shard_map/ppermute | solution.py:423

commit v8 on v7

--- a/solution.py
+++ b/solution.py
@@ -80,10 +80,10 @@
     return [jnp.concatenate(pair, axis=1) for pair in zip(*columns)]
 
 
-def send_planes(first, count, planes_ref, whole_ref, deriv_ref):
+def send_planes(first, count, unroll, planes_ref, whole_ref, deriv_ref):
     def some_peers(step, carry):
-        for turn in range(UNROLL):
-            peer = first + step * UNROLL + turn
+        for turn in range(unroll):
+            peer = first + step * unroll + turn
             for local in range(ROWS):
                 for at, ref in ((0, whole_ref), (HALF, deriv_ref)):
                     start = local % 2 * N + peer * (ROWS // 2) + local // 2
@@ -93,7 +93,7 @@
                     planes_ref[peer, local, :, at : at + HALF] = tile
         return carry
 
-    lax.fori_loop(0, count // UNROLL, some_peers, 0)
+    lax.fori_loop(0, count // unroll, some_peers, 0)
 
 
 def row_of(block, shift=0):
@@ -108,11 +108,15 @@
         deriv_ref[part, :] = found[:, HALF:]
 
 
+def across_z(local):
+    ky_wave = signed(lax.axis_index("fft").astype(jnp.int32) * ROWS + local)
+    kx_wave = iota((1, HALF), 1).astype(F32)
+    return kx_wave * kx_wave + ky_wave * ky_wave
+
+
 def waves_of(local):
-    ky_wave = signed(lax.axis_index("fft").astype(jnp.int32) * ROWS + local)
     kz_wave = signed(iota((N, HALF), 0))
-    kx_wave = iota((N, HALF), 1).astype(F32)
-    return kz_wave, kx_wave * kx_wave + ky_wave * ky_wave + kz_wave * kz_wave
+    return kz_wave, across_z(local) + kz_wave * kz_wave
 
 
 def copy_of(source, target, sem):
@@ -141,14 +145,14 @@
         z_inverse(local, z_rows(real_part, imag_part, kz_wave), table_ref, whole_ref, deriv_ref)
         return carry
 
-    lax.fori_loop(0, ROWS, one_row, 0)
+    lax.fori_loop(0, ROWS, one_row, 0, unroll=2)
 
     def leaving(k):
         part = pl.ds(k * CHUNK, CHUNK)
         return copy_of(planes_ref.at[part], out_hbm.at[part], out_sems.at[k])
 
     def one_chunk(k, carry):
-        send_planes(k * CHUNK, CHUNK, planes_ref, whole_ref, deriv_ref)
+        send_planes(k * CHUNK, CHUNK, UNROLL, planes_ref, whole_ref, deriv_ref)
         leaving(k).start()
         return carry
 
@@ -251,8 +255,9 @@
             total = total + speed_ref[1, step * PAIR + k].astype(F32) * parts[1]
             total = total + speed_ref[2, step * PAIR + k].astype(F32) * parts[2]
             fields.append(total.astype(BF16))
-            square = parts[0] * parts[0] + parts[1] * parts[1] + parts[2] * parts[2]
-            peak_ref[...] = jnp.maximum(peak_ref[...], jnp.max(square.reshape(N // 8, 8, N), axis=0))
+            if apart:
+                square = parts[0] * parts[0] + parts[1] * parts[1] + parts[2] * parts[2]
+                peak_ref[...] = jnp.maximum(peak_ref[...], jnp.max(square.reshape(N // 8, 8, N), axis=0))
         x_section = dot(jnp.concatenate(fields, axis=0), x_fwd_ref[...]).astype(BF16)
         sums = []
         for turn in (0, 1):
@@ -268,14 +273,15 @@
 
     for step in range(ROWS // PAIR):
         one_pair(step)
-    shape = (2 * ROWS, HALF)
-    peak = jnp.sqrt(jnp.max(peak_ref[...], keepdims=True))
-    pieces = []
-    for value in (jnp.sum(stats_ref[0], keepdims=True), jnp.sum(stats_ref[1], keepdims=True), peak):
-        pieces.extend(in_three(jnp.broadcast_to(value, shape)))
-    line = jnp.zeros(shape, F32)
-    for k, piece in enumerate(pieces):
-        line = jnp.where((iota(shape, 0) == k) & (iota(shape, 1) == LIMIT), piece, line)
+    if apart:
+        shape = (2 * ROWS, HALF)
+        peak = jnp.sqrt(jnp.max(peak_ref[...], keepdims=True))
+        pieces = []
+        for value in (jnp.sum(stats_ref[0], keepdims=True), jnp.sum(stats_ref[1], keepdims=True), peak):
+            pieces.extend(in_three(jnp.broadcast_to(value, shape)))
+        line = jnp.zeros(shape, F32)
+        for k, piece in enumerate(pieces):
+            line = jnp.where((iota(shape, 0) == k) & (iota(shape, 1) == LIMIT), piece, line)
 
     def some_peers(step, carry):
         for turn in range(SENDS):
@@ -286,7 +292,8 @@
                 real_part = sums_ref[pl.ds(start, ROWS, stride=PITCH), :]
                 imag_part = sums_ref[pl.ds(start + ROWS, ROWS, stride=PITCH), :]
                 parts.append(jnp.concatenate([real_part, imag_part], axis=0))
-            parts[0] = parts[0] + line
+            if apart:
+                parts[0] = parts[0] + line
             for k, block in enumerate(packed(parts)):
                 at = 2 * ROWS * k
                 out_ref[peer, at : at + block.shape[0], :] = block.astype(BF16)
@@ -343,18 +350,21 @@
     kappa_ref[0] = jnp.max(found)
     kappa = found[0:1, :]
     bound = (bound_ref[0] * bound_ref[0]).astype(F32)
-    for local, (sum_real, sum_imag) in enumerate(tendency(came_ref, z_fwd_ref)):
-        kz_wave, ksquare = waves_of(local)
-        factor = jnp.exp(-kappa * ksquare * STEP)
+    kz_wave = signed(iota((N, HALF), 0))
+    along_z = jnp.exp(-kappa * (kz_wave * kz_wave) * STEP)
+    for local, sums in enumerate(tendency(came_ref, z_fwd_ref)):
+        _, ksquare = waves_of(local)
+        factor = along_z * jnp.exp(-kappa * across_z(local) * STEP)
+        scaled = STEP * factor
         inside = ksquare <= bound
-        first = [jnp.where(inside, -part, 0.0) for part in (sum_real, sum_imag)]
         middle = []
         for part in (0, 1):
-            start = state_ref[part, local]
-            middle.append(factor * (start + STEP * first[part]))
-            kept_ref[part, local] = factor * start + (0.5 * STEP) * (factor * first[part])
+            start = factor * state_ref[part, local]
+            change = jnp.where(inside, scaled * sums[part], 0.0)
+            middle.append(start - change)
+            kept_ref[part, local] = start - 0.5 * change
         z_inverse(local, z_rows(*middle, kz_wave), z_inv_ref, whole_ref, deriv_ref)
-    send_planes(0, PEERS, out_ref, whole_ref, deriv_ref)
+    send_planes(0, PEERS, PEERS, out_ref, whole_ref, deriv_ref)
 
 
 def final_kernel(bound_ref, came_ref, kept_ref, z_fwd_ref, out_hbm, out_ref, out_sems):
@@ -363,8 +373,8 @@
     for local, sums in enumerate(tendency(came_ref, z_fwd_ref)):
         _, ksquare = waves_of(local)
         for part in (0, 1):
-            second = jnp.where(ksquare <= bound, -sums[part], 0.0)
-            out_ref[part, local] = kept_ref[part, local] + (0.5 * STEP) * second
+            change = jnp.where(ksquare <= bound, (0.5 * STEP) * sums[part], 0.0)
+            out_ref[part, local] = kept_ref[part, local] - change
         saves.append(copy_of(out_ref.at[:, local], out_hbm.at[:, local], out_sems.at[local]))
         saves[-1].start()
     for save in saves:

time: 188 us -> 188 us (level)
  no operation moved by 1% of the time
where the time goes in v8:
time: 188 us; the launch traced here: 186 us
  blocking collectives  105 us (56%)
  starting transfers between devices  26.3 us (14%)
  waiting for transfers between devices  26 us (14%)
  Pallas kernels  19.7 us (10%)
  local copies, waits for them, and re-layouts  6.61 us (4%)
  between operations  2.32 us (1%)
    all_to_all x3, blocking collectives, exchanged(): return lax.all_to_all(x, 'fft', 0, 0, tiled=True)  105 us
    ppermute x9, waiting for transfers between devices, moved(): return lax.ppermute(x, 'scal', [(s, change(s)) for s in range(groups)])  20.8 us
    ppermute x9, starting transfers between devices, moved(): return lax.ppermute(x, 'scal', [(s, change(s)) for s in range(groups)])  15.2 us
    all_to_all x1, starting transfers between devices, exchanged(): return lax.all_to_all(x, 'fft', 0, 0, tiled=True)  11.1 us
    pallas_call x2, Pallas kernels, grid_call(): pl.pallas_call(grid_kernel, in_specs=[(SCALARS,) * len(scalars), spec, NE...  10 us
    all_to_all x1, waiting for transfers between devices, exchanged(): return lax.all_to_all(x, 'fft', 0, 0, tiled=True)  5.24 us
    pallas_call x1, Pallas kernels, start_call(): pl.pallas_call(start_kernel, in_specs=[FAR, FAR], out_specs=[FAR, NEAR],...  4.82 us
  transfers between devices with their start and end apart: 10, of which 5 were waited for; matrix products, arithmetic and copies ran while one was open for 4% of the time, Pallas kernels for 0%

profile of v8, /device:TPU:1, one launch (start us, length us, event | category | flops | bytes accessed | tf_op | source)
XLA Modules:
  0.0 186.4 jit_solution(16271981470605910408)
XLA Ops:
  0.6 0.0 copy-start.1
  0.6 4.8 %start.1 = (bf16[32,8,16,256]{3,2,1,0:T(8,128)(2,1)}, f32[2,8,128]{2,1,0:T(8,128)S(1)}) custom-call(f32[2,8,256,128]{3,2,1,0:T(8,128)} %bitcast.12, bf16[2,256,256]{2,1,0:T(8,128)(2,1)} %constant.85.table_hbm.held_5_), custom_call_target="tpu_custom_call" | custom-call | tf_op jit(solution)/shard_map/start/pallas_call | solution.py:464
  5.5 11.1 %all-to-all-start = ((bf16[32,8,16,256]{3,2,1,0:T(8,128)(2,1)}), bf16[32,8,16,256]{3,2,1,0:T(8,128)(2,1)}, u32[]{:S(2)}, u32[]{:S(2)}) async-start(bf16[32,8,16,256]{3,2,1,0:T(8,128)(2,1)} %get-tuple-element.15), calls=%async_computation | async-start | bytes 4194304 | tf_op jit(solution)/shard_map/all_to_all | solution.py:460
  16.6 0.0 copy-done.1
  16.6 0.2 reshape.10
  16.7 0.8 copy.17
  17.6 2.7 %collective-permute-start.1 = (bf16[3,8,2,16,256]{4,3,2,1,0:T(8,128)(2,1)}, bf16[3,8,2,16,256]{4,3,2,1,0:T(8,128)(2,1)}, u32[]{:S(2)}, u32[]{:S(2)}) collective-permute-start(bf16[3,8,2,16,256]{4,3,2,1,0:T(8,128)(2,1)} %bitcast.9), channel_id=1, source_target_pairs={{0,3},{1,0},{2,1},{3,2},{4,7},{5,4},{6,5},{7,6},{8,11},{9,8},{10,9... | collective-permute-start | bytes 1179656 | tf_op jit(solution)/shard_map/ppermute | solution.py:433
  20.3 0.0 collective-permute-start
  20.3 2.4 %collective-permute-start.4 = (bf16[3,8,2,16,256]{4,3,2,1,0:T(8,128)(2,1)}, bf16[3,8,2,16,256]{4,3,2,1,0:T(8,128)(2,1)}, u32[]{:S(2)}, u32[]{:S(2)}) collective-permute-start(bf16[3,8,2,16,256]{4,3,2,1,0:T(8,128)(2,1)} %bitcast.9), channel_id=1, source_target_pairs={{0,4},{1,5},{2,6},{3,7},{4,0},{5,1},{6,2},{7,3},{8,12},{9,13},{10,... | collective-permute-start | bytes 1179656 | tf_op jit(solution)/shard_map/ppermute | solution.py:433
  24.1 0.4 broadcast_in_dim.6
  24.4 0.1 constant_dynamic-update-slice_fusion.9
  24.5 4.3 %collective-permute-done.1 = bf16[3,8,2,16,256]{4,3,2,1,0:T(8,128)(2,1)} collective-permute-done((bf16[3,8,2,16,256]{4,3,2,1,0:T(8,128)(2,1)}, bf16[3,8,2,16,256]{4,3,2,1,0:T(8,128)(2,1)}, u32[]{:S(2)}, u32[]{:S(2)}) %collective-permute-start.1) | collective-permute-done | bytes 393248 | tf_op jit(solution)/shard_map/ppermute | solution.py:433
  28.8 0.9 slice.17
  29.7 3.5 %collective-permute-start.3 = (bf16[3,4,2,16,256]{4,3,2,1,0:T(8,128)(2,1)S(1)}, bf16[3,4,2,16,256]{4,3,2,1,0:T(8,128)(2,1)S(1)}, u32[]{:S(2)}, u32[]{:S(2)}) collective-permute-start(bf16[3,4,2,16,256]{4,3,2,1,0:T(8,128)(2,1)S(1)} %slice.17), channel_id=1, source_target_pairs={{0,3},{1,0},{2,1},{3,2},{4,7},{5,4},{6,5},{7,6},{8,11},{9,8},{10,9... | collective-permute-start | bytes 589832 | tf_op jit(solution)/shard_map/ppermute | solution.py:433
  33.2 0.0 collective-permute-done
  33.2 0.9 slice.16
  34.2 0.0 copy-start
  34.2 0.1 collective-permute-start.2
  34.3 5.5 %collective-permute-done.4 = bf16[3,8,2,16,256]{4,3,2,1,0:T(8,128)(2,1)} collective-permute-done((bf16[3,8,2,16,256]{4,3,2,1,0:T(8,128)(2,1)}, bf16[3,8,2,16,256]{4,3,2,1,0:T(8,128)(2,1)}, u32[]{:S(2)}, u32[]{:S(2)}) %collective-permute-start.4) | collective-permute-done | bytes 393248 | tf_op jit(solution)/shard_map/ppermute | solution.py:433
  39.8 2.7 %collective-permute-start.6 = (bf16[3,8,2,16,256]{4,3,2,1,0:T(8,128)(2,1)}, bf16[3,8,2,16,256]{4,3,2,1,0:T(8,128)(2,1)S(1)}, u32[]{:S(2)}, u32[]{:S(2)}) collective-permute-start(bf16[3,8,2,16,256]{4,3,2,1,0:T(8,128)(2,1)} %collective-permute-done.4), channel_id=1, source_target_pairs={{0,3},{1,0},{2,1},{3,2},{4,7},{5,4},{6,5},{7,6},{8,11},{9,8},{10,9... | collective-permute-start | bytes 1179656 | tf_op jit(solution)/shard_map/ppermute | solution.py:433
  42.4 0.0 collective-permute-start.5
  42.4 1.0 constant_dynamic-update-slice_fusion.8
  43.5 1.0 constant_dynamic-update-slice_fusion.7
  44.5 0.0 collective-permute-done.2
  44.6 0.0 collective-permute-done.3
  44.6 1.0 constant_dynamic-update-slice_fusion.4
  45.6 5.0 %collective-permute-done.6 = bf16[3,8,2,16,256]{4,3,2,1,0:T(8,128)(2,1)S(1)} collective-permute-done((bf16[3,8,2,16,256]{4,3,2,1,0:T(8,128)(2,1)}, bf16[3,8,2,16,256]{4,3,2,1,0:T(8,128)(2,1)S(1)}, u32[]{:S(2)}, u32[]{:S(2)}) %collective-permute-start.6) | collective-permute-done | bytes 393248 | tf_op jit(solution)/shard_map/ppermute | solution.py:433
  50.6 3.5 %collective-permute-start.8 = (bf16[3,4,2,16,256]{4,3,2,1,0:T(8,128)(2,1)S(1)}, bf16[3,4,2,16,256]{4,3,2,1,0:T(8,128)(2,1)S(1)}, u32[]{:S(2)}, u32[]{:S(2)}) collective-permute-start(bf16[3,4,2,16,256]{4,3,2,1,0:T(8,128)(2,1)S(1)} %slice.19), channel_id=1, source_target_pairs={{0,3},{1,0},{2,1},{3,2},{4,7},{5,4},{6,5},{7,6},{8,11},{9,8},{10,9... | collective-permute-start | bytes 589832 | tf_op jit(solution)/shard_map/ppermute | solution.py:433
  54.1 0.0 collective-permute-done.5
  54.2 0.3 collective-permute-start.7
  54.5 6.0 %collective-permute-done.7 = bf16[3,4,2,16,256]{4,3,2,1,0:T(8,128)(2,1)S(1)} collective-permute-done((bf16[3,4,2,16,256]{4,3,2,1,0:T(8,128)(2,1)S(1)}, bf16[3,4,2,16,256]{4,3,2,1,0:T(8,128)(2,1)S(1)}, u32[]{:S(2)}, u32[]{:S(2)}) %collective-permute-start.7) | collective-permute-done | bytes 196640 | tf_op jit(solution)/shard_map/ppermute | solution.py:433
  60.6 0.0 collective-permute-done.8
  60.6 5.2 %all-to-all-done.planes_hbm = bf16[32,8,16,256]{3,2,1,0:T(8,128)(2,1)} async-done(((bf16[32,8,16,256]{3,2,1,0:T(8,128)(2,1)}), bf16[32,8,16,256]{3,2,1,0:T(8,128)(2,1)}, u32[]{:S(2)}, u32[]{:S(2)}) %all-to-all-start) | async-done | bytes 2097184 | tf_op jit(solution)/shard_map/all_to_all | solution.py:460
  65.9 0.0 copy-done
  65.9 6.3 %grid.2 = (bf16[32,88,128]{2,1,0:T(8,128)(2,1)S(1)}, bf16[2,256,256]{2,1,0:T(8,128)(2,1)S(1)}, bf16[256,256]{1,0:T(8,128)(2,1)S(1)}, bf16[256,256]{1,0:T(8,128)(...) custom-call(s32[1]{0:T(128)S(6)} %copy.29.scalars_0_.bound_ref, ...), custom_call_target="tpu_custom_call" | custom-call | tf_op jit(solution)/shard_map/grid/pallas_call | solution.py:481
  72.2 25.5 %all_to_all.20.came_ref = bf16[32,88,128]{2,1,0:T(8,128)(2,1)S(1)} all-to-all(bf16[32,88,128]{2,1,0:T(8,128)(2,1)S(1)} %get-tuple-element.17), channel_id=1, replica_groups=mesh['fft'=32,'scal'=8] {'fft'}, dimensions={0} | all-to-all | bytes 1441792 | tf_op jit(solution)/shard_map/all_to_all | solution.py:460
  97.7 2.8 %middle.1 = (bf16[32,8,16,256]{3,2,1,0:T(8,128)(2,1)S(1)}, f32[2,8,256,128]{3,2,1,0:T(8,128)S(1)}, f32[1]{0:T(128)}) custom-call(s32[1]{0:T(128)S(6)} %copy.29.scalars_0_.bound_ref, s32[1]{0:T(128)S(6)} %copy.28.scalars_1_.species_ref, f32[64]{0:T(128)S(1)} %copy-done, bf16[32,88,128]{2,1,0:T(8,128)(2,1)S(1)} %all_to_all.20.came_ref, ...), custom_call_target="tpu_custom_call" | custom-call | tf_op jit(solution)/shard_map/middle/pallas_call | solution.py:493
  100.6 54.1 %all_to_all.21.planes_hbm = bf16[32,8,16,256]{3,2,1,0:T(8,128)(2,1)S(1)} all-to-all(bf16[32,8,16,256]{3,2,1,0:T(8,128)(2,1)S(1)} %get-tuple-element.21), channel_id=1, replica_groups=mesh['fft'=32,'scal'=8] {'fft'}, dimensions={0} | all-to-all | bytes 4194304 | tf_op jit(solution)/shard_map/all_to_all | solution.py:460
  154.7 3.7 %grid.3 = bf16[32,88,128]{2,1,0:T(8,128)(2,1)S(1)} custom-call(bf16[32,8,16,256]{3,2,1,0:T(8,128)(2,1)S(1)} %all_to_all.21.planes_hbm, bf16[3,8,256,256]{3,2,1,0:T(8,128)(2,1)S(1)} %bitcast.11, f32[2,8,128]{2,1,0:T(8,128)S(1)} %get-tuple-element.16.stats_ref, bf16[2,256,256]{2,1,0:T(8,128)(2,1)S(1)} %get-tuple-element.22.held_0_, ...), custom_call_target="tpu_custom_call" | custom-call | tf_op jit(solution)/shard_map/grid/pallas_call | solution.py:481
  158.4 25.8 %all_to_all.22.came_ref = bf16[32,88,128]{2,1,0:T(8,128)(2,1)S(1)} all-to-all(bf16[32,88,128]{2,1,0:T(8,128)(2,1)S(1)} %grid.3), channel_id=1, replica_groups=mesh['fft'=32,'scal'=8] {'fft'}, dimensions={0} | all-to-all | bytes 1441792 | tf_op jit(solution)/shard_map/all_to_all | solution.py:460
  184.2 2.0 %final.1 = f32[2,8,256,128]{3,2,1,0:T(8,128)} custom-call(s32[1]{0:T(128)S(6)} %copy.29.scalars_0_.bound_ref, bf16[32,88,128]{2,1,0:T(8,128)(2,1)S(1)} %all_to_all.22.came_ref, f32[2,8,256,128]{3,2,1,0:T(8,128)S(1)} %get-tuple-element.26.kept_ref, bf16[352,512]{1,0:T(8,128)(2,1)S(1)} %get-tuple-element.19.z_fwd_ref), custom_call_target="tpu_custom_call" | custom-call | tf_op jit(solution)/shard_map/final/pallas_call | solution.py:505
  (8 shorter events, 0.2 us)
Async XLA Ops:
  0.6 16.0 %copy-start.1 = (bf16[3,8,32,256]{3,2,1,0:T(8,128)(2,1)S(1)}, bf16[3,8,32,256]{3,2,1,0:T(8,128)(2,1)}, u32[]{:S(2)}) copy-start(bf16[3,8,32,256]{3,2,1,0:T(8,128)(2,1)} %param.12) | copy-start | bytes 1179652
  5.5 60.4 %all-to-all-start = ((bf16[32,8,16,256]{3,2,1,0:T(8,128)(2,1)}), bf16[32,8,16,256]{3,2,1,0:T(8,128)(2,1)}, u32[]{:S(2)}, u32[]{:S(2)}) async-start(bf16[32,8,16,256]{3,2,1,0:T(8,128)(2,1)} %get-tuple-element.15), calls=%async_computation | async-start | bytes 4194304 | tf_op jit(solution)/shard_map/all_to_all | solution.py:460
  17.6 11.2 %collective-permute-start.1 = (bf16[3,8,2,16,256]{4,3,2,1,0:T(8,128)(2,1)}, bf16[3,8,2,16,256]{4,3,2,1,0:T(8,128)(2,1)}, u32[]{:S(2)}, u32[]{:S(2)}) collective-permute-start(bf16[3,8,2,16,256]{4,3,2,1,0:T(8,128)(2,1)} %bitcast.9), channel_id=1, source_target_pairs={{0,3},{1,0},{2,1},{3,2},{4,7},{5,4},{6,5},{7,6},{8,11},{9,8},{10,9... | collective-permute-start | bytes 1179656 | tf_op jit(solution)/shard_map/ppermute | solution.py:433
  20.3 12.9 %collective-permute-start = (bf16[3,8,2,16,256]{4,3,2,1,0:T(8,128)(2,1)}, bf16[3,8,2,16,256]{4,3,2,1,0:T(8,128)(2,1)}, u32[]{:S(2)}, u32[]{:S(2)}) collective-permute-start(bf16[3,8,2,16,256]{4,3,2,1,0:T(8,128)(2,1)} %bitcast.9), channel_id=1, source_target_pairs={{0,1},{1,2},{2,3},{3,0},{4,5},{5,6},{6,7},{7,4},{8,9},{9,10},{10,1... | collective-permute-start | bytes 1179656 | tf_op jit(solution)/shard_map/ppermute | solution.py:433
  20.3 19.5 %collective-permute-start.4 = (bf16[3,8,2,16,256]{4,3,2,1,0:T(8,128)(2,1)}, bf16[3,8,2,16,256]{4,3,2,1,0:T(8,128)(2,1)}, u32[]{:S(2)}, u32[]{:S(2)}) collective-permute-start(bf16[3,8,2,16,256]{4,3,2,1,0:T(8,128)(2,1)} %bitcast.9), channel_id=1, source_target_pairs={{0,4},{1,5},{2,6},{3,7},{4,0},{5,1},{6,2},{7,3},{8,12},{9,13},{10,... | collective-permute-start | bytes 1179656 | tf_op jit(solution)/shard_map/ppermute | solution.py:433
  29.7 14.8 %collective-permute-start.3 = (bf16[3,4,2,16,256]{4,3,2,1,0:T(8,128)(2,1)S(1)}, bf16[3,4,2,16,256]{4,3,2,1,0:T(8,128)(2,1)S(1)}, u32[]{:S(2)}, u32[]{:S(2)}) collective-permute-start(bf16[3,4,2,16,256]{4,3,2,1,0:T(8,128)(2,1)S(1)} %slice.17), channel_id=1, source_target_pairs={{0,3},{1,0},{2,1},{3,2},{4,7},{5,4},{6,5},{7,6},{8,11},{9,8},{10,9... | collective-permute-start | bytes 589832 | tf_op jit(solution)/shard_map/ppermute | solution.py:433
  34.2 31.7 %copy-start = (f32[64]{0:T(128)S(1)}, f32[64]{0:T(128)}, u32[]{:S(2)}) copy-start(f32[64]{0:T(128)} %base_ref.1) | copy-start | bytes 772
  34.2 10.4 %collective-permute-start.2 = (bf16[3,4,2,16,256]{4,3,2,1,0:T(8,128)(2,1)S(1)}, bf16[3,4,2,16,256]{4,3,2,1,0:T(8,128)(2,1)S(1)}, u32[]{:S(2)}, u32[]{:S(2)}) collective-permute-start(bf16[3,4,2,16,256]{4,3,2,1,0:T(8,128)(2,1)S(1)} %slice.16), channel_id=1, source_target_pairs={{0,1},{1,2},{2,3},{3,0},{4,5},{5,6},{6,7},{7,4},{8,9},{9,10},{10,1... | collective-permute-start | bytes 589832 | tf_op jit(solution)/shard_map/ppermute | solution.py:433
  39.8 10.9 %collective-permute-start.6 = (bf16[3,8,2,16,256]{4,3,2,1,0:T(8,128)(2,1)}, bf16[3,8,2,16,256]{4,3,2,1,0:T(8,128)(2,1)S(1)}, u32[]{:S(2)}, u32[]{:S(2)}) collective-permute-start(bf16[3,8,2,16,256]{4,3,2,1,0:T(8,128)(2,1)} %collective-permute-done.4), channel_id=1, source_target_pairs={{0,3},{1,0},{2,1},{3,2},{4,7},{5,4},{6,5},{7,6},{8,11},{9,8},{10,9... | collective-permute-start | bytes 1179656 | tf_op jit(solution)/shard_map/ppermute | solution.py:433
  42.4 11.7 %collective-permute-start.5 = (bf16[3,8,2,16,256]{4,3,2,1,0:T(8,128)(2,1)}, bf16[3,8,2,16,256]{4,3,2,1,0:T(8,128)(2,1)S(1)}, u32[]{:S(2)}, u32[]{:S(2)}) collective-permute-start(bf16[3,8,2,16,256]{4,3,2,1,0:T(8,128)(2,1)} %collective-permute-done.4), channel_id=1, source_target_pairs={{0,1},{1,2},{2,3},{3,0},{4,5},{5,6},{6,7},{7,4},{8,9},{9,10},{10,1... | collective-permute-start | bytes 1179656 | tf_op jit(solution)/shard_map/ppermute | solution.py:433
  50.6 10.0 %collective-permute-start.8 = (bf16[3,4,2,16,256]{4,3,2,1,0:T(8,128)(2,1)S(1)}, bf16[3,4,2,16,256]{4,3,2,1,0:T(8,128)(2,1)S(1)}, u32[]{:S(2)}, u32[]{:S(2)}) collective-permute-start(bf16[3,4,2,16,256]{4,3,2,1,0:T(8,128)(2,1)S(1)} %slice.19), channel_id=1, source_target_pairs={{0,3},{1,0},{2,1},{3,2},{4,7},{5,4},{6,5},{7,6},{8,11},{9,8},{10,9... | collective-permute-start | bytes 589832 | tf_op jit(solution)/shard_map/ppermute | solution.py:433
  54.2 6.4 %collective-permute-start.7 = (bf16[3,4,2,16,256]{4,3,2,1,0:T(8,128)(2,1)S(1)}, bf16[3,4,2,16,256]{4,3,2,1,0:T(8,128)(2,1)S(1)}, u32[]{:S(2)}, u32[]{:S(2)}) collective-permute-start(bf16[3,4,2,16,256]{4,3,2,1,0:T(8,128)(2,1)S(1)} %slice.18), channel_id=1, source_target_pairs={{0,1},{1,2},{2,3},{3,0},{4,5},{5,6},{6,7},{7,4},{8,9},{9,10},{10,1... | collective-permute-start | bytes 589832 | tf_op jit(solution)/shard_map/ppermute | solution.py:433

commit v9 on v8

--- a/solution.py
+++ b/solution.py
@@ -133,19 +133,18 @@
     stats_ref[...] = jnp.zeros_like(stats_ref)
     loads[0].wait()
 
-    def one_row(local, carry):
-        copy_of(state_hbm.at[:, local], state_ref.at[:, local], in_sems.at[local]).wait()
-        kz_wave, ksquare = waves_of(local)
-        real_part = state_ref[0, local]
-        imag_part = state_ref[1, local]
-        weight = jnp.where(iota((N, HALF), 1) == 0, 1.0, 2.0)
-        energy = weight * (real_part * real_part + imag_part * imag_part)
-        stats_ref[0] += jnp.sum(energy.reshape(N // 8, 8, HALF), axis=0)
-        stats_ref[1] += jnp.sum((ksquare * energy).reshape(N // 8, 8, HALF), axis=0)
-        z_inverse(local, z_rows(real_part, imag_part, kz_wave), table_ref, whole_ref, deriv_ref)
-        return carry
-
-    lax.fori_loop(0, ROWS, one_row, 0, unroll=2)
+    for first in range(0, ROWS, AT_ONCE):
+        for local in range(first, first + AT_ONCE):
+            loads[1 + local].wait()
+        for local in range(first, first + AT_ONCE):
+            kz_wave, ksquare = waves_of(local)
+            real_part = state_ref[0, local]
+            imag_part = state_ref[1, local]
+            weight = jnp.where(iota((N, HALF), 1) == 0, 1.0, 2.0)
+            energy = weight * (real_part * real_part + imag_part * imag_part)
+            stats_ref[0] += jnp.sum(energy.reshape(N // 8, 8, HALF), axis=0)
+            stats_ref[1] += jnp.sum((ksquare * energy).reshape(N // 8, 8, HALF), axis=0)
+            z_inverse(local, z_rows(real_part, imag_part, kz_wave), table_ref, whole_ref, deriv_ref)
 
     def leaving(k):
         part = pl.ds(k * CHUNK, CHUNK)
@@ -229,11 +228,12 @@
         if apart:
             for k in range(PAIR):
                 came_plane(step * PAIR + k).wait()
+        if apart and step == 0:
+            for load in loads[:4]:
+                load.wait()
         came = [planes_ref[:, step * PAIR + k].reshape(count, N) for k in range(PAIR)]
         scaled = [ky_wave * part[:, :HALF] for part in came]
         pairs = both_turns(jnp.concatenate(came + scaled, axis=1))
-        if apart and step == 0:
-            loads[0].wait()
         y_section = [dot(y_inv_ref[turn], pairs[turn]) for turn in (0, 1)]
         x_rows = []
         for k in range(PAIR):
@@ -244,9 +244,6 @@
                     if which == 0:
                         halves = [kx_wave * half for half in halves]
                     x_rows.append(jnp.concatenate(halves, axis=1).astype(BF16))
-        if apart and step == 0:
-            for load in loads[1:4]:
-                load.wait()
         gradients = dot(jnp.concatenate(x_rows, axis=0), x_inv_ref[...])
         fields = []
         for k in range(PAIR):
@@ -388,6 +385,7 @@
 SENT = (PEERS, 2 * ROWS * KEPT * ROWS // HALF, HALF)
 STATE = (2, ROWS, N, HALF)
 PAIR = 4
+AT_ONCE = 4
 CHUNK = 8
 UNROLL = 4
 SENDS = 32

time: 188 us -> 186 us (0.989)
  no operation moved by 1% of the time
where the time goes in v9:
time: 186 us; the launch traced here: 185 us
  blocking collectives  105 us (56%)
  starting transfers between devices  26.3 us (14%)
  waiting for transfers between devices  26 us (14%)
  Pallas kernels  18.5 us (10%)
  local copies, waits for them, and re-layouts  6.61 us (4%)
  between operations  2.32 us (1%)
    all_to_all x3, blocking collectives, exchanged(): return lax.all_to_all(x, 'fft', 0, 0, tiled=True)  105 us
    ppermute x9, waiting for transfers between devices, moved(): return lax.ppermute(x, 'scal', [(s, change(s)) for s in range(groups)])  20.8 us
    ppermute x9, starting transfers between devices, moved(): return lax.ppermute(x, 'scal', [(s, change(s)) for s in range(groups)])  15.2 us
    all_to_all x1, starting transfers between devices, exchanged(): return lax.all_to_all(x, 'fft', 0, 0, tiled=True)  11.1 us
    pallas_call x2, Pallas kernels, grid_call(): pl.pallas_call(grid_kernel, in_specs=[(SCALARS,) * len(scalars), spec, NE...  9.8 us
    all_to_all x1, waiting for transfers between devices, exchanged(): return lax.all_to_all(x, 'fft', 0, 0, tiled=True)  5.26 us
    pallas_call x1, Pallas kernels, start_call(): pl.pallas_call(start_kernel, in_specs=[FAR, FAR], out_specs=[FAR, NEAR],...  3.85 us
  transfers between devices with their start and end apart: 10, of which 5 were waited for; matrix products, arithmetic and copies ran while one was open for 4% of the time, Pallas kernels for 0%

profile of v9, /device:TPU:1, one launch (start us, length us, event | category | flops | bytes accessed | tf_op | source)
XLA Modules:
  0.0 185.2 jit_solution(16139876666131494517)
XLA Ops:
  0.6 0.0 copy-start.1
  0.6 3.9 %start.1 = (bf16[32,8,16,256]{3,2,1,0:T(8,128)(2,1)}, f32[2,8,128]{2,1,0:T(8,128)S(1)}) custom-call(f32[2,8,256,128]{3,2,1,0:T(8,128)} %bitcast.12, bf16[2,256,256]{2,1,0:T(8,128)(2,1)} %constant.85.table_hbm.held_5_), custom_call_target="tpu_custom_call" | custom-call | tf_op jit(solution)/shard_map/start/pallas_call | solution.py:462
  4.5 11.1 %all-to-all-start = ((bf16[32,8,16,256]{3,2,1,0:T(8,128)(2,1)}), bf16[32,8,16,256]{3,2,1,0:T(8,128)(2,1)}, u32[]{:S(2)}, u32[]{:S(2)}) async-start(bf16[32,8,16,256]{3,2,1,0:T(8,128)(2,1)} %get-tuple-element.15), calls=%async_computation | async-start | bytes 4194304 | tf_op jit(solution)/shard_map/all_to_all | solution.py:458
  15.6 0.0 copy-done.1
  15.6 0.2 reshape.10
  15.8 0.8 copy.17
  16.6 2.7 %collective-permute-start.1 = (bf16[3,8,2,16,256]{4,3,2,1,0:T(8,128)(2,1)}, bf16[3,8,2,16,256]{4,3,2,1,0:T(8,128)(2,1)}, u32[]{:S(2)}, u32[]{:S(2)}) collective-permute-start(bf16[3,8,2,16,256]{4,3,2,1,0:T(8,128)(2,1)} %bitcast.9), channel_id=1, source_target_pairs={{0,3},{1,0},{2,1},{3,2},{4,7},{5,4},{6,5},{7,6},{8,11},{9,8},{10,9... | collective-permute-start | bytes 1179656 | tf_op jit(solution)/shard_map/ppermute | solution.py:431
  19.3 0.0 collective-permute-start
  19.3 2.4 %collective-permute-start.4 = (bf16[3,8,2,16,256]{4,3,2,1,0:T(8,128)(2,1)}, bf16[3,8,2,16,256]{4,3,2,1,0:T(8,128)(2,1)}, u32[]{:S(2)}, u32[]{:S(2)}) collective-permute-start(bf16[3,8,2,16,256]{4,3,2,1,0:T(8,128)(2,1)} %bitcast.9), channel_id=1, source_target_pairs={{0,4},{1,5},{2,6},{3,7},{4,0},{5,1},{6,2},{7,3},{8,12},{9,13},{10,... | collective-permute-start | bytes 1179656 | tf_op jit(solution)/shard_map/ppermute | solution.py:431
  23.1 0.4 broadcast_in_dim.6
  23.5 0.1 constant_dynamic-update-slice_fusion.9
  23.6 4.3 %collective-permute-done.1 = bf16[3,8,2,16,256]{4,3,2,1,0:T(8,128)(2,1)} collective-permute-done((bf16[3,8,2,16,256]{4,3,2,1,0:T(8,128)(2,1)}, bf16[3,8,2,16,256]{4,3,2,1,0:T(8,128)(2,1)}, u32[]{:S(2)}, u32[]{:S(2)}) %collective-permute-start.1) | collective-permute-done | bytes 393248 | tf_op jit(solution)/shard_map/ppermute | solution.py:431
  27.8 0.9 slice.17
  28.8 3.5 %collective-permute-start.3 = (bf16[3,4,2,16,256]{4,3,2,1,0:T(8,128)(2,1)S(1)}, bf16[3,4,2,16,256]{4,3,2,1,0:T(8,128)(2,1)S(1)}, u32[]{:S(2)}, u32[]{:S(2)}) collective-permute-start(bf16[3,4,2,16,256]{4,3,2,1,0:T(8,128)(2,1)S(1)} %slice.17), channel_id=1, source_target_pairs={{0,3},{1,0},{2,1},{3,2},{4,7},{5,4},{6,5},{7,6},{8,11},{9,8},{10,9... | collective-permute-start | bytes 589832 | tf_op jit(solution)/shard_map/ppermute | solution.py:431
  32.2 0.0 collective-permute-done
  32.2 0.9 slice.16
  33.2 0.0 copy-start
  33.2 0.1 collective-permute-start.2
  33.3 5.5 %collective-permute-done.4 = bf16[3,8,2,16,256]{4,3,2,1,0:T(8,128)(2,1)} collective-permute-done((bf16[3,8,2,16,256]{4,3,2,1,0:T(8,128)(2,1)}, bf16[3,8,2,16,256]{4,3,2,1,0:T(8,128)(2,1)}, u32[]{:S(2)}, u32[]{:S(2)}) %collective-permute-start.4) | collective-permute-done | bytes 393248 | tf_op jit(solution)/shard_map/ppermute | solution.py:431
  38.8 2.7 %collective-permute-start.6 = (bf16[3,8,2,16,256]{4,3,2,1,0:T(8,128)(2,1)}, bf16[3,8,2,16,256]{4,3,2,1,0:T(8,128)(2,1)S(1)}, u32[]{:S(2)}, u32[]{:S(2)}) collective-permute-start(bf16[3,8,2,16,256]{4,3,2,1,0:T(8,128)(2,1)} %collective-permute-done.4), channel_id=1, source_target_pairs={{0,3},{1,0},{2,1},{3,2},{4,7},{5,4},{6,5},{7,6},{8,11},{9,8},{10,9... | collective-permute-start | bytes 1179656 | tf_op jit(solution)/shard_map/ppermute | solution.py:431
  41.4 0.0 collective-permute-start.5
  41.5 1.0 constant_dynamic-update-slice_fusion.8
  42.5 1.0 constant_dynamic-update-slice_fusion.7
  43.5 0.0 collective-permute-done.2
  43.6 0.0 collective-permute-done.3
  43.6 1.0 constant_dynamic-update-slice_fusion.4
  44.7 5.0 %collective-permute-done.6 = bf16[3,8,2,16,256]{4,3,2,1,0:T(8,128)(2,1)S(1)} collective-permute-done((bf16[3,8,2,16,256]{4,3,2,1,0:T(8,128)(2,1)}, bf16[3,8,2,16,256]{4,3,2,1,0:T(8,128)(2,1)S(1)}, u32[]{:S(2)}, u32[]{:S(2)}) %collective-permute-start.6) | collective-permute-done | bytes 393248 | tf_op jit(solution)/shard_map/ppermute | solution.py:431
  49.7 3.5 %collective-permute-start.8 = (bf16[3,4,2,16,256]{4,3,2,1,0:T(8,128)(2,1)S(1)}, bf16[3,4,2,16,256]{4,3,2,1,0:T(8,128)(2,1)S(1)}, u32[]{:S(2)}, u32[]{:S(2)}) collective-permute-start(bf16[3,4,2,16,256]{4,3,2,1,0:T(8,128)(2,1)S(1)} %slice.19), channel_id=1, source_target_pairs={{0,3},{1,0},{2,1},{3,2},{4,7},{5,4},{6,5},{7,6},{8,11},{9,8},{10,9... | collective-permute-start | bytes 589832 | tf_op jit(solution)/shard_map/ppermute | solution.py:431
  53.2 0.0 collective-permute-done.5
  53.2 0.3 collective-permute-start.7
  53.6 6.0 %collective-permute-done.7 = bf16[3,4,2,16,256]{4,3,2,1,0:T(8,128)(2,1)S(1)} collective-permute-done((bf16[3,4,2,16,256]{4,3,2,1,0:T(8,128)(2,1)S(1)}, bf16[3,4,2,16,256]{4,3,2,1,0:T(8,128)(2,1)S(1)}, u32[]{:S(2)}, u32[]{:S(2)}) %collective-permute-start.7) | collective-permute-done | bytes 196640 | tf_op jit(solution)/shard_map/ppermute | solution.py:431
  59.6 0.0 collective-permute-done.8
  59.7 5.3 %all-to-all-done.planes_hbm = bf16[32,8,16,256]{3,2,1,0:T(8,128)(2,1)} async-done(((bf16[32,8,16,256]{3,2,1,0:T(8,128)(2,1)}), bf16[32,8,16,256]{3,2,1,0:T(8,128)(2,1)}, u32[]{:S(2)}, u32[]{:S(2)}) %all-to-all-start) | async-done | bytes 2097184 | tf_op jit(solution)/shard_map/all_to_all | solution.py:458
  64.9 0.0 copy-done
  64.9 6.1 %grid.2 = (bf16[32,88,128]{2,1,0:T(8,128)(2,1)S(1)}, bf16[2,256,256]{2,1,0:T(8,128)(2,1)S(1)}, bf16[256,256]{1,0:T(8,128)(2,1)S(1)}, bf16[256,256]{1,0:T(8,128)(...) custom-call(s32[1]{0:T(128)S(6)} %copy.29.scalars_0_.bound_ref, ...), custom_call_target="tpu_custom_call" | custom-call | tf_op jit(solution)/shard_map/grid/pallas_call | solution.py:479
  71.0 25.5 %all_to_all.20.came_ref = bf16[32,88,128]{2,1,0:T(8,128)(2,1)S(1)} all-to-all(bf16[32,88,128]{2,1,0:T(8,128)(2,1)S(1)} %get-tuple-element.17), channel_id=1, replica_groups=mesh['fft'=32,'scal'=8] {'fft'}, dimensions={0} | all-to-all | bytes 1441792 | tf_op jit(solution)/shard_map/all_to_all | solution.py:458
  96.5 2.8 %middle.1 = (bf16[32,8,16,256]{3,2,1,0:T(8,128)(2,1)S(1)}, f32[2,8,256,128]{3,2,1,0:T(8,128)S(1)}, f32[1]{0:T(128)}) custom-call(s32[1]{0:T(128)S(6)} %copy.29.scalars_0_.bound_ref, s32[1]{0:T(128)S(6)} %copy.28.scalars_1_.species_ref, f32[64]{0:T(128)S(1)} %copy-done, bf16[32,88,128]{2,1,0:T(8,128)(2,1)S(1)} %all_to_all.20.came_ref, ...), custom_call_target="tpu_custom_call" | custom-call | tf_op jit(solution)/shard_map/middle/pallas_call | solution.py:491
  99.4 54.1 %all_to_all.21.planes_hbm = bf16[32,8,16,256]{3,2,1,0:T(8,128)(2,1)S(1)} all-to-all(bf16[32,8,16,256]{3,2,1,0:T(8,128)(2,1)S(1)} %get-tuple-element.21), channel_id=1, replica_groups=mesh['fft'=32,'scal'=8] {'fft'}, dimensions={0} | all-to-all | bytes 4194304 | tf_op jit(solution)/shard_map/all_to_all | solution.py:458
  153.5 3.7 %grid.3 = bf16[32,88,128]{2,1,0:T(8,128)(2,1)S(1)} custom-call(bf16[32,8,16,256]{3,2,1,0:T(8,128)(2,1)S(1)} %all_to_all.21.planes_hbm, bf16[3,8,256,256]{3,2,1,0:T(8,128)(2,1)S(1)} %bitcast.11, f32[2,8,128]{2,1,0:T(8,128)S(1)} %get-tuple-element.16.stats_ref, bf16[2,256,256]{2,1,0:T(8,128)(2,1)S(1)} %get-tuple-element.22.held_0_, ...), custom_call_target="tpu_custom_call" | custom-call | tf_op jit(solution)/shard_map/grid/pallas_call | solution.py:479
  157.2 25.8 %all_to_all.22.came_ref = bf16[32,88,128]{2,1,0:T(8,128)(2,1)S(1)} all-to-all(bf16[32,88,128]{2,1,0:T(8,128)(2,1)S(1)} %grid.3), channel_id=1, replica_groups=mesh['fft'=32,'scal'=8] {'fft'}, dimensions={0} | all-to-all | bytes 1441792 | tf_op jit(solution)/shard_map/all_to_all | solution.py:458
  183.0 2.0 %final.1 = f32[2,8,256,128]{3,2,1,0:T(8,128)} custom-call(s32[1]{0:T(128)S(6)} %copy.29.scalars_0_.bound_ref, bf16[32,88,128]{2,1,0:T(8,128)(2,1)S(1)} %all_to_all.22.came_ref, f32[2,8,256,128]{3,2,1,0:T(8,128)S(1)} %get-tuple-element.26.kept_ref, bf16[352,512]{1,0:T(8,128)(2,1)S(1)} %get-tuple-element.19.z_fwd_ref), custom_call_target="tpu_custom_call" | custom-call | tf_op jit(solution)/shard_map/final/pallas_call | solution.py:503
  (8 shorter events, 0.2 us)
Async XLA Ops:
  0.6 15.0 %copy-start.1 = (bf16[3,8,32,256]{3,2,1,0:T(8,128)(2,1)S(1)}, bf16[3,8,32,256]{3,2,1,0:T(8,128)(2,1)}, u32[]{:S(2)}) copy-start(bf16[3,8,32,256]{3,2,1,0:T(8,128)(2,1)} %param.12) | copy-start | bytes 1179652
  4.5 60.4 %all-to-all-start = ((bf16[32,8,16,256]{3,2,1,0:T(8,128)(2,1)}), bf16[32,8,16,256]{3,2,1,0:T(8,128)(2,1)}, u32[]{:S(2)}, u32[]{:S(2)}) async-start(bf16[32,8,16,256]{3,2,1,0:T(8,128)(2,1)} %get-tuple-element.15), calls=%async_computation | async-start | bytes 4194304 | tf_op jit(solution)/shard_map/all_to_all | solution.py:458
  16.6 11.2 %collective-permute-start.1 = (bf16[3,8,2,16,256]{4,3,2,1,0:T(8,128)(2,1)}, bf16[3,8,2,16,256]{4,3,2,1,0:T(8,128)(2,1)}, u32[]{:S(2)}, u32[]{:S(2)}) collective-permute-start(bf16[3,8,2,16,256]{4,3,2,1,0:T(8,128)(2,1)} %bitcast.9), channel_id=1, source_target_pairs={{0,3},{1,0},{2,1},{3,2},{4,7},{5,4},{6,5},{7,6},{8,11},{9,8},{10,9... | collective-permute-start | bytes 1179656 | tf_op jit(solution)/shard_map/ppermute | solution.py:431
  19.3 12.9 %collective-permute-start = (bf16[3,8,2,16,256]{4,3,2,1,0:T(8,128)(2,1)}, bf16[3,8,2,16,256]{4,3,2,1,0:T(8,128)(2,1)}, u32[]{:S(2)}, u32[]{:S(2)}) collective-permute-start(bf16[3,8,2,16,256]{4,3,2,1,0:T(8,128)(2,1)} %bitcast.9), channel_id=1, source_target_pairs={{0,1},{1,2},{2,3},{3,0},{4,5},{5,6},{6,7},{7,4},{8,9},{9,10},{10,1... | collective-permute-start | bytes 1179656 | tf_op jit(solution)/shard_map/ppermute | solution.py:431
  19.3 19.5 %collective-permute-start.4 = (bf16[3,8,2,16,256]{4,3,2,1,0:T(8,128)(2,1)}, bf16[3,8,2,16,256]{4,3,2,1,0:T(8,128)(2,1)}, u32[]{:S(2)}, u32[]{:S(2)}) collective-permute-start(bf16[3,8,2,16,256]{4,3,2,1,0:T(8,128)(2,1)} %bitcast.9), channel_id=1, source_target_pairs={{0,4},{1,5},{2,6},{3,7},{4,0},{5,1},{6,2},{7,3},{8,12},{9,13},{10,... | collective-permute-start | bytes 1179656 | tf_op jit(solution)/shard_map/ppermute | solution.py:431
  28.8 14.8 %collective-permute-start.3 = (bf16[3,4,2,16,256]{4,3,2,1,0:T(8,128)(2,1)S(1)}, bf16[3,4,2,16,256]{4,3,2,1,0:T(8,128)(2,1)S(1)}, u32[]{:S(2)}, u32[]{:S(2)}) collective-permute-start(bf16[3,4,2,16,256]{4,3,2,1,0:T(8,128)(2,1)S(1)} %slice.17), channel_id=1, source_target_pairs={{0,3},{1,0},{2,1},{3,2},{4,7},{5,4},{6,5},{7,6},{8,11},{9,8},{10,9... | collective-permute-start | bytes 589832 | tf_op jit(solution)/shard_map/ppermute | solution.py:431
  33.2 31.7 %copy-start = (f32[64]{0:T(128)S(1)}, f32[64]{0:T(128)}, u32[]{:S(2)}) copy-start(f32[64]{0:T(128)} %base_ref.1) | copy-start | bytes 772
  33.2 10.3 %collective-permute-start.2 = (bf16[3,4,2,16,256]{4,3,2,1,0:T(8,128)(2,1)S(1)}, bf16[3,4,2,16,256]{4,3,2,1,0:T(8,128)(2,1)S(1)}, u32[]{:S(2)}, u32[]{:S(2)}) collective-permute-start(bf16[3,4,2,16,256]{4,3,2,1,0:T(8,128)(2,1)S(1)} %slice.16), channel_id=1, source_target_pairs={{0,1},{1,2},{2,3},{3,0},{4,5},{5,6},{6,7},{7,4},{8,9},{9,10},{10,1... | collective-permute-start | bytes 589832 | tf_op jit(solution)/shard_map/ppermute | solution.py:431
  38.8 10.9 %collective-permute-start.6 = (bf16[3,8,2,16,256]{4,3,2,1,0:T(8,128)(2,1)}, bf16[3,8,2,16,256]{4,3,2,1,0:T(8,128)(2,1)S(1)}, u32[]{:S(2)}, u32[]{:S(2)}) collective-permute-start(bf16[3,8,2,16,256]{4,3,2,1,0:T(8,128)(2,1)} %collective-permute-done.4), channel_id=1, source_target_pairs={{0,3},{1,0},{2,1},{3,2},{4,7},{5,4},{6,5},{7,6},{8,11},{9,8},{10,9... | collective-permute-start | bytes 1179656 | tf_op jit(solution)/shard_map/ppermute | solution.py:431
  41.4 11.7 %collective-permute-start.5 = (bf16[3,8,2,16,256]{4,3,2,1,0:T(8,128)(2,1)}, bf16[3,8,2,16,256]{4,3,2,1,0:T(8,128)(2,1)S(1)}, u32[]{:S(2)}, u32[]{:S(2)}) collective-permute-start(bf16[3,8,2,16,256]{4,3,2,1,0:T(8,128)(2,1)} %collective-permute-done.4), channel_id=1, source_target_pairs={{0,1},{1,2},{2,3},{3,0},{4,5},{5,6},{6,7},{7,4},{8,9},{9,10},{10,1... | collective-permute-start | bytes 1179656 | tf_op jit(solution)/shard_map/ppermute | solution.py:431
  49.7 10.0 %collective-permute-start.8 = (bf16[3,4,2,16,256]{4,3,2,1,0:T(8,128)(2,1)S(1)}, bf16[3,4,2,16,256]{4,3,2,1,0:T(8,128)(2,1)S(1)}, u32[]{:S(2)}, u32[]{:S(2)}) collective-permute-start(bf16[3,4,2,16,256]{4,3,2,1,0:T(8,128)(2,1)S(1)} %slice.19), channel_id=1, source_target_pairs={{0,3},{1,0},{2,1},{3,2},{4,7},{5,4},{6,5},{7,6},{8,11},{9,8},{10,9... | collective-permute-start | bytes 589832 | tf_op jit(solution)/shard_map/ppermute | solution.py:431
  53.2 6.4 %collective-permute-start.7 = (bf16[3,4,2,16,256]{4,3,2,1,0:T(8,128)(2,1)S(1)}, bf16[3,4,2,16,256]{4,3,2,1,0:T(8,128)(2,1)S(1)}, u32[]{:S(2)}, u32[]{:S(2)}) collective-permute-start(bf16[3,4,2,16,256]{4,3,2,1,0:T(8,128)(2,1)S(1)} %slice.18), channel_id=1, source_target_pairs={{0,1},{1,2},{2,3},{3,0},{4,5},{5,6},{6,7},{7,4},{8,9},{9,10},{10,1... | collective-permute-start | bytes 589832 | tf_op jit(solution)/shard_map/ppermute | solution.py:431

commit v10 on v9

--- a/solution.py
+++ b/solution.py
@@ -366,14 +366,18 @@
 
 def final_kernel(bound_ref, came_ref, kept_ref, z_fwd_ref, out_hbm, out_ref, out_sems):
     bound = (bound_ref[0] * bound_ref[0]).astype(F32)
-    saves = []
+    bands = (slice(0, KEPT), slice(N - KEPT, N))
+    between = slice(KEPT, N - KEPT)
+    saves = [copy_of(kept_ref.at[:, :, between], out_hbm.at[:, :, between], out_sems.at[0])]
+    saves[0].start()
     for local, sums in enumerate(tendency(came_ref, z_fwd_ref)):
         _, ksquare = waves_of(local)
-        for part in (0, 1):
-            change = jnp.where(ksquare <= bound, (0.5 * STEP) * sums[part], 0.0)
-            out_ref[part, local] = kept_ref[part, local] - change
-        saves.append(copy_of(out_ref.at[:, local], out_hbm.at[:, local], out_sems.at[local]))
-        saves[-1].start()
+        for band in bands:
+            for part in (0, 1):
+                change = jnp.where(ksquare[band] <= bound, (0.5 * STEP) * sums[part][band], 0.0)
+                out_ref[part, local, band] = kept_ref[part, local, band] - change
+            saves.append(copy_of(out_ref.at[:, local, band], out_hbm.at[:, local, band], out_sems.at[len(saves)]))
+            saves[-1].start()
     for save in saves:
         save.wait()
 
@@ -505,7 +509,7 @@
         in_specs=[SCALARS, NEAR, NEAR, NEAR],
         out_specs=FAR,
         out_shape=pltpu.HBM(STATE, F32),
-        scratch_shapes=[HELD, sems(ROWS)],
+        scratch_shapes=[HELD, sems(2 * ROWS + 1)],
         compiler_params=params(24),
         name="final",
     )(bound, near(came), near(kept), near(z_fwd))

time: 186 us -> 186 us (level)
  no operation moved by 1% of the time
where the time goes in v10:
time: 186 us; the launch traced here: 185 us
  blocking collectives  105 us (56%)
  starting transfers between devices  26.3 us (14%)
  waiting for transfers between devices  26 us (14%)
  Pallas kernels  18.4 us (10%)
  local copies, waits for them, and re-layouts  6.61 us (4%)
  between operations  2.32 us (1%)
    all_to_all x3, blocking collectives, exchanged(): return lax.all_to_all(x, 'fft', 0, 0, tiled=True)  105 us
    ppermute x9, waiting for transfers between devices, moved(): return lax.ppermute(x, 'scal', [(s, change(s)) for s in range(groups)])  20.8 us
    ppermute x9, starting transfers between devices, moved(): return lax.ppermute(x, 'scal', [(s, change(s)) for s in range(groups)])  15.2 us
    all_to_all x1, starting transfers between devices, exchanged(): return lax.all_to_all(x, 'fft', 0, 0, tiled=True)  11.1 us
    pallas_call x2, Pallas kernels, grid_call(): pl.pallas_call(grid_kernel, in_specs=[(SCALARS,) * len(scalars), spec, NE...  9.8 us
    all_to_all x1, waiting for transfers between devices, exchanged(): return lax.all_to_all(x, 'fft', 0, 0, tiled=True)  5.26 us
    pallas_call x1, Pallas kernels, start_call(): pl.pallas_call(start_kernel, in_specs=[FAR, FAR], out_specs=[FAR, NEAR],...  3.85 us
  transfers between devices with their start and end apart: 10, of which 5 were waited for; matrix products, arithmetic and copies ran while one was open for 4% of the time, Pallas kernels for 0%

profile of v10, /device:TPU:1, one launch (start us, length us, event | category | flops | bytes accessed | tf_op | source)
XLA Modules:
  0.0 185.0 jit_solution(15978298290546639625)
XLA Ops:
  0.6 0.0 copy-start.1
  0.6 3.9 %start.1 = (bf16[32,8,16,256]{3,2,1,0:T(8,128)(2,1)}, f32[2,8,128]{2,1,0:T(8,128)S(1)}) custom-call(f32[2,8,256,128]{3,2,1,0:T(8,128)} %bitcast.12, bf16[2,256,256]{2,1,0:T(8,128)(2,1)} %constant.85.table_hbm.held_5_), custom_call_target="tpu_custom_call" | custom-call | tf_op jit(solution)/shard_map/start/pallas_call | solution.py:466
  4.5 11.1 %all-to-all-start = ((bf16[32,8,16,256]{3,2,1,0:T(8,128)(2,1)}), bf16[32,8,16,256]{3,2,1,0:T(8,128)(2,1)}, u32[]{:S(2)}, u32[]{:S(2)}) async-start(bf16[32,8,16,256]{3,2,1,0:T(8,128)(2,1)} %get-tuple-element.15), calls=%async_computation | async-start | bytes 4194304 | tf_op jit(solution)/shard_map/all_to_all | solution.py:462
  15.6 0.0 copy-done.1
  15.6 0.2 reshape.10
  15.8 0.8 copy.17
  16.6 2.7 %collective-permute-start.1 = (bf16[3,8,2,16,256]{4,3,2,1,0:T(8,128)(2,1)}, bf16[3,8,2,16,256]{4,3,2,1,0:T(8,128)(2,1)}, u32[]{:S(2)}, u32[]{:S(2)}) collective-permute-start(bf16[3,8,2,16,256]{4,3,2,1,0:T(8,128)(2,1)} %bitcast.9), channel_id=1, source_target_pairs={{0,3},{1,0},{2,1},{3,2},{4,7},{5,4},{6,5},{7,6},{8,11},{9,8},{10,9... | collective-permute-start | bytes 1179656 | tf_op jit(solution)/shard_map/ppermute | solution.py:435
  19.3 0.0 collective-permute-start
  19.3 2.4 %collective-permute-start.4 = (bf16[3,8,2,16,256]{4,3,2,1,0:T(8,128)(2,1)}, bf16[3,8,2,16,256]{4,3,2,1,0:T(8,128)(2,1)}, u32[]{:S(2)}, u32[]{:S(2)}) collective-permute-start(bf16[3,8,2,16,256]{4,3,2,1,0:T(8,128)(2,1)} %bitcast.9), channel_id=1, source_target_pairs={{0,4},{1,5},{2,6},{3,7},{4,0},{5,1},{6,2},{7,3},{8,12},{9,13},{10,... | collective-permute-start | bytes 1179656 | tf_op jit(solution)/shard_map/ppermute | solution.py:435
  23.1 0.4 broadcast_in_dim.6
  23.5 0.1 constant_dynamic-update-slice_fusion.9
  23.6 4.3 %collective-permute-done.1 = bf16[3,8,2,16,256]{4,3,2,1,0:T(8,128)(2,1)} collective-permute-done((bf16[3,8,2,16,256]{4,3,2,1,0:T(8,128)(2,1)}, bf16[3,8,2,16,256]{4,3,2,1,0:T(8,128)(2,1)}, u32[]{:S(2)}, u32[]{:S(2)}) %collective-permute-start.1) | collective-permute-done | bytes 393248 | tf_op jit(solution)/shard_map/ppermute | solution.py:435
  27.8 0.9 slice.17
  28.8 3.5 %collective-permute-start.3 = (bf16[3,4,2,16,256]{4,3,2,1,0:T(8,128)(2,1)S(1)}, bf16[3,4,2,16,256]{4,3,2,1,0:T(8,128)(2,1)S(1)}, u32[]{:S(2)}, u32[]{:S(2)}) collective-permute-start(bf16[3,4,2,16,256]{4,3,2,1,0:T(8,128)(2,1)S(1)} %slice.17), channel_id=1, source_target_pairs={{0,3},{1,0},{2,1},{3,2},{4,7},{5,4},{6,5},{7,6},{8,11},{9,8},{10,9... | collective-permute-start | bytes 589832 | tf_op jit(solution)/shard_map/ppermute | solution.py:435
  32.2 0.0 collective-permute-done
  32.2 0.9 slice.16
  33.2 0.0 copy-start
  33.2 0.1 collective-permute-start.2
  33.3 5.5 %collective-permute-done.4 = bf16[3,8,2,16,256]{4,3,2,1,0:T(8,128)(2,1)} collective-permute-done((bf16[3,8,2,16,256]{4,3,2,1,0:T(8,128)(2,1)}, bf16[3,8,2,16,256]{4,3,2,1,0:T(8,128)(2,1)}, u32[]{:S(2)}, u32[]{:S(2)}) %collective-permute-start.4) | collective-permute-done | bytes 393248 | tf_op jit(solution)/shard_map/ppermute | solution.py:435
  38.8 2.7 %collective-permute-start.6 = (bf16[3,8,2,16,256]{4,3,2,1,0:T(8,128)(2,1)}, bf16[3,8,2,16,256]{4,3,2,1,0:T(8,128)(2,1)S(1)}, u32[]{:S(2)}, u32[]{:S(2)}) collective-permute-start(bf16[3,8,2,16,256]{4,3,2,1,0:T(8,128)(2,1)} %collective-permute-done.4), channel_id=1, source_target_pairs={{0,3},{1,0},{2,1},{3,2},{4,7},{5,4},{6,5},{7,6},{8,11},{9,8},{10,9... | collective-permute-start | bytes 1179656 | tf_op jit(solution)/shard_map/ppermute | solution.py:435
  41.4 0.0 collective-permute-start.5
  41.5 1.0 constant_dynamic-update-slice_fusion.8
  42.5 1.0 constant_dynamic-update-slice_fusion.7
  43.5 0.0 collective-permute-done.2
  43.6 0.0 collective-permute-done.3
  43.6 1.0 constant_dynamic-update-slice_fusion.4
  44.7 5.0 %collective-permute-done.6 = bf16[3,8,2,16,256]{4,3,2,1,0:T(8,128)(2,1)S(1)} collective-permute-done((bf16[3,8,2,16,256]{4,3,2,1,0:T(8,128)(2,1)}, bf16[3,8,2,16,256]{4,3,2,1,0:T(8,128)(2,1)S(1)}, u32[]{:S(2)}, u32[]{:S(2)}) %collective-permute-start.6) | collective-permute-done | bytes 393248 | tf_op jit(solution)/shard_map/ppermute | solution.py:435
  49.7 3.5 %collective-permute-start.8 = (bf16[3,4,2,16,256]{4,3,2,1,0:T(8,128)(2,1)S(1)}, bf16[3,4,2,16,256]{4,3,2,1,0:T(8,128)(2,1)S(1)}, u32[]{:S(2)}, u32[]{:S(2)}) collective-permute-start(bf16[3,4,2,16,256]{4,3,2,1,0:T(8,128)(2,1)S(1)} %slice.19), channel_id=1, source_target_pairs={{0,3},{1,0},{2,1},{3,2},{4,7},{5,4},{6,5},{7,6},{8,11},{9,8},{10,9... | collective-permute-start | bytes 589832 | tf_op jit(solution)/shard_map/ppermute | solution.py:435
  53.2 0.0 collective-permute-done.5
  53.2 0.3 collective-permute-start.7
  53.6 6.0 %collective-permute-done.7 = bf16[3,4,2,16,256]{4,3,2,1,0:T(8,128)(2,1)S(1)} collective-permute-done((bf16[3,4,2,16,256]{4,3,2,1,0:T(8,128)(2,1)S(1)}, bf16[3,4,2,16,256]{4,3,2,1,0:T(8,128)(2,1)S(1)}, u32[]{:S(2)}, u32[]{:S(2)}) %collective-permute-start.7) | collective-permute-done | bytes 196640 | tf_op jit(solution)/shard_map/ppermute | solution.py:435
  59.6 0.0 collective-permute-done.8
  59.7 5.3 %all-to-all-done.planes_hbm = bf16[32,8,16,256]{3,2,1,0:T(8,128)(2,1)} async-done(((bf16[32,8,16,256]{3,2,1,0:T(8,128)(2,1)}), bf16[32,8,16,256]{3,2,1,0:T(8,128)(2,1)}, u32[]{:S(2)}, u32[]{:S(2)}) %all-to-all-start) | async-done | bytes 2097184 | tf_op jit(solution)/shard_map/all_to_all | solution.py:462
  64.9 0.0 copy-done
  64.9 6.1 %grid.2 = (bf16[32,88,128]{2,1,0:T(8,128)(2,1)S(1)}, bf16[2,256,256]{2,1,0:T(8,128)(2,1)S(1)}, bf16[256,256]{1,0:T(8,128)(2,1)S(1)}, bf16[256,256]{1,0:T(8,128)(...) custom-call(s32[1]{0:T(128)S(6)} %copy.29.scalars_0_.bound_ref, ...), custom_call_target="tpu_custom_call" | custom-call | tf_op jit(solution)/shard_map/grid/pallas_call | solution.py:483
  71.0 25.5 %all_to_all.20.came_ref = bf16[32,88,128]{2,1,0:T(8,128)(2,1)S(1)} all-to-all(bf16[32,88,128]{2,1,0:T(8,128)(2,1)S(1)} %get-tuple-element.17), channel_id=1, replica_groups=mesh['fft'=32,'scal'=8] {'fft'}, dimensions={0} | all-to-all | bytes 1441792 | tf_op jit(solution)/shard_map/all_to_all | solution.py:462
  96.5 2.8 %middle.1 = (bf16[32,8,16,256]{3,2,1,0:T(8,128)(2,1)S(1)}, f32[2,8,256,128]{3,2,1,0:T(8,128)S(1)}, f32[1]{0:T(128)}) custom-call(s32[1]{0:T(128)S(6)} %copy.29.scalars_0_.bound_ref, s32[1]{0:T(128)S(6)} %copy.28.scalars_1_.species_ref, f32[64]{0:T(128)S(1)} %copy-done, bf16[32,88,128]{2,1,0:T(8,128)(2,1)S(1)} %all_to_all.20.came_ref, ...), custom_call_target="tpu_custom_call" | custom-call | tf_op jit(solution)/shard_map/middle/pallas_call | solution.py:495
  99.4 54.1 %all_to_all.21.planes_hbm = bf16[32,8,16,256]{3,2,1,0:T(8,128)(2,1)S(1)} all-to-all(bf16[32,8,16,256]{3,2,1,0:T(8,128)(2,1)S(1)} %get-tuple-element.21), channel_id=1, replica_groups=mesh['fft'=32,'scal'=8] {'fft'}, dimensions={0} | all-to-all | bytes 4194304 | tf_op jit(solution)/shard_map/all_to_all | solution.py:462
  153.5 3.7 %grid.3 = bf16[32,88,128]{2,1,0:T(8,128)(2,1)S(1)} custom-call(bf16[32,8,16,256]{3,2,1,0:T(8,128)(2,1)S(1)} %all_to_all.21.planes_hbm, bf16[3,8,256,256]{3,2,1,0:T(8,128)(2,1)S(1)} %bitcast.11, f32[2,8,128]{2,1,0:T(8,128)S(1)} %get-tuple-element.16.stats_ref, bf16[2,256,256]{2,1,0:T(8,128)(2,1)S(1)} %get-tuple-element.22.held_0_, ...), custom_call_target="tpu_custom_call" | custom-call | tf_op jit(solution)/shard_map/grid/pallas_call | solution.py:483
  157.2 25.8 %all_to_all.22.came_ref = bf16[32,88,128]{2,1,0:T(8,128)(2,1)S(1)} all-to-all(bf16[32,88,128]{2,1,0:T(8,128)(2,1)S(1)} %grid.3), channel_id=1, replica_groups=mesh['fft'=32,'scal'=8] {'fft'}, dimensions={0} | all-to-all | bytes 1441792 | tf_op jit(solution)/shard_map/all_to_all | solution.py:462
  183.0 1.9 %final.1 = f32[2,8,256,128]{3,2,1,0:T(8,128)} custom-call(s32[1]{0:T(128)S(6)} %copy.29.scalars_0_.bound_ref, bf16[32,88,128]{2,1,0:T(8,128)(2,1)S(1)} %all_to_all.22.came_ref, f32[2,8,256,128]{3,2,1,0:T(8,128)S(1)} %get-tuple-element.26.kept_ref, bf16[352,512]{1,0:T(8,128)(2,1)S(1)} %get-tuple-element.19.z_fwd_ref), custom_call_target="tpu_custom_call" | custom-call | tf_op jit(solution)/shard_map/final/pallas_call | solution.py:507
  (8 shorter events, 0.2 us)
Async XLA Ops:
  0.6 15.0 %copy-start.1 = (bf16[3,8,32,256]{3,2,1,0:T(8,128)(2,1)S(1)}, bf16[3,8,32,256]{3,2,1,0:T(8,128)(2,1)}, u32[]{:S(2)}) copy-start(bf16[3,8,32,256]{3,2,1,0:T(8,128)(2,1)} %param.12) | copy-start | bytes 1179652
  4.5 60.4 %all-to-all-start = ((bf16[32,8,16,256]{3,2,1,0:T(8,128)(2,1)}), bf16[32,8,16,256]{3,2,1,0:T(8,128)(2,1)}, u32[]{:S(2)}, u32[]{:S(2)}) async-start(bf16[32,8,16,256]{3,2,1,0:T(8,128)(2,1)} %get-tuple-element.15), calls=%async_computation | async-start | bytes 4194304 | tf_op jit(solution)/shard_map/all_to_all | solution.py:462
  16.6 11.2 %collective-permute-start.1 = (bf16[3,8,2,16,256]{4,3,2,1,0:T(8,128)(2,1)}, bf16[3,8,2,16,256]{4,3,2,1,0:T(8,128)(2,1)}, u32[]{:S(2)}, u32[]{:S(2)}) collective-permute-start(bf16[3,8,2,16,256]{4,3,2,1,0:T(8,128)(2,1)} %bitcast.9), channel_id=1, source_target_pairs={{0,3},{1,0},{2,1},{3,2},{4,7},{5,4},{6,5},{7,6},{8,11},{9,8},{10,9... | collective-permute-start | bytes 1179656 | tf_op jit(solution)/shard_map/ppermute | solution.py:435
  19.3 12.9 %collective-permute-start = (bf16[3,8,2,16,256]{4,3,2,1,0:T(8,128)(2,1)}, bf16[3,8,2,16,256]{4,3,2,1,0:T(8,128)(2,1)}, u32[]{:S(2)}, u32[]{:S(2)}) collective-permute-start(bf16[3,8,2,16,256]{4,3,2,1,0:T(8,128)(2,1)} %bitcast.9), channel_id=1, source_target_pairs={{0,1},{1,2},{2,3},{3,0},{4,5},{5,6},{6,7},{7,4},{8,9},{9,10},{10,1... | collective-permute-start | bytes 1179656 | tf_op jit(solution)/shard_map/ppermute | solution.py:435
  19.3 19.5 %collective-permute-start.4 = (bf16[3,8,2,16,256]{4,3,2,1,0:T(8,128)(2,1)}, bf16[3,8,2,16,256]{4,3,2,1,0:T(8,128)(2,1)}, u32[]{:S(2)}, u32[]{:S(2)}) collective-permute-start(bf16[3,8,2,16,256]{4,3,2,1,0:T(8,128)(2,1)} %bitcast.9), channel_id=1, source_target_pairs={{0,4},{1,5},{2,6},{3,7},{4,0},{5,1},{6,2},{7,3},{8,12},{9,13},{10,... | collective-permute-start | bytes 1179656 | tf_op jit(solution)/shard_map/ppermute | solution.py:435
  28.8 14.8 %collective-permute-start.3 = (bf16[3,4,2,16,256]{4,3,2,1,0:T(8,128)(2,1)S(1)}, bf16[3,4,2,16,256]{4,3,2,1,0:T(8,128)(2,1)S(1)}, u32[]{:S(2)}, u32[]{:S(2)}) collective-permute-start(bf16[3,4,2,16,256]{4,3,2,1,0:T(8,128)(2,1)S(1)} %slice.17), channel_id=1, source_target_pairs={{0,3},{1,0},{2,1},{3,2},{4,7},{5,4},{6,5},{7,6},{8,11},{9,8},{10,9... | collective-permute-start | bytes 589832 | tf_op jit(solution)/shard_map/ppermute | solution.py:435
  33.2 31.7 %copy-start = (f32[64]{0:T(128)S(1)}, f32[64]{0:T(128)}, u32[]{:S(2)}) copy-start(f32[64]{0:T(128)} %base_ref.1) | copy-start | bytes 772
  33.2 10.3 %collective-permute-start.2 = (bf16[3,4,2,16,256]{4,3,2,1,0:T(8,128)(2,1)S(1)}, bf16[3,4,2,16,256]{4,3,2,1,0:T(8,128)(2,1)S(1)}, u32[]{:S(2)}, u32[]{:S(2)}) collective-permute-start(bf16[3,4,2,16,256]{4,3,2,1,0:T(8,128)(2,1)S(1)} %slice.16), channel_id=1, source_target_pairs={{0,1},{1,2},{2,3},{3,0},{4,5},{5,6},{6,7},{7,4},{8,9},{9,10},{10,1... | collective-permute-start | bytes 589832 | tf_op jit(solution)/shard_map/ppermute | solution.py:435
  38.8 10.9 %collective-permute-start.6 = (bf16[3,8,2,16,256]{4,3,2,1,0:T(8,128)(2,1)}, bf16[3,8,2,16,256]{4,3,2,1,0:T(8,128)(2,1)S(1)}, u32[]{:S(2)}, u32[]{:S(2)}) collective-permute-start(bf16[3,8,2,16,256]{4,3,2,1,0:T(8,128)(2,1)} %collective-permute-done.4), channel_id=1, source_target_pairs={{0,3},{1,0},{2,1},{3,2},{4,7},{5,4},{6,5},{7,6},{8,11},{9,8},{10,9... | collective-permute-start | bytes 1179656 | tf_op jit(solution)/shard_map/ppermute | solution.py:435
  41.4 11.7 %collective-permute-start.5 = (bf16[3,8,2,16,256]{4,3,2,1,0:T(8,128)(2,1)}, bf16[3,8,2,16,256]{4,3,2,1,0:T(8,128)(2,1)S(1)}, u32[]{:S(2)}, u32[]{:S(2)}) collective-permute-start(bf16[3,8,2,16,256]{4,3,2,1,0:T(8,128)(2,1)} %collective-permute-done.4), channel_id=1, source_target_pairs={{0,1},{1,2},{2,3},{3,0},{4,5},{5,6},{6,7},{7,4},{8,9},{9,10},{10,1... | collective-permute-start | bytes 1179656 | tf_op jit(solution)/shard_map/ppermute | solution.py:435
  49.7 10.0 %collective-permute-start.8 = (bf16[3,4,2,16,256]{4,3,2,1,0:T(8,128)(2,1)S(1)}, bf16[3,4,2,16,256]{4,3,2,1,0:T(8,128)(2,1)S(1)}, u32[]{:S(2)}, u32[]{:S(2)}) collective-permute-start(bf16[3,4,2,16,256]{4,3,2,1,0:T(8,128)(2,1)S(1)} %slice.19), channel_id=1, source_target_pairs={{0,3},{1,0},{2,1},{3,2},{4,7},{5,4},{6,5},{7,6},{8,11},{9,8},{10,9... | collective-permute-start | bytes 589832 | tf_op jit(solution)/shard_map/ppermute | solution.py:435
  53.2 6.4 %collective-permute-start.7 = (bf16[3,4,2,16,256]{4,3,2,1,0:T(8,128)(2,1)S(1)}, bf16[3,4,2,16,256]{4,3,2,1,0:T(8,128)(2,1)S(1)}, u32[]{:S(2)}, u32[]{:S(2)}) collective-permute-start(bf16[3,4,2,16,256]{4,3,2,1,0:T(8,128)(2,1)S(1)} %slice.18), channel_id=1, source_target_pairs={{0,1},{1,2},{2,3},{3,0},{4,5},{5,6},{6,7},{7,4},{8,9},{9,10},{10,1... | collective-permute-start | bytes 589832 | tf_op jit(solution)/shard_map/ppermute | solution.py:435
